TPU v7x, 1024 devices: a whole 4x8x16 slice. The times are simulated.
1024 devices in a mesh: dp: 32 (over y, z_hi, core), tensor: 32 (over z_lo, x).
Axes of the slice: x: 4, y: 8, z: 16 (z_hi: 2, z_lo: 8; z = z_hi * 8 + z_lo), core: 2. Of those that a mesh axis runs over, the one named last changes fastest.
Arguments:
- hidden_in: bfloat16 [4096, 8192], P('dp'), may hold values from -20 to 20
- norm_gain: bfloat16 [8192], replicated, may hold values from 0.25 to 1.75
- q_weight: bfloat16 [8192, 8192], P(None, 'tensor'), as said below
- q_grad: bfloat16 [4096, 8192], P('dp', 'tensor'), may hold values from -6 to 6
- q_main: float32 [8192, 8192], P('dp', 'tensor'), may hold values from -6 to 6
- weight_main_gradient: float32 [8192], P('tensor'), may hold values from -6 to 6
Outputs:
- hidden_state_gradient: bfloat16 [4096, 8192], P('dp', 'tensor')
- q_main_new: float32 [8192, 8192], P('dp', 'tensor')
- weight_main_updated: float32 [8192], P('tensor')
Inputs may be any that keep to these rules, and one draw needn't show every extreme that they name: `q_weight`: entries of mean 0 and deviation about 8192 ** -0.5.
All inputs are finite; a program needn't handle non-finite values.
Results may differ from a plain program's by a relative error of at most 0.03.
Values may be sent and summed in bfloat16 or wider, within the bound.
No kernel may reach another device: no remote copies, remote signals or barrier semaphores. Data moves between devices by JAX's collectives and lax.ppermute only.
A program may use at most 64 MiB of HBM per device.

v0:
```python
import jax
import jax.numpy as jnp
from jax import lax
from jax.sharding import PartitionSpec as P


def in_blocks(shard, dim, count):
    before, after = (shard.shape[:dim], shard.shape[dim + 1 :])
    return jnp.moveaxis(shard.reshape(*before, count, -1, *after), dim, 0)


def sum_at_owner(shard, axis, dim):
    count = lax.axis_size(axis)
    parts = lax.all_to_all(in_blocks(shard, dim, count), axis, 0, 0, tiled=True)
    return jnp.sum(parts.astype(jnp.float32), axis=0)


def sent_to_all(shard, axis):
    count = lax.axis_size(axis)
    return lax.all_to_all(
        jnp.broadcast_to(shard[None], (count, *shard.shape)), axis, 0, 0, tiled=True
    )


def taken_together(shard, axis):
    everything = sent_to_all(shard, axis)
    return jnp.sum(everything, axis=0)


def body(hidden_in, norm_gain, q_weight, q_grad, q_main, weight_main_gradient):
    hidden_state = hidden_in.astype(jnp.float32)
    inverse_root_mean = lax.rsqrt(
        jnp.mean(hidden_state * hidden_state, axis=-1, keepdims=True) + 1e-05
    )
    normalized_rows = hidden_state * inverse_root_mean
    norm_weight = norm_gain.astype(jnp.float32)
    normalized_input = (normalized_rows * norm_weight).astype(jnp.bfloat16)
    hidden_width = q_weight.shape[1]
    features = hidden_in.shape[1]
    ndp = lax.axis_size("dp")
    owner_start = lax.axis_index("tensor") * hidden_width
    partial_value = lax.dot_general(
        q_grad, q_weight, (((1,), (1,)), ((), ())), preferred_element_type=jnp.float32
    )
    owned_normalized_rows = lax.dynamic_slice_in_dim(normalized_rows, owner_start, hidden_width, 1)
    owned_norm_weight = lax.dynamic_slice_in_dim(norm_weight, owner_start, hidden_width, 0)
    owned_gradient = sum_at_owner(partial_value.astype(jnp.bfloat16), "tensor", 1)
    local_stat = jnp.sum(
        owned_gradient * owned_norm_weight * owned_normalized_rows, axis=-1, keepdims=True
    )
    row_statistic = taken_together(local_stat, "tensor") / features
    hidden_state_gradient = (
        inverse_root_mean
        * (owned_gradient * owned_norm_weight - owned_normalized_rows * row_statistic)
    ).astype(jnp.bfloat16)
    weight_contribution = jnp.sum(owned_gradient * owned_normalized_rows, axis=0)
    weight_main_updated = weight_main_gradient + taken_together(weight_contribution, "dp") / ndp
    product = lax.dot_general(
        normalized_input, q_grad, (((0,), (0,)), ((), ())), preferred_element_type=jnp.float32
    )
    q_main_new = q_main + lax.psum_scatter(
        (product / ndp).astype(jnp.bfloat16), "dp", scatter_dimension=0, tiled=True
    ).astype(jnp.float32)
    return (hidden_state_gradient, q_main_new, weight_main_updated)


def solution(mesh):
    in_specs = (
        P("dp", None),
        P(),
        P(None, "tensor"),
        P("dp", "tensor"),
        P("dp", "tensor"),
        P("tensor"),
    )
    out_specs = (P("dp", "tensor"), P("dp", "tensor"), P("tensor"))
    return jax.shard_map(body, mesh=mesh, in_specs=in_specs, out_specs=out_specs, check_vma=False)
```

profile of v0, /device:TPU:1, one launch (start us, length us, event | category | flops | bytes accessed | tf_op | source)
XLA Modules:
  0.0 282.1 jit_solution(16495753620775578377)
XLA Ops:
  7.2 0.0 copy-start
  7.2 0.8 copy-done
  8.0 3.7 %convolution_convert_fusion = bf16[128,8192]{1,0:T(8,128)(2,1)S(1)} fusion(bf16[128,256]{1,0:T(8,128)(2,1)S(1)} %copy-done, bf16[8192,256]{1,0:T(8,128)(2,1)} %param.8), kind=kOutput, calls=%fused_computation.2 | convolution fusion | flops 537919488 | bytes 6356992 | tf_op jit(solution)/shard_map/dot_general | solution.py:42
  11.7 0.0 copy-start.3
  11.7 0.0 copy-start.1
  11.7 1.6 copy.16
  13.3 19.2 %all-to-all-start = ((bf16[32,128,256]{2,1,0:T(8,128)(2,1)}), bf16[32,128,256]{2,1,0:T(8,128)(2,1)}, u32[]{:S(2)}, u32[]{:S(2)}) async-start(bf16[32,128,256]{2,1,0:T(8,128)(2,1)} %bitcast.11), calls=%async_computation | async-start | bytes 4194304 | tf_op jit(solution)/shard_map/all_to_all | solution.py:14
  32.5 0.0 reduce-scatter.2.cloned.1.call-start
  32.6 0.0 copy-done.3
  32.6 0.0 copy-done.1
  32.6 0.5 fusion.1
  33.1 3.4 %fusion = bf16[8192,256]{1,0:T(8,128)(2,1)} fusion(bf16[128,256]{1,0:T(8,128)(2,1)S(1)} %copy-done, f32[8192]{0:T(1024)S(1)} %convert_element_type.27, bf16[128,8192]{1,0:T(8,128)(2,1)S(1)} %copy-done.1, f32[128]{0:T(128)S(1)} %add_rsqrt_fusion), kind=kOutput, calls=%fused_computation.1 | convolution fusion | flops 545259520 | bytes 6390272 | tf_op jit(solution)/shard_map/dot_general | solution.py:58
  36.5 0.0 reduce-scatter.2.cloned.1.call-update
  36.5 0.1 dynamic_slice.6
  36.6 0.0 copy-start.2
  36.6 0.0 copy-start.4
  36.6 2.4 convert_multiply_fusion
  39.0 132.6 %all-to-all-done = bf16[32,128,256]{2,1,0:T(8,128)(2,1)} async-done(((bf16[32,128,256]{2,1,0:T(8,128)(2,1)}), bf16[32,128,256]{2,1,0:T(8,128)(2,1)}, u32[]{:S(2)}, u32[]{:S(2)}) %all-to-all-start) | async-done | bytes 2097184 | tf_op jit(solution)/shard_map/all_to_all | solution.py:14
  171.6 1.9 convert_reduce_fusion
  173.5 1.0 multiply_reduce_fusion
  174.5 0.6 broadcast_in_dim.4
  175.2 8.8 %all-to-all-start.1 = ((f32[32,128,1]{1,2,0:T(1,128)}), f32[32,128,1]{1,2,0:T(1,128)S(1)}, u32[]{:S(2)}, u32[]{:S(2)}) async-start(f32[32,128,1]{1,2,0:T(1,128)} %broadcast_in_dim.4), calls=%async_computation.1 | async-start | bytes 32768 | tf_op jit(solution)/shard_map/all_to_all | solution.py:20
  184.0 60.6 %reduce-scatter.2.cloned.1.call-done = bf16[256,256]{1,0:T(8,128)(2,1)} async-done(((bf16[8192,256]{1,0:T(8,128)(2,1)}), bf16[256,256]{1,0:T(8,128)(2,1)}) %reduce-scatter.2.cloned.1.call-update) | async-done | bytes 131088 | tf_op jit(solution)/shard_map/reduce_scatter | solution.py:61
  244.6 0.0 copy-done.2
  244.6 1.6 convert_add_fusion
  246.2 0.0 all-to-all-done.1
  246.2 0.6 broadcast_in_dim.5
  246.8 10.9 %all-to-all-start.2 = ((f32[32,1,256]{2,1,0:T(1,128)}), f32[32,1,256]{2,1,0:T(1,128)S(1)}, u32[]{:S(2)}, u32[]{:S(2)}) async-start(f32[32,1,256]{2,1,0:T(1,128)} %broadcast_in_dim.5), calls=%async_computation.3 | async-start | bytes 65536 | tf_op jit(solution)/shard_map/all_to_all | solution.py:20
  257.7 0.1 reduce_sum.57
  257.8 1.6 multiply_convert_fusion.2
  259.4 15.1 %all-to-all-done.2 = f32[32,1,256]{2,1,0:T(1,128)S(1)} async-done(((f32[32,1,256]{2,1,0:T(1,128)}), f32[32,1,256]{2,1,0:T(1,128)S(1)}, u32[]{:S(2)}, u32[]{:S(2)}) %all-to-all-start.2) | async-done | bytes 32800 | tf_op jit(solution)/shard_map/all_to_all | solution.py:20
  274.6 0.1 reduce_sum.59
  274.6 0.0 copy-done.4
  274.6 0.6 multiply_add_fusion
  (3 shorter events, 0.0 us)
Async XLA Ops:
  7.2 0.8 copy-start
  11.7 20.9 %copy-start.3 = (bf16[8192]{0:T(1024)(128)(2,1)S(1)}, bf16[8192]{0:T(1024)(128)(2,1)}, u32[]{:S(2)}) copy-start(bf16[8192]{0:T(1024)(128)(2,1)} %param.7) | copy-start | bytes 49156
  11.7 20.9 %copy-start.1 = (bf16[128,8192]{1,0:T(8,128)(2,1)S(1)}, bf16[128,8192]{1,0:T(8,128)(2,1)}, u32[]{:S(2)}) copy-start(bf16[128,8192]{1,0:T(8,128)(2,1)} %param.6) | copy-start | bytes 6291460
  13.3 158.3 %all-to-all-start = ((bf16[32,128,256]{2,1,0:T(8,128)(2,1)}), bf16[32,128,256]{2,1,0:T(8,128)(2,1)}, u32[]{:S(2)}, u32[]{:S(2)}) async-start(bf16[32,128,256]{2,1,0:T(8,128)(2,1)} %bitcast.11), calls=%async_computation | async-start | bytes 4194304 | tf_op jit(solution)/shard_map/all_to_all | solution.py:14
  32.5 212.1 %reduce-scatter.2.cloned.1.call-start = ((), (), s32[]{:S(2)}) async-start(), calls=%async_computation.4 | async-start | bytes 4325376 | tf_op jit(solution)/shard_map/reduce_scatter | solution.py:61
  36.6 208.0 %copy-start.2 = (f32[256,256]{1,0:T(8,128)S(1)}, f32[256,256]{1,0:T(8,128)}, u32[]{:S(2)}) copy-start(f32[256,256]{1,0:T(8,128)} %param.10) | copy-start | bytes 786436
  36.6 238.0 %copy-start.4 = (f32[256]{0:T(256)S(1)}, f32[256]{0:T(256)}, u32[]{:S(2)}) copy-start(f32[256]{0:T(256)} %param.11) | copy-start | bytes 3076
  175.2 71.0 %all-to-all-start.1 = ((f32[32,128,1]{1,2,0:T(1,128)}), f32[32,128,1]{1,2,0:T(1,128)S(1)}, u32[]{:S(2)}, u32[]{:S(2)}) async-start(f32[32,128,1]{1,2,0:T(1,128)} %broadcast_in_dim.4), calls=%async_computation.1 | async-start | bytes 32768 | tf_op jit(solution)/shard_map/all_to_all | solution.py:20
  246.8 27.8 %all-to-all-start.2 = ((f32[32,1,256]{2,1,0:T(1,128)}), f32[32,1,256]{2,1,0:T(1,128)S(1)}, u32[]{:S(2)}, u32[]{:S(2)}) async-start(f32[32,1,256]{2,1,0:T(1,128)} %broadcast_in_dim.5), calls=%async_computation.3 | async-start | bytes 65536 | tf_op jit(solution)/shard_map/all_to_all | solution.py:20
Sparse Core Ops, SparseCore 0:
  39.3 205.2 reduce-scatter.1
where the time goes:
time: 283 us; the launch traced here: 282 us
  waiting for transfers between devices  208 us (73%)
  starting transfers between devices  39 us (14%)
  between operations  14.1 us (5%)
  other arithmetic  9.77 us (3%)
  matrix products  7.08 us (3%)
  local copies, waits for them, and re-layouts  3.73 us (1%)
    all_to_all x1, waiting for transfers between devices, sum_at_owner(): parts = lax.all_to_all(in_blocks(shard, dim, count), axis, 0, 0, tiled=True)  133 us
    reduce_scatter x1, waiting for transfers between devices, body(): lax.psum_scatter((product / ndp).astype(jnp.bfloat16), 'dp', scatter_dime...  60.6 us
    all_to_all x2, starting transfers between devices, sent_to_all(): lax.all_to_all(jnp.broadcast_to(shard[None], (count, *shard.shape)), axis...  19.7 us
    all_to_all x1, starting transfers between devices, sum_at_owner(): parts = lax.all_to_all(in_blocks(shard, dim, count), axis, 0, 0, tiled=True)  19.2 us
    all_to_all x2, waiting for transfers between devices, sent_to_all(): lax.all_to_all(jnp.broadcast_to(shard[None], (count, *shard.shape)), axis...  15.1 us
  transfers between devices with their start and end apart: 4, of which 3 were waited for; matrix products, arithmetic and copies ran while one was open for 5% of the time, Pallas kernels for 0%

commit v1 on v0

v1 whole, which is shorter than its diff:
```python
import functools

import jax
import jax.numpy as jnp
from jax import lax
from jax.experimental import pallas as pl
from jax.experimental.pallas import tpu as pltpu
from jax.sharding import Mesh, PartitionSpec as P


BF = jnp.bfloat16
F32 = jnp.float32
NY, NH, NC, NZ, NX = 8, 2, 2, 8, 4
TOK = 128
D = 8192
B = 256
MB = 2**20
VM = pl.BlockSpec(memory_space=pltpu.VMEM)


def cost(flops, nbytes):
    return pl.CostEstimate(flops=flops, bytes_accessed=nbytes, transcendentals=0)


def params(mib):
    return pltpu.CompilerParams(vmem_limit_bytes=mib * MB)


def call(kernel, out_shape, args, mib, flops, nbytes, **kw):
    return pl.pallas_call(
        kernel,
        out_shape=out_shape,
        compiler_params=params(mib),
        cost_estimate=cost(flops, nbytes),
        **kw,
    )(*args)


def aligned(start, size):
    return pl.ds(pl.multiple_of(start, size), size)


def two_rows(g_ref, block):
    at = lambda i: g_ref[pl.ds(2 * block + i, 1), :]
    return jnp.concatenate([at(0), at(1)], axis=1)


ROWS = 64


def norm_kernel(h_ref, g_ref, q_ref, send_ref, own_ref, rinv_ref, g32):
    par, core = lax.rem(lax.axis_index("y"), 2), lax.axis_index("c")
    g32[...] = g_ref[...].astype(F32)
    acc = jnp.zeros((ROWS, 128), F32)
    for j in range(D // 128):
        h = h_ref[:, j * 128 : (j + 1) * 128].astype(F32)
        acc = acc + h * h
    rinv = lax.rsqrt(jnp.sum(acc, axis=1, keepdims=True) / D + 1e-05)
    rinv_ref[...] = rinv
    for out, which in ((send_ref, 1 - core), (own_ref, core)):
        for j in range(16):
            o, k, zh = j // 8, (j // 2) % 4, j % 2
            y = 2 * k + (1 - par if o == 0 else par)
            block = y * 4 + zh * 2 + which
            h = h_ref[:, aligned(block * B, B)].astype(F32)
            out[:, j * B : (j + 1) * B] = (h * rinv * two_rows(g32, block)).astype(BF)
    send_ref[:, 16 * B :] = q_ref[...]


def norm(hidden, gain, q_grad):
    row = lambda n: pl.BlockSpec((ROWS, n), lambda i: (i, 0))
    return call(
        norm_kernel,
        (
            jax.ShapeDtypeStruct((TOK, 17 * B), BF),
            jax.ShapeDtypeStruct((TOK, 16 * B), BF),
            jax.ShapeDtypeStruct((TOK, 1), F32),
        ),
        (hidden, gain, q_grad),
        16,
        6 * TOK * D,
        4 * TOK * D,
        grid=(TOK // ROWS,),
        in_specs=[row(D), pl.BlockSpec((64, 128), lambda i: (0, 0)), row(B)],
        out_specs=(row(17 * B), row(16 * B), row(1)),
        scratch_shapes=[pltpu.VMEM((64, 128), F32)],
        name="norm",
    )


def eye():
    a = lax.broadcasted_iota(jnp.int32, (128, 128), 0)
    b = lax.broadcasted_iota(jnp.int32, (128, 128), 1)
    return a == b


def stat_rows(row):
    hi = row.astype(BF).astype(F32)
    both = jnp.concatenate([hi, row - hi], axis=1)
    first = lax.broadcasted_iota(jnp.int32, (8, 256), 0) == 0
    return jnp.where(first, jnp.broadcast_to(both, (8, 256)), 0.0).astype(BF)


def stat_of(block):
    both = jnp.sum(block.astype(F32), axis=0, keepdims=True)
    return both[:, :128] + both[:, 128:]


def partial_kernel(q_ref, w_ref, h_ref, g_ref, rinv_ref, out_ref):
    q = q_ref[...]
    g = g_ref[...].astype(F32)
    acc = jnp.zeros((TOK, 128), F32)
    for z in range(NZ):
        for x in range(NX):
            b = z * NX + x
            at = slice(b * B, (b + 1) * B)
            p = lax.dot_general(q, w_ref[at, :], (((1,), (1,)), ((), ())), preferred_element_type=F32)
            p = p.astype(BF)
            out_ref[x, z * TOK : (z + 1) * TOK, :] = p
            t = p.astype(F32) * h_ref[:, at].astype(F32)
            acc = acc + t[:, :128] * g[2 * b : 2 * b + 1, :] + t[:, 128:] * g[2 * b + 1 : 2 * b + 2, :]
    s = jnp.sum(acc, axis=1, keepdims=True) * rinv_ref[...]
    rows = stat_rows(jnp.sum(jnp.where(eye(), s, 0.0), axis=0, keepdims=True))
    for x in range(NX):
        out_ref[x, NZ * TOK :, :] = rows


def partial(q_grad, weight, hidden, gain, rinv):
    return call(
        partial_kernel,
        jax.ShapeDtypeStruct((NX, NZ * TOK + 8, B), BF),
        (q_grad, weight, hidden, gain, rinv),
        24,
        2 * TOK * D * B,
        8 * MB,
        in_specs=[VM] * 5,
        out_specs=VM,
        name="partial",
    )


def sum_x_kernel(in_ref, send_ref, keep_ref):
    bit = lax.rem(lax.axis_index("zl"), 2)

    def total(at):
        s = in_ref[0, at, :].astype(F32)
        for x in range(1, NX):
            s = s + in_ref[x, at, :].astype(F32)
        return s

    for k in range(4):
        at = slice(k * TOK, (k + 1) * TOK)
        send_ref[at, :] = total(aligned((2 * k + 1 - bit) * TOK, TOK)).astype(BF)
    rows = stat_rows(stat_of(total(slice(NZ * TOK, NZ * TOK + 8))))
    send_ref[4 * TOK :, :] = rows
    for k in range(4):
        at = slice(k * TOK, (k + 1) * TOK)
        keep_ref[at, :] = total(aligned((2 * k + bit) * TOK, TOK))
    keep_ref[4 * TOK :, :] = rows.astype(F32)


def sum_x(got):
    rows = 4 * TOK + 8
    return call(
        sum_x_kernel,
        (jax.ShapeDtypeStruct((rows, B), BF), jax.ShapeDtypeStruct((rows, B), F32)),
        (got,),
        12,
        TOK * D,
        4 * MB,
        in_specs=[VM],
        out_specs=(VM, VM),
        name="sum_x",
    )


def sum_z_kernel(count, shift, keep_ref, got_ref, send_ref, out_ref):
    bit = lax.rem(lax.div(lax.axis_index("zl"), shift), 2)
    half = count // 2

    def total(at):
        return keep_ref[at, :] + got_ref[at, :].astype(F32)

    for k in range(half):
        at = slice(k * TOK, (k + 1) * TOK)
        send_ref[at, :] = total(aligned((2 * k + 1 - bit) * TOK, TOK)).astype(BF)
    rows = stat_rows(stat_of(total(slice(count * TOK, count * TOK + 8))))
    send_ref[half * TOK :, :] = rows
    for k in range(half):
        at = slice(k * TOK, (k + 1) * TOK)
        out_ref[at, :] = total(aligned((2 * k + bit) * TOK, TOK))
    out_ref[half * TOK :, :] = rows.astype(F32)


def sum_z(keep, got, count, shift):
    rows = count // 2 * TOK + 8
    return call(
        functools.partial(sum_z_kernel, count, shift),
        (jax.ShapeDtypeStruct((rows, B), BF), jax.ShapeDtypeStruct((rows, B), F32)),
        (keep, got),
        6,
        count * TOK * B,
        count * MB // 2,
        in_specs=[VM, VM],
        out_specs=(VM, VM),
        name=f"sum_z{shift}",
    )


def finish_kernel(keep_ref, got_ref, h_ref, g_ref, rinv_ref, out_ref, gain_ref, g32):
    own = lax.axis_index("zl") * NX + lax.axis_index("x")
    g32[...] = g_ref[...].astype(F32)
    grad = keep_ref[:TOK, :] + got_ref[:TOK, :].astype(F32)
    stat = stat_of(keep_ref[TOK:, :] + got_ref[TOK:, :].astype(F32))
    stat = jnp.sum(jnp.where(eye(), stat, 0.0), axis=1, keepdims=True) / D
    rinv = rinv_ref[...]
    xhat = h_ref[:, aligned(own * B, B)].astype(F32) * rinv
    total = jnp.sum(grad * xhat, axis=0, keepdims=True)
    for i in range(NY * NH * NC):
        gain_ref[i] = total
    out_ref[...] = (rinv * (grad * two_rows(g32, own) - xhat * stat)).astype(BF)


def finish(keep, got, hidden, gain, rinv):
    return call(
        finish_kernel,
        (
            jax.ShapeDtypeStruct((TOK, B), BF),
            jax.ShapeDtypeStruct((NY * NH * NC, 1, B), F32),
        ),
        (keep, got, hidden, gain, rinv),
        10,
        TOK * B * 16,
        MB,
        in_specs=[VM] * 5,
        out_specs=(VM, VM),
        scratch_shapes=[pltpu.VMEM((64, 128), F32)],
        name="finish",
    )


STEPS = 4


def product_kernel(own_ref, got_ref, q_ref, gq_ref, left_ref, right_ref, keep_ref):
    i = pl.program_id(0)
    a = jnp.concatenate([own_ref[...], got_ref[...]], axis=0)
    q = jnp.concatenate([q_ref[...], gq_ref[...]], axis=0)
    p = lax.dot_general(q, a, (((0,), (0,)), ((), ())), preferred_element_type=F32).astype(BF)

    @pl.when(i < STEPS // 2)
    def _():
        left_ref[...] = p[:128, :]
        right_ref[...] = p[128:, :]

    @pl.when(i >= STEPS // 2)
    def _():
        keep_ref[...] = p


def product(own, got, q_grad):
    w = 16 * B // STEPS
    half = jax.ShapeDtypeStruct((128, 8 * B), BF)
    first = lambda i: (0, jnp.minimum(i, STEPS // 2 - 1))
    return call(
        product_kernel,
        (half, half, jax.ShapeDtypeStruct((B, 8 * B), BF)),
        (own, got, q_grad, got),
        16,
        2 * TOK * D * B,
        4 * MB,
        grid=(STEPS,),
        in_specs=[
            pl.BlockSpec((TOK, w), lambda i: (0, i)),
            pl.BlockSpec((TOK, w), lambda i: (0, i)),
            pl.BlockSpec((TOK, B), lambda i: (0, 0)),
            pl.BlockSpec((TOK, B), lambda i: (0, 16)),
        ],
        out_specs=(
            pl.BlockSpec((128, w), first),
            pl.BlockSpec((128, w), first),
            pl.BlockSpec((B, w), lambda i: (0, jnp.maximum(i - STEPS // 2, 0))),
        ),
        name="product",
    )


def sum_y_kernel(keep_ref, left_ref, right_ref, out_ref):
    for k in range(4):
        at = slice(k * 512, (k + 1) * 512)
        out_ref[k, :128, :] = (keep_ref[:128, at].astype(F32) + left_ref[:, at].astype(F32)).astype(BF)
        out_ref[k, 128:, :] = (keep_ref[128:, at].astype(F32) + right_ref[:, at].astype(F32)).astype(BF)


def sum_y(keep, left, right):
    return call(
        sum_y_kernel,
        jax.ShapeDtypeStruct((4, B, 512), BF),
        (keep, left, right),
        8,
        TOK * D,
        3 * MB,
        in_specs=[VM] * 3,
        out_specs=VM,
        name="sum_y",
    )


def sum_y4_kernel(in_ref, send_ref, keep_ref):
    zh = lax.axis_index("zh")

    def total(z):
        at = aligned(z * B, B)
        s = in_ref[0, :, at].astype(F32)
        for k in range(1, 4):
            s = s + in_ref[k, :, at].astype(F32)
        return s

    send_ref[...] = total(1 - zh).astype(BF)
    keep_ref[...] = total(zh)


def sum_y4(got):
    return call(
        sum_y4_kernel,
        (jax.ShapeDtypeStruct((B, B), BF), jax.ShapeDtypeStruct((B, B), F32)),
        (got,),
        6,
        TOK * D,
        2 * MB,
        in_specs=[VM],
        out_specs=(VM, VM),
        name="sum_y4",
    )


def last_kernel(main_ref, keep_ref, got_ref, out_ref):
    s = keep_ref[...] + got_ref[...].astype(F32)
    out_ref[...] = main_ref[...] + s.T / (NY * NH * NC)


def last(main, keep, got):
    return call(
        last_kernel,
        jax.ShapeDtypeStruct((B, B), F32),
        (main, keep, got),
        4,
        B * B * 4,
        MB,
        in_specs=[VM] * 3,
        out_specs=VM,
        name="last",
    )


def pairs(n, f):
    return [(i, f(i) % n) for i in range(n)]


def swap(v, axis, n, f):
    return lax.ppermute(v, axis, pairs(n, f))


def exchange(v, axis, **kw):
    return lax.all_to_all(v, axis, 0, 0, tiled=True, **kw)


def body(hidden, gain, weight, q_grad, q_main, gain_main):
    gain2 = gain.reshape(64, 128)
    send, own, rinv = norm(hidden, gain2, q_grad)
    got = swap(send, "c", NC, lambda i: i ^ 1)
    part = partial(q_grad, weight, hidden, gain2, rinv)
    part = exchange(part, "x")

    left, right, keep = product(own, got, q_grad)
    left = swap(left, "y", NY, lambda i: i ^ 1)
    right = swap(right, "y", NY, lambda i: i + 1 if i % 2 else i - 1)

    send1, keep1 = sum_x(part)
    got1 = swap(send1, "zl", NZ, lambda i: i ^ 1)

    four = sum_y(keep, left, right)
    four = exchange(four, "y", axis_index_groups=[[0, 2, 4, 6], [1, 3, 5, 7]])

    send2, keep2 = sum_z(keep1, got1, 4, 2)
    got2 = swap(send2, "zl", NZ, lambda i: i ^ 2)
    send3, keep3 = sum_z(keep2, got2, 2, 4)
    got3 = swap(send3, "zl", NZ, lambda i: i ^ 4)
    grad, all_gain = finish(keep3, got3, hidden, gain2, rinv)
    all_gain = exchange(all_gain, ("y", "zh", "c"))

    send_h, keep_h = sum_y4(four)
    got_h = swap(send_h, "zh", NH, lambda i: i ^ 1)
    q_new = last(q_main, keep_h, got_h)
    gain_new = gain_main + jnp.sum(all_gain, axis=(0, 1)) / (NY * NH * NC)
    return grad, q_new, gain_new


def solution(mesh):
    fine = Mesh(mesh.devices.reshape(NY, NH, NC, NZ, NX), ("y", "zh", "c", "zl", "x"))
    dp, tp = ("y", "zh", "c"), ("zl", "x")
    in_specs = (P(dp, None), P(), P(None, tp), P(dp, tp), P(dp, tp), P(tp))
    out_specs = (P(dp, tp), P(dp, tp), P(tp))
    return jax.shard_map(body, mesh=fine, in_specs=in_specs, out_specs=out_specs, check_vma=False)
```

time: 283 us -> 170 us (0.60)
  waiting for transfers between devices: 208 us -> 63.9 us
  starting transfers between devices: 39 us -> 80.7 us
  between operations: 14.1 us -> 0.83 us
  Pallas kernels: 0 us -> 10.8 us
  other arithmetic: 9.77 us -> 0.62 us
  matrix products: 7.08 us -> 0 us
  local copies, waits for them, and re-layouts: 3.73 us -> 9.93 us
    all_to_all x3, waiting for transfers between devices: 148 us -> 40.5 us  [exchange(): return lax.all_to_all(v, axis, 0, 0, tiled=True, **kw)]
    reduce_scatter x1 -> x0, waiting for transfers between devices: 60.6 us -> none  [body(): lax.psum_scatter((product / ndp).astype(jnp.bfloat16), 'dp', scatter_dime...]
    ppermute x0 -> x7, starting transfers between devices: none -> 57 us  [swap(): return lax.ppermute(v, axis, pairs(n, f))]
    ppermute x0 -> x7, waiting for transfers between devices: none -> 23.4 us  [swap(): return lax.ppermute(v, axis, pairs(n, f))]
    all_to_all x3, starting transfers between devices: 39 us -> 23.7 us  [exchange(): return lax.all_to_all(v, axis, 0, 0, tiled=True, **kw)]
    pallas_call x0 -> x10, Pallas kernels: none -> 10.8 us  [call(): pl.pallas_call(kernel, out_shape=out_shape, compiler_params=params(mib),...]
    unnamed x10 -> x30, local copies, waits for them, and re-layouts: 0.86 us -> 9.93 us
    dot_general x2 -> x0, matrix products: 7.08 us -> none  [the longest x1 3.67 us: body(): lax.dot_general(q_grad, q_weight, (((1,), (1,)), ((), ())), preferred_ele...]
  transfers between devices with their start and end apart: 4 -> 10, of which waited for: 3 -> 6; matrix products, arithmetic and copies ran while one was open for 5% -> 0% of each run, Pallas kernels for 0% -> 4%
where the time goes in v1:
time: 170 us; the launch traced here: 167 us
  starting transfers between devices  80.7 us (47%)
  waiting for transfers between devices  63.9 us (38%)
  Pallas kernels  10.8 us (6%)
  local copies, waits for them, and re-layouts  9.93 us (6%)
    ppermute x7, starting transfers between devices, swap(): return lax.ppermute(v, axis, pairs(n, f))  57 us
    all_to_all x3, waiting for transfers between devices, exchange(): return lax.all_to_all(v, axis, 0, 0, tiled=True, **kw)  40.5 us
    all_to_all x3, starting transfers between devices, exchange(): return lax.all_to_all(v, axis, 0, 0, tiled=True, **kw)  23.7 us
    ppermute x7, waiting for transfers between devices, swap(): return lax.ppermute(v, axis, pairs(n, f))  23.4 us
    pallas_call x10, Pallas kernels, call(): pl.pallas_call(kernel, out_shape=out_shape, compiler_params=params(mib),...  10.8 us
    unnamed x30, local copies, waits for them, and re-layouts  9.93 us
  transfers between devices with their start and end apart: 10, of which 6 were waited for; matrix products, arithmetic and copies ran while one was open for 0% of the time, Pallas kernels for 4%

profile of v1, /device:TPU:1, one launch (start us, length us, event | category | flops | bytes accessed | tf_op | source)
XLA Modules:
  0.0 166.8 jit_solution(11456036157265605067)
XLA Ops:
  0.6 0.0 copy-start
  0.6 1.6 copy-done
  2.2 0.0 copy-start.8
  2.2 0.8 copy-done.8
  3.1 0.0 copy-start.11
  3.1 0.7 copy-done.11
  3.8 0.0 copy-start.1
  3.8 0.0 copy-start.9
  3.8 0.0 copy-start.12
  3.8 1.0 norm.1
  4.8 0.0 copy-start.6
  4.8 1.0 copy-done.6
  5.8 0.0 copy-start.13
  5.8 1.0 copy-done.13
  6.8 0.0 copy-done.1
  6.8 0.0 copy-done.9
  6.8 0.0 copy-done.12
  6.8 0.0 copy-start.3
  6.8 2.2 %copy-done.3 = bf16[8192,256]{1,0:T(8,128)(2,1)S(1)} copy-done((bf16[8192,256]{1,0:T(8,128)(2,1)S(1)}, bf16[8192,256]{1,0:T(8,128)(2,1)}, u32[]{:S(2)}) %copy-start.3) | copy-done | bytes 4194328
  9.0 1.7 %partial.1 = bf16[4,1032,256]{2,1,0:T(8,128)(2,1)S(1)} custom-call(bf16[128,256]{1,0:T(8,128)(2,1)S(1)} %copy-done.9, bf16[8192,256]{1,0:T(8,128)(2,1)S(1)} %copy-done.3, bf16[128,8192]{1,0:T(8,128)(2,1)S(1)} %copy-done.1, bf16[64,128]{1,0:T(8,128)(2,1)S(1)} %bitcast.2, f32[128,1]{1,0:T(8,128)S(1)} %get-tuple-element.19.rinv_ref), custom_call_target="tpu_custom_call" | custom-call | flops 536870912 | bytes 8388608 | tf_op jit(solution)/shard_map/partial/pallas_call | solution.py:30
  10.8 0.0 copy-start.2
  10.8 1.3 copy-done.2
  12.1 4.8 %all-to-all-start = ((bf16[4,1032,256]{2,1,0:T(8,128)(2,1)}), bf16[4,1032,256]{2,1,0:T(8,128)(2,1)}, u32[]{:S(2)}, u32[]{:S(2)}) async-start(bf16[4,1032,256]{2,1,0:T(8,128)(2,1)} %copy-done.2), calls=%async_computation | async-start | bytes 4227072 | tf_op jit(solution)/shard_map/all_to_all | solution.py:365
  16.9 15.7 %collective-permute-start.3 = (bf16[128,4352]{1,0:T(8,128)(2,1)}, bf16[128,4352]{1,0:T(8,128)(2,1)S(1)}, u32[]{:S(2)}, u32[]{:S(2)}) collective-permute-start(bf16[128,4352]{1,0:T(8,128)(2,1)} %copy-done.13), channel_id=1, source_target_pairs={{0,32},{32,0},{1,33},{33,1},{2,34},{34,2},{3,35},{35,3},{4,36},{36... | collective-permute-start | bytes 3342344 | tf_op jit(solution)/shard_map/ppermute | solution.py:361
  32.6 0.1 all-to-all-done.in_ref
  32.7 0.0 copy-start.7
  32.7 1.9 %sum_x.1 = (bf16[520,256]{1,0:T(8,128)(2,1)S(1)}, f32[520,256]{1,0:T(8,128)S(1)}) custom-call(bf16[4,1032,256]{2,1,0:T(8,128)(2,1)} %all-to-all-done.in_ref), custom_call_target="tpu_custom_call" | custom-call | flops 1048576 | bytes 4194304 | tf_op jit(solution)/shard_map/sum_x/pallas_call | solution.py:30
  34.6 14.7 %collective-permute-start = (bf16[520,256]{1,0:T(8,128)(2,1)S(1)}, bf16[520,256]{1,0:T(8,128)(2,1)S(1)}, u32[]{:S(2)}, u32[]{:S(2)}) collective-permute-start(bf16[520,256]{1,0:T(8,128)(2,1)S(1)} %get-tuple-element.21), channel_id=1, source_target_pairs={{0,4},{4,0},{8,12},{12,8},{16,20},{20,16},{24,28},{28,24},{1,5},{5... | collective-permute-start | bytes 798728 | tf_op jit(solution)/shard_map/ppermute | solution.py:361
  49.3 0.0 collective-permute-done.3.got_ref.gq_ref
  49.3 0.0 copy-done.7
  49.4 3.1 %product.1 = (bf16[128,2048]{1,0:T(8,128)(2,1)}, bf16[128,2048]{1,0:T(8,128)(2,1)}, bf16[256,2048]{1,0:T(8,128)(2,1)S(1)}) custom-call(bf16[128,4096]{1,0:T(8,128)(2,1)S(1)} %copy-done.7, bf16[128,4352]{1,0:T(8,128)(2,1)S(1)} %collective-permute-done.3.got_ref.gq_ref, bf16[128,256]{1,0:T(8,128)(2,1)S(1)} %copy-done.9, ...), custom_call_target="tpu_custom_call" | custom-call | flops 536870912 | bytes 4194304 | tf_op jit(solution)/shard_map/product/pallas_call | solution.py:30
  52.4 0.0 copy-start.4
  52.4 3.2 %collective-permute-start.4 = (bf16[128,2048]{1,0:T(8,128)(2,1)}, bf16[128,2048]{1,0:T(8,128)(2,1)S(1)}, u32[]{:S(2)}, u32[]{:S(2)}) collective-permute-start(bf16[128,2048]{1,0:T(8,128)(2,1)} %get-tuple-element.30), channel_id=1, source_target_pairs={{0,128},{128,0},{256,384},{384,256},{512,640},{640,512},{768,896},... | collective-permute-start | bytes 1572872 | tf_op jit(solution)/shard_map/ppermute | solution.py:361
  55.6 4.9 %collective-permute-start.5 = (bf16[128,2048]{1,0:T(8,128)(2,1)}, bf16[128,2048]{1,0:T(8,128)(2,1)S(1)}, u32[]{:S(2)}, u32[]{:S(2)}) collective-permute-start(bf16[128,2048]{1,0:T(8,128)(2,1)} %get-tuple-element.31), channel_id=1, source_target_pairs={{0,896},{128,256},{256,128},{384,512},{512,384},{640,768},{768,640... | collective-permute-start | bytes 1572872 | tf_op jit(solution)/shard_map/ppermute | solution.py:361
  60.5 0.0 collective-permute-done.got_ref
  60.5 0.1 sum_z2.1
  60.6 5.8 %collective-permute-start.1 = (bf16[264,256]{1,0:T(8,128)(2,1)S(1)}, bf16[264,256]{1,0:T(8,128)(2,1)S(1)}, u32[]{:S(2)}, u32[]{:S(2)}) collective-permute-start(bf16[264,256]{1,0:T(8,128)(2,1)S(1)} %get-tuple-element.23), channel_id=1, source_target_pairs={{0,8},{4,12},{8,0},{12,4},{16,24},{20,28},{24,16},{28,20},{1,9},{5... | collective-permute-start | bytes 405512 | tf_op jit(solution)/shard_map/ppermute | solution.py:361
  66.4 5.8 %collective-permute-done.1.got_ref = bf16[264,256]{1,0:T(8,128)(2,1)S(1)} collective-permute-done((bf16[264,256]{1,0:T(8,128)(2,1)S(1)}, bf16[264,256]{1,0:T(8,128)(2,1)S(1)}, u32[]{:S(2)}, u32[]{:S(2)}) %collective-permute-start.1) | collective-permute-done | bytes 135200 | tf_op jit(solution)/shard_map/ppermute | solution.py:361
  72.3 10.6 %collective-permute-start.2 = (bf16[136,256]{1,0:T(8,128)(2,1)S(1)}, bf16[136,256]{1,0:T(8,128)(2,1)S(1)}, u32[]{:S(2)}, u32[]{:S(2)}) collective-permute-start(bf16[136,256]{1,0:T(8,128)(2,1)S(1)} %get-tuple-element.25), channel_id=1, source_target_pairs={{0,16},{4,20},{8,24},{12,28},{16,0},{20,4},{24,8},{28,12},{1,17},{... | collective-permute-start | bytes 208904 | tf_op jit(solution)/shard_map/ppermute | solution.py:361
  82.9 4.6 %collective-permute-done.2.got_ref = bf16[136,256]{1,0:T(8,128)(2,1)S(1)} collective-permute-done((bf16[136,256]{1,0:T(8,128)(2,1)S(1)}, bf16[136,256]{1,0:T(8,128)(2,1)S(1)}, u32[]{:S(2)}, u32[]{:S(2)}) %collective-permute-start.2) | collective-permute-done | bytes 69664 | tf_op jit(solution)/shard_map/ppermute | solution.py:361
  87.5 0.8 finish.1
  88.2 0.0 copy-done.4
  88.2 15.4 %all-to-all-start.2 = ((f32[32,1,256]{2,1,0:T(1,128)}), f32[32,1,256]{2,1,0:T(1,128)S(1)}, u32[]{:S(2)}, u32[]{:S(2)}) async-start(f32[32,1,256]{2,1,0:T(1,128)} %get-tuple-element.34), calls=%async_computation.2 | async-start | bytes 65536 | tf_op jit(solution)/shard_map/all_to_all | solution.py:365
  103.6 0.0 collective-permute-done.4.left_ref
  103.6 0.0 collective-permute-done.5.right_ref
  103.6 0.0 copy-start.5
  103.7 1.2 copy-done.5
  104.9 1.2 sum_y.1
  106.1 0.0 copy-start.14
  106.1 0.0 copy-start.10
  106.1 14.4 %all-to-all-done.2 = f32[32,1,256]{2,1,0:T(1,128)S(1)} async-done(((f32[32,1,256]{2,1,0:T(1,128)}), f32[32,1,256]{2,1,0:T(1,128)S(1)}, u32[]{:S(2)}, u32[]{:S(2)}) %all-to-all-start.2) | async-done | bytes 32800 | tf_op jit(solution)/shard_map/all_to_all | solution.py:365
  120.5 3.5 %all-to-all-start.1 = ((bf16[4,256,512]{2,1,0:T(8,128)(2,1)}), bf16[4,256,512]{2,1,0:T(8,128)(2,1)S(1)}, u32[]{:S(2)}, u32[]{:S(2)}) async-start(bf16[4,256,512]{2,1,0:T(8,128)(2,1)} %sum_y.1), calls=%async_computation.1 | async-start | bytes 2097152 | tf_op jit(solution)/shard_map/all_to_all | solution.py:365
  124.0 0.1 reduce_sum.9
  124.0 26.1 %all-to-all-done.1.in_ref = bf16[4,256,512]{2,1,0:T(8,128)(2,1)S(1)} async-done(((bf16[4,256,512]{2,1,0:T(8,128)(2,1)}), bf16[4,256,512]{2,1,0:T(8,128)(2,1)S(1)}, u32[]{:S(2)}, u32[]{:S(2)}) %all-to-all-start.1) | async-done | bytes 1048608 | tf_op jit(solution)/shard_map/all_to_all | solution.py:365
  150.1 0.1 sum_y4.1
  150.2 2.2 %collective-permute-start.6 = (bf16[256,256]{1,0:T(8,128)(2,1)S(1)}, bf16[256,256]{1,0:T(8,128)(2,1)S(1)}, u32[]{:S(2)}, u32[]{:S(2)}) collective-permute-start(bf16[256,256]{1,0:T(8,128)(2,1)S(1)} %get-tuple-element.33), channel_id=1, source_target_pairs={{0,64},{64,0},{1,65},{65,1},{2,66},{66,2},{3,67},{67,3},{4,68},{68... | collective-permute-start | bytes 393224 | tf_op jit(solution)/shard_map/ppermute | solution.py:361
  152.4 0.0 copy-done.14
  152.4 0.6 multiply_add_fusion
  153.0 12.9 %collective-permute-done.6.got_ref = bf16[256,256]{1,0:T(8,128)(2,1)S(1)} collective-permute-done((bf16[256,256]{1,0:T(8,128)(2,1)S(1)}, bf16[256,256]{1,0:T(8,128)(2,1)S(1)}, u32[]{:S(2)}, u32[]{:S(2)}) %collective-permute-start.6) | collective-permute-done | bytes 131104 | tf_op jit(solution)/shard_map/ppermute | solution.py:361
  165.9 0.0 copy-done.10
  165.9 0.8 last.1
  (1 shorter events, 0.0 us)
Async XLA Ops:
  0.6 1.6 copy-start
  2.2 0.8 copy-start.8
  3.1 0.7 copy-start.11
  3.8 3.1 %copy-start.1 = (bf16[128,8192]{1,0:T(8,128)(2,1)S(1)}, bf16[128,8192]{1,0:T(8,128)(2,1)}, u32[]{:S(2)}) copy-start(bf16[128,8192]{1,0:T(8,128)(2,1)} %h_ref.5) | copy-start | bytes 6291460
  3.8 3.1 %copy-start.9 = (bf16[128,256]{1,0:T(8,128)(2,1)S(1)}, bf16[128,256]{1,0:T(8,128)(2,1)}, u32[]{:S(2)}) copy-start(bf16[128,256]{1,0:T(8,128)(2,1)} %q_ref.5) | copy-start | bytes 196612
  3.8 3.1 %copy-start.12 = (bf16[8192]{0:T(1024)(128)(2,1)S(1)}, bf16[8192]{0:T(1024)(128)(2,1)}, u32[]{:S(2)}) copy-start(bf16[8192]{0:T(1024)(128)(2,1)} %param.7) | copy-start | bytes 49156
  4.8 1.0 copy-start.6
  5.8 1.0 copy-start.13
  6.8 2.2 %copy-start.3 = (bf16[8192,256]{1,0:T(8,128)(2,1)S(1)}, bf16[8192,256]{1,0:T(8,128)(2,1)}, u32[]{:S(2)}) copy-start(bf16[8192,256]{1,0:T(8,128)(2,1)} %w_ref.1) | copy-start | bytes 12582916
  10.8 1.3 copy-start.2
  12.1 20.6 %all-to-all-start = ((bf16[4,1032,256]{2,1,0:T(8,128)(2,1)}), bf16[4,1032,256]{2,1,0:T(8,128)(2,1)}, u32[]{:S(2)}, u32[]{:S(2)}) async-start(bf16[4,1032,256]{2,1,0:T(8,128)(2,1)} %copy-done.2), calls=%async_computation | async-start | bytes 4227072 | tf_op jit(solution)/shard_map/all_to_all | solution.py:365
  16.9 32.4 %collective-permute-start.3 = (bf16[128,4352]{1,0:T(8,128)(2,1)}, bf16[128,4352]{1,0:T(8,128)(2,1)S(1)}, u32[]{:S(2)}, u32[]{:S(2)}) collective-permute-start(bf16[128,4352]{1,0:T(8,128)(2,1)} %copy-done.13), channel_id=1, source_target_pairs={{0,32},{32,0},{1,33},{33,1},{2,34},{34,2},{3,35},{35,3},{4,36},{36... | collective-permute-start | bytes 3342344 | tf_op jit(solution)/shard_map/ppermute | solution.py:361
  32.7 16.7 %copy-start.7 = (bf16[128,4096]{1,0:T(8,128)(2,1)S(1)}, bf16[128,4096]{1,0:T(8,128)(2,1)}, u32[]{:S(2)}) copy-start(bf16[128,4096]{1,0:T(8,128)(2,1)} %copy-done.6) | copy-start | bytes 3145732
  34.6 25.9 %collective-permute-start = (bf16[520,256]{1,0:T(8,128)(2,1)S(1)}, bf16[520,256]{1,0:T(8,128)(2,1)S(1)}, u32[]{:S(2)}, u32[]{:S(2)}) collective-permute-start(bf16[520,256]{1,0:T(8,128)(2,1)S(1)} %get-tuple-element.21), channel_id=1, source_target_pairs={{0,4},{4,0},{8,12},{12,8},{16,20},{20,16},{24,28},{28,24},{1,5},{5... | collective-permute-start | bytes 798728 | tf_op jit(solution)/shard_map/ppermute | solution.py:361
  52.4 35.8 %copy-start.4 = (bf16[256,2048]{1,0:T(8,128)(2,1)}, bf16[256,2048]{1,0:T(8,128)(2,1)S(1)}, u32[]{:S(2)}) copy-start(bf16[256,2048]{1,0:T(8,128)(2,1)S(1)} %get-tuple-element.29.keep_ref) | copy-start | bytes 3145732
  52.4 51.2 %collective-permute-start.4 = (bf16[128,2048]{1,0:T(8,128)(2,1)}, bf16[128,2048]{1,0:T(8,128)(2,1)S(1)}, u32[]{:S(2)}, u32[]{:S(2)}) collective-permute-start(bf16[128,2048]{1,0:T(8,128)(2,1)} %get-tuple-element.30), channel_id=1, source_target_pairs={{0,128},{128,0},{256,384},{384,256},{512,640},{640,512},{768,896},... | collective-permute-start | bytes 1572872 | tf_op jit(solution)/shard_map/ppermute | solution.py:361
  55.6 48.0 %collective-permute-start.5 = (bf16[128,2048]{1,0:T(8,128)(2,1)}, bf16[128,2048]{1,0:T(8,128)(2,1)S(1)}, u32[]{:S(2)}, u32[]{:S(2)}) collective-permute-start(bf16[128,2048]{1,0:T(8,128)(2,1)} %get-tuple-element.31), channel_id=1, source_target_pairs={{0,896},{128,256},{256,128},{384,512},{512,384},{640,768},{768,640... | collective-permute-start | bytes 1572872 | tf_op jit(solution)/shard_map/ppermute | solution.py:361
  60.6 11.7 %collective-permute-start.1 = (bf16[264,256]{1,0:T(8,128)(2,1)S(1)}, bf16[264,256]{1,0:T(8,128)(2,1)S(1)}, u32[]{:S(2)}, u32[]{:S(2)}) collective-permute-start(bf16[264,256]{1,0:T(8,128)(2,1)S(1)} %get-tuple-element.23), channel_id=1, source_target_pairs={{0,8},{4,12},{8,0},{12,4},{16,24},{20,28},{24,16},{28,20},{1,9},{5... | collective-permute-start | bytes 405512 | tf_op jit(solution)/shard_map/ppermute | solution.py:361
  72.3 15.2 %collective-permute-start.2 = (bf16[136,256]{1,0:T(8,128)(2,1)S(1)}, bf16[136,256]{1,0:T(8,128)(2,1)S(1)}, u32[]{:S(2)}, u32[]{:S(2)}) collective-permute-start(bf16[136,256]{1,0:T(8,128)(2,1)S(1)} %get-tuple-element.25), channel_id=1, source_target_pairs={{0,16},{4,20},{8,24},{12,28},{16,0},{20,4},{24,8},{28,12},{1,17},{... | collective-permute-start | bytes 208904 | tf_op jit(solution)/shard_map/ppermute | solution.py:361
  88.2 32.2 %all-to-all-start.2 = ((f32[32,1,256]{2,1,0:T(1,128)}), f32[32,1,256]{2,1,0:T(1,128)S(1)}, u32[]{:S(2)}, u32[]{:S(2)}) async-start(f32[32,1,256]{2,1,0:T(1,128)} %get-tuple-element.34), calls=%async_computation.2 | async-start | bytes 65536 | tf_op jit(solution)/shard_map/all_to_all | solution.py:365
  103.6 1.2 copy-start.5
  106.1 46.3 %copy-start.14 = (f32[256]{0:T(256)S(1)}, f32[256]{0:T(256)}, u32[]{:S(2)}) copy-start(f32[256]{0:T(256)} %param.11) | copy-start | bytes 3076
  106.1 59.8 %copy-start.10 = (f32[256,256]{1,0:T(8,128)S(1)}, f32[256,256]{1,0:T(8,128)}, u32[]{:S(2)}) copy-start(f32[256,256]{1,0:T(8,128)} %main_ref.1) | copy-start | bytes 786436
  120.5 29.6 %all-to-all-start.1 = ((bf16[4,256,512]{2,1,0:T(8,128)(2,1)}), bf16[4,256,512]{2,1,0:T(8,128)(2,1)S(1)}, u32[]{:S(2)}, u32[]{:S(2)}) async-start(bf16[4,256,512]{2,1,0:T(8,128)(2,1)} %sum_y.1), calls=%async_computation.1 | async-start | bytes 2097152 | tf_op jit(solution)/shard_map/all_to_all | solution.py:365
  150.2 15.7 %collective-permute-start.6 = (bf16[256,256]{1,0:T(8,128)(2,1)S(1)}, bf16[256,256]{1,0:T(8,128)(2,1)S(1)}, u32[]{:S(2)}, u32[]{:S(2)}) collective-permute-start(bf16[256,256]{1,0:T(8,128)(2,1)S(1)} %get-tuple-element.33), channel_id=1, source_target_pairs={{0,64},{64,0},{1,65},{65,1},{2,66},{66,2},{3,67},{67,3},{4,68},{68... | collective-permute-start | bytes 393224 | tf_op jit(solution)/shard_map/ppermute | solution.py:361

commit v2 on v1

--- a/solution.py
+++ b/solution.py
@@ -23,7 +23,7 @@
 
 
 def params(mib):
-    return pltpu.CompilerParams(vmem_limit_bytes=mib * MB)
+    return pltpu.CompilerParams(vmem_limit_bytes=mib * MB if mib else None)
 
 
 def call(kernel, out_shape, args, mib, flops, nbytes, **kw):
@@ -77,7 +77,7 @@
             jax.ShapeDtypeStruct((TOK, 1), F32),
         ),
         (hidden, gain, q_grad),
-        16,
+        None,
         6 * TOK * D,
         4 * TOK * D,
         grid=(TOK // ROWS,),
@@ -106,63 +106,112 @@
     return both[:, :128] + both[:, 128:]
 
 
-def partial_kernel(q_ref, w_ref, h_ref, g_ref, rinv_ref, out_ref):
+ZQ = NZ // 2
+NG = 2 * NX
+PIECE = ZQ * TOK + 8
+
+
+def partial_kernel(q_ref, g_ref, w_hbm, h_hbm, out_hbm, w_ref, h_ref, out_ref, w_sem, h_sem, out_sem):
+    wide = NX * B
+
+    def w_copy(z):
+        at = slice(z * wide, (z + 1) * wide)
+        return pltpu.make_async_copy(w_hbm.at[at, :], w_ref.at[at, :], w_sem.at[z])
+
+    def h_copy(z):
+        at = slice(z * wide, (z + 1) * wide)
+        return pltpu.make_async_copy(h_hbm.at[:, at], h_ref.at[:, at], h_sem.at[z])
+
+    def out_copy(z, x):
+        at = (z % 2 * NX + x, slice(z // 2 * TOK, (z // 2 + 1) * TOK))
+        return pltpu.make_async_copy(out_ref.at[at], out_hbm.at[at], out_sem.at[z * NX + x])
+
+    def stat_copy(d):
+        at = (d, slice(ZQ * TOK, PIECE))
+        return pltpu.make_async_copy(out_ref.at[at], out_hbm.at[at], out_sem.at[NZ * NX + d])
+
+    for z in range(NZ):
+        w_copy(z).start()
+        h_copy(z).start()
     q = q_ref[...]
     g = g_ref[...].astype(F32)
     acc = jnp.zeros((TOK, 128), F32)
     for z in range(NZ):
+        w_copy(z).wait()
+        h_copy(z).wait()
         for x in range(NX):
             b = z * NX + x
             at = slice(b * B, (b + 1) * B)
             p = lax.dot_general(q, w_ref[at, :], (((1,), (1,)), ((), ())), preferred_element_type=F32)
             p = p.astype(BF)
-            out_ref[x, z * TOK : (z + 1) * TOK, :] = p
+            out_ref[z % 2 * NX + x, z // 2 * TOK : (z // 2 + 1) * TOK, :] = p
             t = p.astype(F32) * h_ref[:, at].astype(F32)
             acc = acc + t[:, :128] * g[2 * b : 2 * b + 1, :] + t[:, 128:] * g[2 * b + 1 : 2 * b + 2, :]
-    s = jnp.sum(acc, axis=1, keepdims=True) * rinv_ref[...]
+        if z > 0:
+            for x in range(NX):
+                out_copy(z - 1, x).start()
+    s = jnp.sum(acc, axis=1, keepdims=True)
     rows = stat_rows(jnp.sum(jnp.where(eye(), s, 0.0), axis=0, keepdims=True))
+    for d in range(NG):
+        out_ref[d, ZQ * TOK :, :] = rows
     for x in range(NX):
-        out_ref[x, NZ * TOK :, :] = rows
-
-
-def partial(q_grad, weight, hidden, gain, rinv):
+        out_copy(NZ - 1, x).start()
+    for d in range(NG):
+        stat_copy(d).start()
+    for z in range(NZ):
+        for x in range(NX):
+            out_copy(z, x).wait()
+    for d in range(NG):
+        stat_copy(d).wait()
+
+
+HBM = pl.BlockSpec(memory_space=pltpu.HBM)
+
+
+def partial(q_grad, weight, hidden, gain):
     return call(
         partial_kernel,
-        jax.ShapeDtypeStruct((NX, NZ * TOK + 8, B), BF),
-        (q_grad, weight, hidden, gain, rinv),
-        24,
+        jax.ShapeDtypeStruct((NG, PIECE, B), BF),
+        (q_grad, gain, weight, hidden),
+        None,
         2 * TOK * D * B,
         8 * MB,
-        in_specs=[VM] * 5,
-        out_specs=VM,
+        in_specs=[VM, VM, HBM, HBM],
+        out_specs=HBM,
+        scratch_shapes=[
+            pltpu.VMEM((D, B), BF),
+            pltpu.VMEM((TOK, D), BF),
+            pltpu.VMEM((NG, PIECE, B), BF),
+            pltpu.SemaphoreType.DMA((NZ,)),
+            pltpu.SemaphoreType.DMA((NZ,)),
+            pltpu.SemaphoreType.DMA((NZ * NX + NG,)),
+        ],
         name="partial",
     )
 
 
-def sum_x_kernel(in_ref, send_ref, keep_ref):
-    bit = lax.rem(lax.axis_index("zl"), 2)
+def sum_xz_kernel(in_ref, send_ref, keep_ref):
+    bit = lax.rem(lax.div(lax.axis_index("zl"), 2), 2)
 
     def total(at):
         s = in_ref[0, at, :].astype(F32)
-        for x in range(1, NX):
-            s = s + in_ref[x, at, :].astype(F32)
+        for d in range(1, NG):
+            s = s + in_ref[d, at, :].astype(F32)
         return s
 
-    for k in range(4):
+    rows = stat_rows(stat_of(total(slice(ZQ * TOK, PIECE))))
+    for k in range(ZQ // 2):
         at = slice(k * TOK, (k + 1) * TOK)
         send_ref[at, :] = total(aligned((2 * k + 1 - bit) * TOK, TOK)).astype(BF)
-    rows = stat_rows(stat_of(total(slice(NZ * TOK, NZ * TOK + 8))))
-    send_ref[4 * TOK :, :] = rows
-    for k in range(4):
-        at = slice(k * TOK, (k + 1) * TOK)
         keep_ref[at, :] = total(aligned((2 * k + bit) * TOK, TOK))
-    keep_ref[4 * TOK :, :] = rows.astype(F32)
-
-
-def sum_x(got):
-    rows = 4 * TOK + 8
-    return call(
-        sum_x_kernel,
+    send_ref[ZQ // 2 * TOK :, :] = rows
+    keep_ref[ZQ // 2 * TOK :, :] = rows.astype(F32)
+
+
+def sum_xz(got):
+    rows = ZQ // 2 * TOK + 8
+    return call(
+        sum_xz_kernel,
         (jax.ShapeDtypeStruct((rows, B), BF), jax.ShapeDtypeStruct((rows, B), F32)),
         (got,),
         12,
@@ -170,7 +219,7 @@
         4 * MB,
         in_specs=[VM],
         out_specs=(VM, VM),
-        name="sum_x",
+        name="sum_xz",
     )
 
 
@@ -212,8 +261,8 @@
     g32[...] = g_ref[...].astype(F32)
     grad = keep_ref[:TOK, :] + got_ref[:TOK, :].astype(F32)
     stat = stat_of(keep_ref[TOK:, :] + got_ref[TOK:, :].astype(F32))
-    stat = jnp.sum(jnp.where(eye(), stat, 0.0), axis=1, keepdims=True) / D
     rinv = rinv_ref[...]
+    stat = jnp.sum(jnp.where(eye(), stat, 0.0), axis=1, keepdims=True) * rinv / D
     xhat = h_ref[:, aligned(own * B, B)].astype(F32) * rinv
     total = jnp.sum(grad * xhat, axis=0, keepdims=True)
     for i in range(NY * NH * NC):
@@ -286,10 +335,8 @@
 
 
 def sum_y_kernel(keep_ref, left_ref, right_ref, out_ref):
-    for k in range(4):
-        at = slice(k * 512, (k + 1) * 512)
-        out_ref[k, :128, :] = (keep_ref[:128, at].astype(F32) + left_ref[:, at].astype(F32)).astype(BF)
-        out_ref[k, 128:, :] = (keep_ref[128:, at].astype(F32) + right_ref[:, at].astype(F32)).astype(BF)
+    out_ref[0, :128, :] = (keep_ref[:128, :].astype(F32) + left_ref[...].astype(F32)).astype(BF)
+    out_ref[0, 128:, :] = (keep_ref[128:, :].astype(F32) + right_ref[...].astype(F32)).astype(BF)
 
 
 def sum_y(keep, left, right):
@@ -300,8 +347,13 @@
         8,
         TOK * D,
         3 * MB,
-        in_specs=[VM] * 3,
-        out_specs=VM,
+        grid=(4,),
+        in_specs=[
+            pl.BlockSpec((B, 512), lambda k: (0, k)),
+            pl.BlockSpec((128, 512), lambda k: (0, k)),
+            pl.BlockSpec((128, 512), lambda k: (0, k)),
+        ],
+        out_specs=pl.BlockSpec((1, B, 512), lambda k: (k, 0, 0)),
         name="sum_y",
     )
 
@@ -367,23 +419,22 @@
 
 def body(hidden, gain, weight, q_grad, q_main, gain_main):
     gain2 = gain.reshape(64, 128)
+    part = partial(q_grad, weight, hidden, gain2)
+    groups = [list(range(i * NG, (i + 1) * NG)) for i in range(NZ * NX // NG)]
+    part = exchange(part, ("zl", "x"), axis_index_groups=groups)
+
     send, own, rinv = norm(hidden, gain2, q_grad)
     got = swap(send, "c", NC, lambda i: i ^ 1)
-    part = partial(q_grad, weight, hidden, gain2, rinv)
-    part = exchange(part, "x")
-
     left, right, keep = product(own, got, q_grad)
     left = swap(left, "y", NY, lambda i: i ^ 1)
     right = swap(right, "y", NY, lambda i: i + 1 if i % 2 else i - 1)
 
-    send1, keep1 = sum_x(part)
-    got1 = swap(send1, "zl", NZ, lambda i: i ^ 1)
+    send2, keep2 = sum_xz(part)
+    got2 = swap(send2, "zl", NZ, lambda i: i ^ 2)
 
     four = sum_y(keep, left, right)
     four = exchange(four, "y", axis_index_groups=[[0, 2, 4, 6], [1, 3, 5, 7]])
 
-    send2, keep2 = sum_z(keep1, got1, 4, 2)
-    got2 = swap(send2, "zl", NZ, lambda i: i ^ 2)
     send3, keep3 = sum_z(keep2, got2, 2, 4)
     got3 = swap(send3, "zl", NZ, lambda i: i ^ 4)
     grad, all_gain = finish(keep3, got3, hidden, gain2, rinv)

time: 170 us -> 129 us (0.76); the launches traced: 167 us -> 128 us
  starting transfers between devices: 80.7 us -> 55 us
  waiting for transfers between devices: 63.9 us -> 47.8 us
  Pallas kernels: 10.8 us -> 16.4 us
  local copies, waits for them, and re-layouts: 9.93 us -> 7.31 us
    ppermute x7 -> x6, starting transfers between devices: 57 us -> 35.9 us  [swap(): return lax.ppermute(v, axis, pairs(n, f))]
    all_to_all x3, waiting for transfers between devices: 40.5 us -> 25.9 us  [exchange(): return lax.all_to_all(v, axis, 0, 0, tiled=True, **kw)]
    pallas_call x10 -> x9, Pallas kernels: 10.8 us -> 16.4 us  [call(): pl.pallas_call(kernel, out_shape=out_shape, compiler_params=params(mib),...]
    all_to_all x3, starting transfers between devices: 23.7 us -> 19.1 us  [exchange(): return lax.all_to_all(v, axis, 0, 0, tiled=True, **kw)]
    unnamed x30 -> x26, local copies, waits for them, and re-layouts: 9.93 us -> 7.31 us
    ppermute x7 -> x6, waiting for transfers between devices: 23.4 us -> 21.9 us  [swap(): return lax.ppermute(v, axis, pairs(n, f))]
  transfers between devices with their start and end apart: 10 -> 9, of which waited for: 6 -> 6; matrix products, arithmetic and copies ran while one was open for 0% -> 0% of each run, Pallas kernels for 4% -> 8%
where the time goes in v2:
time: 129 us; the launch traced here: 128 us
  starting transfers between devices  55 us (43%)
  waiting for transfers between devices  47.8 us (37%)
  Pallas kernels  16.4 us (13%)
  local copies, waits for them, and re-layouts  7.31 us (6%)
    ppermute x6, starting transfers between devices, swap(): return lax.ppermute(v, axis, pairs(n, f))  35.9 us
    all_to_all x3, waiting for transfers between devices, exchange(): return lax.all_to_all(v, axis, 0, 0, tiled=True, **kw)  25.9 us
    ppermute x6, waiting for transfers between devices, swap(): return lax.ppermute(v, axis, pairs(n, f))  21.9 us
    all_to_all x3, starting transfers between devices, exchange(): return lax.all_to_all(v, axis, 0, 0, tiled=True, **kw)  19.1 us
    pallas_call x9, Pallas kernels, call(): pl.pallas_call(kernel, out_shape=out_shape, compiler_params=params(mib),...  16.4 us
    unnamed x26, local copies, waits for them, and re-layouts  7.31 us
  transfers between devices with their start and end apart: 9, of which 6 were waited for; matrix products, arithmetic and copies ran while one was open for 0% of the time, Pallas kernels for 8%

profile of v2, /device:TPU:1, one launch (start us, length us, event | category | flops | bytes accessed | tf_op | source)
XLA Modules:
  0.0 127.9 jit_solution(11326985162001486860)
XLA Ops:
  0.6 6.0 %partial.1 = bf16[8,520,256]{2,1,0:T(8,128)(2,1)} custom-call(bf16[128,256]{1,0:T(8,128)(2,1)} %q_ref.5, bf16[64,128]{1,0:T(8,128)(2,1)} %bitcast.1, bf16[8192,256]{1,0:T(8,128)(2,1)} %w_hbm.1, bf16[128,8192]{1,0:T(8,128)(2,1)} %h_ref.3), custom_call_target="tpu_custom_call" | custom-call | flops 536870912 | bytes 8388608 | tf_op jit(solution)/shard_map/partial/pallas_call | solution.py:30
  6.6 6.7 %all-to-all-start = ((bf16[8,520,256]{2,1,0:T(8,128)(2,1)}), bf16[8,520,256]{2,1,0:T(8,128)(2,1)S(1)}, u32[]{:S(2)}, u32[]{:S(2)}) async-start(bf16[8,520,256]{2,1,0:T(8,128)(2,1)} %partial.1), calls=%async_computation | async-start | bytes 4259840 | tf_op jit(solution)/shard_map/all_to_all | solution.py:417
  13.3 0.0 copy-start.4
  13.3 3.3 %norm.1 = (bf16[128,4352]{1,0:T(8,128)(2,1)}, bf16[128,4096]{1,0:T(8,128)(2,1)}, f32[128,1]{1,0:T(8,128)}) custom-call(bf16[128,8192]{1,0:T(8,128)(2,1)} %h_ref.3, bf16[64,128]{1,0:T(8,128)(2,1)} %bitcast.2, bf16[128,256]{1,0:T(8,128)(2,1)} %q_ref.5), custom_call_target="tpu_custom_call" | custom-call | flops 6291456 | bytes 4194304 | tf_op jit(solution)/shard_map/norm/pallas_call | solution.py:30
  16.5 13.0 %collective-permute-start.2 = (bf16[128,4352]{1,0:T(8,128)(2,1)}, bf16[128,4352]{1,0:T(8,128)(2,1)S(1)}, u32[]{:S(2)}, u32[]{:S(2)}) collective-permute-start(bf16[128,4352]{1,0:T(8,128)(2,1)} %get-tuple-element.24), channel_id=1, source_target_pairs={{0,32},{32,0},{1,33},{33,1},{2,34},{34,2},{3,35},{35,3},{4,36},{36... | collective-permute-start | bytes 3342344 | tf_op jit(solution)/shard_map/ppermute | solution.py:413
  29.5 2.6 %collective-permute-done.2.got_ref.gq_ref = bf16[128,4352]{1,0:T(8,128)(2,1)S(1)} collective-permute-done((bf16[128,4352]{1,0:T(8,128)(2,1)}, bf16[128,4352]{1,0:T(8,128)(2,1)S(1)}, u32[]{:S(2)}, u32[]{:S(2)}) %collective-permute-start.2) | collective-permute-done | bytes 1114144 | tf_op jit(solution)/shard_map/ppermute | solution.py:413
  32.1 0.0 copy-done.4
  32.1 0.0 copy-start.3
  32.1 1.2 copy-done.3
  33.3 2.1 %product.1 = (bf16[128,2048]{1,0:T(8,128)(2,1)S(1)}, bf16[128,2048]{1,0:T(8,128)(2,1)S(1)}, bf16[256,2048]{1,0:T(8,128)(2,1)S(1)}) custom-call(bf16[128,4096]{1,0:T(8,128)(2,1)S(1)} %copy-done.3, bf16[128,4352]{1,0:T(8,128)(2,1)S(1)} %collective-permute-done.2.got_ref.gq_ref, bf16[128,256]{1,0:T(8,128)(2,1)S(1)} %copy-done.4, ...), custom_call_target="tpu_custom_call" | custom-call | flops 536870912 | bytes 4194304 | tf_op jit(solution)/shard_map/product/pallas_call | solution.py:30
  35.4 1.9 %collective-permute-start.3 = (bf16[128,2048]{1,0:T(8,128)(2,1)S(1)}, bf16[128,2048]{1,0:T(8,128)(2,1)S(1)}, u32[]{:S(2)}, u32[]{:S(2)}) collective-permute-start(bf16[128,2048]{1,0:T(8,128)(2,1)S(1)} %get-tuple-element.26), channel_id=1, source_target_pairs={{0,128},{128,0},{256,384},{384,256},{512,640},{640,512},{768,896},... | collective-permute-start | bytes 1572872 | tf_op jit(solution)/shard_map/ppermute | solution.py:413
  37.3 1.9 %collective-permute-start.4 = (bf16[128,2048]{1,0:T(8,128)(2,1)S(1)}, bf16[128,2048]{1,0:T(8,128)(2,1)S(1)}, u32[]{:S(2)}, u32[]{:S(2)}) collective-permute-start(bf16[128,2048]{1,0:T(8,128)(2,1)S(1)} %get-tuple-element.27), channel_id=1, source_target_pairs={{0,896},{128,256},{256,128},{384,512},{512,384},{640,768},{768,640... | collective-permute-start | bytes 1572872 | tf_op jit(solution)/shard_map/ppermute | solution.py:413
  39.2 11.1 %collective-permute-done.3.left_ref = bf16[128,2048]{1,0:T(8,128)(2,1)S(1)} collective-permute-done((bf16[128,2048]{1,0:T(8,128)(2,1)S(1)}, bf16[128,2048]{1,0:T(8,128)(2,1)S(1)}, u32[]{:S(2)}, u32[]{:S(2)}) %collective-permute-start.3) | collective-permute-done | bytes 524320 | tf_op jit(solution)/shard_map/ppermute | solution.py:413
  50.4 3.1 %collective-permute-done.4.right_ref = bf16[128,2048]{1,0:T(8,128)(2,1)S(1)} collective-permute-done((bf16[128,2048]{1,0:T(8,128)(2,1)S(1)}, bf16[128,2048]{1,0:T(8,128)(2,1)S(1)}, u32[]{:S(2)}, u32[]{:S(2)}) %collective-permute-start.4) | collective-permute-done | bytes 524320 | tf_op jit(solution)/shard_map/ppermute | solution.py:413
  53.5 1.8 %sum_y.1 = bf16[4,256,512]{2,1,0:T(8,128)(2,1)} custom-call(bf16[256,2048]{1,0:T(8,128)(2,1)S(1)} %get-tuple-element.25.keep_ref, bf16[128,2048]{1,0:T(8,128)(2,1)S(1)} %collective-permute-done.3.left_ref, bf16[128,2048]{1,0:T(8,128)(2,1)S(1)} %collective-permute-done.4.right_ref), custom_call_target="tpu_custom_call" | custom-call | flops 1048576 | bytes 3145728 | tf_op jit(solution)/shard_map/sum_y/pallas_call | solution.py:30
  55.3 0.0 all-to-all-done.in_ref
  55.3 0.0 copy-start.1
  55.3 1.4 %copy-done.1 = bf16[8,520,256]{2,1,0:T(8,128)(2,1)} copy-done((bf16[8,520,256]{2,1,0:T(8,128)(2,1)}, bf16[8,520,256]{2,1,0:T(8,128)(2,1)S(1)}, u32[]{:S(2)}) %copy-start.1) | copy-done | bytes 2129944
  56.7 3.5 %all-to-all-start.1 = ((bf16[4,256,512]{2,1,0:T(8,128)(2,1)}), bf16[4,256,512]{2,1,0:T(8,128)(2,1)S(1)}, u32[]{:S(2)}, u32[]{:S(2)}) async-start(bf16[4,256,512]{2,1,0:T(8,128)(2,1)} %sum_y.1), calls=%async_computation.1 | async-start | bytes 2097152 | tf_op jit(solution)/shard_map/all_to_all | solution.py:417
  60.2 0.0 copy-start.2
  60.2 1.6 %copy-done.2 = bf16[8,520,256]{2,1,0:T(8,128)(2,1)S(1)} copy-done((bf16[8,520,256]{2,1,0:T(8,128)(2,1)S(1)}, bf16[8,520,256]{2,1,0:T(8,128)(2,1)}, u32[]{:S(2)}) %copy-start.2) | copy-done | bytes 2129944
  61.8 0.0 copy-start
  61.8 0.0 copy-start.8
  61.8 0.3 sum_xz.1
  62.1 0.0 copy-start.5
  62.1 2.1 %collective-permute-start = (bf16[264,256]{1,0:T(8,128)(2,1)S(1)}, bf16[264,256]{1,0:T(8,128)(2,1)S(1)}, u32[]{:S(2)}, u32[]{:S(2)}) collective-permute-start(bf16[264,256]{1,0:T(8,128)(2,1)S(1)} %get-tuple-element.18), channel_id=1, source_target_pairs={{0,8},{4,12},{8,0},{12,4},{16,24},{20,28},{24,16},{28,20},{1,9},{5... | collective-permute-start | bytes 405512 | tf_op jit(solution)/shard_map/ppermute | solution.py:413
  64.1 5.0 %collective-permute-done.got_ref = bf16[264,256]{1,0:T(8,128)(2,1)S(1)} collective-permute-done((bf16[264,256]{1,0:T(8,128)(2,1)S(1)}, bf16[264,256]{1,0:T(8,128)(2,1)S(1)}, u32[]{:S(2)}, u32[]{:S(2)}) %collective-permute-start) | collective-permute-done | bytes 135200 | tf_op jit(solution)/shard_map/ppermute | solution.py:413
  69.2 0.6 sum_z4.1
  69.8 0.0 copy-start.9
  69.8 0.7 copy-done.9
  70.5 0.0 copy-start.12
  70.5 5.6 %collective-permute-start.1 = (bf16[136,256]{1,0:T(8,128)(2,1)}, bf16[136,256]{1,0:T(8,128)(2,1)S(1)}, u32[]{:S(2)}, u32[]{:S(2)}) collective-permute-start(bf16[136,256]{1,0:T(8,128)(2,1)} %get-tuple-element.20), channel_id=1, source_target_pairs={{0,16},{4,20},{8,24},{12,28},{16,0},{20,4},{24,8},{28,12},{1,17},{... | collective-permute-start | bytes 208904 | tf_op jit(solution)/shard_map/ppermute | solution.py:413
  76.1 10.0 %all-to-all-done.1.in_ref = bf16[4,256,512]{2,1,0:T(8,128)(2,1)S(1)} async-done(((bf16[4,256,512]{2,1,0:T(8,128)(2,1)}), bf16[4,256,512]{2,1,0:T(8,128)(2,1)S(1)}, u32[]{:S(2)}, u32[]{:S(2)}) %all-to-all-start.1) | async-done | bytes 1048608 | tf_op jit(solution)/shard_map/all_to_all | solution.py:417
  86.0 0.7 sum_y4.1
  86.7 0.0 copy-start.6
  86.7 0.7 copy-done.6
  87.4 0.0 copy-start.7
  87.4 11.5 %collective-permute-start.5 = (bf16[256,256]{1,0:T(8,128)(2,1)}, bf16[256,256]{1,0:T(8,128)(2,1)S(1)}, u32[]{:S(2)}, u32[]{:S(2)}) collective-permute-start(bf16[256,256]{1,0:T(8,128)(2,1)} %get-tuple-element.29), channel_id=1, source_target_pairs={{0,64},{64,0},{1,65},{65,1},{2,66},{66,2},{3,67},{67,3},{4,68},{68... | collective-permute-start | bytes 393224 | tf_op jit(solution)/shard_map/ppermute | solution.py:413
  98.9 0.0 collective-permute-done.1.got_ref
  99.0 0.0 copy-done
  99.0 0.0 copy-done.8
  99.0 0.0 copy-start.10
  99.0 0.9 copy-done.10
  99.9 0.0 copy-start.11
  99.9 0.8 copy-done.11
  100.7 0.8 finish.1
  101.5 8.9 %all-to-all-start.2 = ((f32[32,1,256]{2,1,0:T(1,128)}), f32[32,1,256]{2,1,0:T(1,128)S(1)}, u32[]{:S(2)}, u32[]{:S(2)}) async-start(f32[32,1,256]{2,1,0:T(1,128)} %get-tuple-element.30), calls=%async_computation.2 | async-start | bytes 65536 | tf_op jit(solution)/shard_map/all_to_all | solution.py:417
  110.4 0.0 collective-permute-done.5.got_ref
  110.5 0.0 copy-done.5
  110.5 0.0 copy-done.7
  110.5 0.8 last.1
  111.3 16.0 %all-to-all-done.2 = f32[32,1,256]{2,1,0:T(1,128)S(1)} async-done(((f32[32,1,256]{2,1,0:T(1,128)}), f32[32,1,256]{2,1,0:T(1,128)S(1)}, u32[]{:S(2)}, u32[]{:S(2)}) %all-to-all-start.2) | async-done | bytes 32800 | tf_op jit(solution)/shard_map/all_to_all | solution.py:417
  127.3 0.1 reduce_sum.9
  127.3 0.0 copy-done.12
  127.3 0.6 multiply_add_fusion
Async XLA Ops:
  6.6 48.7 %all-to-all-start = ((bf16[8,520,256]{2,1,0:T(8,128)(2,1)}), bf16[8,520,256]{2,1,0:T(8,128)(2,1)S(1)}, u32[]{:S(2)}, u32[]{:S(2)}) async-start(bf16[8,520,256]{2,1,0:T(8,128)(2,1)} %partial.1), calls=%async_computation | async-start | bytes 4259840 | tf_op jit(solution)/shard_map/all_to_all | solution.py:417
  13.3 18.8 %copy-start.4 = (bf16[128,256]{1,0:T(8,128)(2,1)S(1)}, bf16[128,256]{1,0:T(8,128)(2,1)}, u32[]{:S(2)}) copy-start(bf16[128,256]{1,0:T(8,128)(2,1)} %q_ref.5) | copy-start | bytes 196612
  16.5 15.6 %collective-permute-start.2 = (bf16[128,4352]{1,0:T(8,128)(2,1)}, bf16[128,4352]{1,0:T(8,128)(2,1)S(1)}, u32[]{:S(2)}, u32[]{:S(2)}) collective-permute-start(bf16[128,4352]{1,0:T(8,128)(2,1)} %get-tuple-element.24), channel_id=1, source_target_pairs={{0,32},{32,0},{1,33},{33,1},{2,34},{34,2},{3,35},{35,3},{4,36},{36... | collective-permute-start | bytes 3342344 | tf_op jit(solution)/shard_map/ppermute | solution.py:413
  32.1 1.2 copy-start.3
  35.4 15.0 %collective-permute-start.3 = (bf16[128,2048]{1,0:T(8,128)(2,1)S(1)}, bf16[128,2048]{1,0:T(8,128)(2,1)S(1)}, u32[]{:S(2)}, u32[]{:S(2)}) collective-permute-start(bf16[128,2048]{1,0:T(8,128)(2,1)S(1)} %get-tuple-element.26), channel_id=1, source_target_pairs={{0,128},{128,0},{256,384},{384,256},{512,640},{640,512},{768,896},... | collective-permute-start | bytes 1572872 | tf_op jit(solution)/shard_map/ppermute | solution.py:413
  37.3 16.2 %collective-permute-start.4 = (bf16[128,2048]{1,0:T(8,128)(2,1)S(1)}, bf16[128,2048]{1,0:T(8,128)(2,1)S(1)}, u32[]{:S(2)}, u32[]{:S(2)}) collective-permute-start(bf16[128,2048]{1,0:T(8,128)(2,1)S(1)} %get-tuple-element.27), channel_id=1, source_target_pairs={{0,896},{128,256},{256,128},{384,512},{512,384},{640,768},{768,640... | collective-permute-start | bytes 1572872 | tf_op jit(solution)/shard_map/ppermute | solution.py:413
  55.3 1.4 %copy-start.1 = (bf16[8,520,256]{2,1,0:T(8,128)(2,1)}, bf16[8,520,256]{2,1,0:T(8,128)(2,1)S(1)}, u32[]{:S(2)}) copy-start(bf16[8,520,256]{2,1,0:T(8,128)(2,1)S(1)} %all-to-all-done.in_ref) | copy-start | bytes 6389764
  56.7 29.4 %all-to-all-start.1 = ((bf16[4,256,512]{2,1,0:T(8,128)(2,1)}), bf16[4,256,512]{2,1,0:T(8,128)(2,1)S(1)}, u32[]{:S(2)}, u32[]{:S(2)}) async-start(bf16[4,256,512]{2,1,0:T(8,128)(2,1)} %sum_y.1), calls=%async_computation.1 | async-start | bytes 2097152 | tf_op jit(solution)/shard_map/all_to_all | solution.py:417
  60.2 1.6 %copy-start.2 = (bf16[8,520,256]{2,1,0:T(8,128)(2,1)S(1)}, bf16[8,520,256]{2,1,0:T(8,128)(2,1)}, u32[]{:S(2)}) copy-start(bf16[8,520,256]{2,1,0:T(8,128)(2,1)} %copy-done.1) | copy-start | bytes 6389764
  61.8 37.2 %copy-start = (bf16[128,8192]{1,0:T(8,128)(2,1)S(1)}, bf16[128,8192]{1,0:T(8,128)(2,1)}, u32[]{:S(2)}) copy-start(bf16[128,8192]{1,0:T(8,128)(2,1)} %h_ref.3) | copy-start | bytes 6291460
  61.8 37.2 %copy-start.8 = (bf16[8192]{0:T(1024)(128)(2,1)S(1)}, bf16[8192]{0:T(1024)(128)(2,1)}, u32[]{:S(2)}) copy-start(bf16[8192]{0:T(1024)(128)(2,1)} %param.7) | copy-start | bytes 49156
  62.1 48.4 %copy-start.5 = (f32[256,256]{1,0:T(8,128)S(1)}, f32[256,256]{1,0:T(8,128)}, u32[]{:S(2)}) copy-start(f32[256,256]{1,0:T(8,128)} %main_ref.1) | copy-start | bytes 786436
  62.1 7.1 %collective-permute-start = (bf16[264,256]{1,0:T(8,128)(2,1)S(1)}, bf16[264,256]{1,0:T(8,128)(2,1)S(1)}, u32[]{:S(2)}, u32[]{:S(2)}) collective-permute-start(bf16[264,256]{1,0:T(8,128)(2,1)S(1)} %get-tuple-element.18), channel_id=1, source_target_pairs={{0,8},{4,12},{8,0},{12,4},{16,24},{20,28},{24,16},{28,20},{1,9},{5... | collective-permute-start | bytes 405512 | tf_op jit(solution)/shard_map/ppermute | solution.py:413
  69.8 0.7 copy-start.9
  70.5 56.9 %copy-start.12 = (f32[256]{0:T(256)S(1)}, f32[256]{0:T(256)}, u32[]{:S(2)}) copy-start(f32[256]{0:T(256)} %param.11) | copy-start | bytes 3076
  70.5 28.5 %collective-permute-start.1 = (bf16[136,256]{1,0:T(8,128)(2,1)}, bf16[136,256]{1,0:T(8,128)(2,1)S(1)}, u32[]{:S(2)}, u32[]{:S(2)}) collective-permute-start(bf16[136,256]{1,0:T(8,128)(2,1)} %get-tuple-element.20), channel_id=1, source_target_pairs={{0,16},{4,20},{8,24},{12,28},{16,0},{20,4},{24,8},{28,12},{1,17},{... | collective-permute-start | bytes 208904 | tf_op jit(solution)/shard_map/ppermute | solution.py:413
  86.7 0.7 copy-start.6
  87.4 23.0 %copy-start.7 = (f32[256,256]{1,0:T(8,128)S(1)}, f32[256,256]{1,0:T(8,128)}, u32[]{:S(2)}) copy-start(f32[256,256]{1,0:T(8,128)} %copy-done.6) | copy-start | bytes 786436
  87.4 23.0 %collective-permute-start.5 = (bf16[256,256]{1,0:T(8,128)(2,1)}, bf16[256,256]{1,0:T(8,128)(2,1)S(1)}, u32[]{:S(2)}, u32[]{:S(2)}) collective-permute-start(bf16[256,256]{1,0:T(8,128)(2,1)} %get-tuple-element.29), channel_id=1, source_target_pairs={{0,64},{64,0},{1,65},{65,1},{2,66},{66,2},{3,67},{67,3},{4,68},{68... | collective-permute-start | bytes 393224 | tf_op jit(solution)/shard_map/ppermute | solution.py:413
  99.0 0.9 copy-start.10
  99.9 0.8 copy-start.11
  101.5 25.8 %all-to-all-start.2 = ((f32[32,1,256]{2,1,0:T(1,128)}), f32[32,1,256]{2,1,0:T(1,128)S(1)}, u32[]{:S(2)}, u32[]{:S(2)}) async-start(f32[32,1,256]{2,1,0:T(1,128)} %get-tuple-element.30), calls=%async_computation.2 | async-start | bytes 65536 | tf_op jit(solution)/shard_map/all_to_all | solution.py:417

commit v3 on v2

--- a/solution.py
+++ b/solution.py
@@ -45,49 +45,6 @@
     return jnp.concatenate([at(0), at(1)], axis=1)
 
 
-ROWS = 64
-
-
-def norm_kernel(h_ref, g_ref, q_ref, send_ref, own_ref, rinv_ref, g32):
-    par, core = lax.rem(lax.axis_index("y"), 2), lax.axis_index("c")
-    g32[...] = g_ref[...].astype(F32)
-    acc = jnp.zeros((ROWS, 128), F32)
-    for j in range(D // 128):
-        h = h_ref[:, j * 128 : (j + 1) * 128].astype(F32)
-        acc = acc + h * h
-    rinv = lax.rsqrt(jnp.sum(acc, axis=1, keepdims=True) / D + 1e-05)
-    rinv_ref[...] = rinv
-    for out, which in ((send_ref, 1 - core), (own_ref, core)):
-        for j in range(16):
-            o, k, zh = j // 8, (j // 2) % 4, j % 2
-            y = 2 * k + (1 - par if o == 0 else par)
-            block = y * 4 + zh * 2 + which
-            h = h_ref[:, aligned(block * B, B)].astype(F32)
-            out[:, j * B : (j + 1) * B] = (h * rinv * two_rows(g32, block)).astype(BF)
-    send_ref[:, 16 * B :] = q_ref[...]
-
-
-def norm(hidden, gain, q_grad):
-    row = lambda n: pl.BlockSpec((ROWS, n), lambda i: (i, 0))
-    return call(
-        norm_kernel,
-        (
-            jax.ShapeDtypeStruct((TOK, 17 * B), BF),
-            jax.ShapeDtypeStruct((TOK, 16 * B), BF),
-            jax.ShapeDtypeStruct((TOK, 1), F32),
-        ),
-        (hidden, gain, q_grad),
-        None,
-        6 * TOK * D,
-        4 * TOK * D,
-        grid=(TOK // ROWS,),
-        in_specs=[row(D), pl.BlockSpec((64, 128), lambda i: (0, 0)), row(B)],
-        out_specs=(row(17 * B), row(16 * B), row(1)),
-        scratch_shapes=[pltpu.VMEM((64, 128), F32)],
-        name="norm",
-    )
-
-
 def eye():
     a = lax.broadcasted_iota(jnp.int32, (128, 128), 0)
     b = lax.broadcasted_iota(jnp.int32, (128, 128), 1)
@@ -109,55 +66,91 @@
 ZQ = NZ // 2
 NG = 2 * NX
 PIECE = ZQ * TOK + 8
-
-
-def partial_kernel(q_ref, g_ref, w_hbm, h_hbm, out_hbm, w_ref, h_ref, out_ref, w_sem, h_sem, out_sem):
+ROWS = 64
+HBM = pl.BlockSpec(memory_space=pltpu.HBM)
+
+
+def front_kernel(
+    q_ref, g_ref, w_hbm, h_hbm, part_hbm, send_hbm, own_hbm, rinv_ref,
+    w_ref, h_ref, part_ref, send_ref, own_ref, g32, w_sem, h_sem, out_sem, normed_sem,
+):
     wide = NX * B
+    par, core = lax.rem(lax.axis_index("y"), 2), lax.axis_index("c")
 
     def w_copy(z):
         at = slice(z * wide, (z + 1) * wide)
         return pltpu.make_async_copy(w_hbm.at[at, :], w_ref.at[at, :], w_sem.at[z])
 
-    def h_copy(z):
-        at = slice(z * wide, (z + 1) * wide)
-        return pltpu.make_async_copy(h_hbm.at[:, at], h_ref.at[:, at], h_sem.at[z])
+    def h_copy(r):
+        at = slice(r * ROWS, (r + 1) * ROWS)
+        return pltpu.make_async_copy(h_hbm.at[at, :], h_ref.at[at, :], h_sem.at[r])
 
     def out_copy(z, x):
         at = (z % 2 * NX + x, slice(z // 2 * TOK, (z // 2 + 1) * TOK))
-        return pltpu.make_async_copy(out_ref.at[at], out_hbm.at[at], out_sem.at[z * NX + x])
+        return pltpu.make_async_copy(part_ref.at[at], part_hbm.at[at], out_sem.at[z * NX + x])
 
     def stat_copy(d):
         at = (d, slice(ZQ * TOK, PIECE))
-        return pltpu.make_async_copy(out_ref.at[at], out_hbm.at[at], out_sem.at[NZ * NX + d])
-
-    for z in range(NZ):
-        w_copy(z).start()
-        h_copy(z).start()
+        return pltpu.make_async_copy(part_ref.at[at], part_hbm.at[at], out_sem.at[NZ * NX + d])
+
+    send_copy = pltpu.make_async_copy(send_ref, send_hbm, normed_sem.at[0])
+    own_copy = pltpu.make_async_copy(own_ref, own_hbm, normed_sem.at[1])
+
+    for r in range(TOK // ROWS):
+        h_copy(r).start()
+    g32[...] = g_ref[...].astype(F32)
+    send_ref[:, 16 * B :] = q_ref[...]
+    for r in range(TOK // ROWS):
+        h_copy(r).wait()
+        if r == 0:
+            for z in range(NZ // 2):
+                w_copy(z).start()
+        at = slice(r * ROWS, (r + 1) * ROWS)
+        acc = jnp.zeros((ROWS, 128), F32)
+        for j in range(D // 128):
+            h = h_ref[at, j * 128 : (j + 1) * 128].astype(F32)
+            acc = acc + h * h
+        rinv = lax.rsqrt(jnp.sum(acc, axis=1, keepdims=True) / D + 1e-05)
+        rinv_ref[at, :] = rinv
+        for out, which in ((send_ref, 1 - core), (own_ref, core)):
+            for j in range(16):
+                o, k, zh = j // 8, (j // 2) % 4, j % 2
+                y = 2 * k + (1 - par if o == 0 else par)
+                block = y * 4 + zh * 2 + which
+                h = h_ref[at, aligned(block * B, B)].astype(F32)
+                out[at, j * B : (j + 1) * B] = (h * rinv * two_rows(g32, block)).astype(BF)
+
     q = q_ref[...]
-    g = g_ref[...].astype(F32)
+    g = g32[...]
     acc = jnp.zeros((TOK, 128), F32)
     for z in range(NZ):
+        if z < NZ // 2:
+            w_copy(z + NZ // 2).start()
         w_copy(z).wait()
-        h_copy(z).wait()
         for x in range(NX):
             b = z * NX + x
             at = slice(b * B, (b + 1) * B)
             p = lax.dot_general(q, w_ref[at, :], (((1,), (1,)), ((), ())), preferred_element_type=F32)
             p = p.astype(BF)
-            out_ref[z % 2 * NX + x, z // 2 * TOK : (z // 2 + 1) * TOK, :] = p
+            part_ref[z % 2 * NX + x, z // 2 * TOK : (z // 2 + 1) * TOK, :] = p
             t = p.astype(F32) * h_ref[:, at].astype(F32)
             acc = acc + t[:, :128] * g[2 * b : 2 * b + 1, :] + t[:, 128:] * g[2 * b + 1 : 2 * b + 2, :]
-        if z > 0:
+        if z == 0:
+            send_copy.start()
+            own_copy.start()
+        else:
             for x in range(NX):
                 out_copy(z - 1, x).start()
     s = jnp.sum(acc, axis=1, keepdims=True)
     rows = stat_rows(jnp.sum(jnp.where(eye(), s, 0.0), axis=0, keepdims=True))
     for d in range(NG):
-        out_ref[d, ZQ * TOK :, :] = rows
+        part_ref[d, ZQ * TOK :, :] = rows
     for x in range(NX):
         out_copy(NZ - 1, x).start()
     for d in range(NG):
         stat_copy(d).start()
+    send_copy.wait()
+    own_copy.wait()
     for z in range(NZ):
         for x in range(NX):
             out_copy(z, x).wait()
@@ -165,28 +158,34 @@
         stat_copy(d).wait()
 
 
-HBM = pl.BlockSpec(memory_space=pltpu.HBM)
-
-
-def partial(q_grad, weight, hidden, gain):
-    return call(
-        partial_kernel,
-        jax.ShapeDtypeStruct((NG, PIECE, B), BF),
+def front(q_grad, gain, weight, hidden):
+    return call(
+        front_kernel,
+        (
+            jax.ShapeDtypeStruct((NG, PIECE, B), BF),
+            jax.ShapeDtypeStruct((TOK, 17 * B), BF),
+            jax.ShapeDtypeStruct((TOK, 16 * B), BF),
+            jax.ShapeDtypeStruct((TOK, 1), F32),
+        ),
         (q_grad, gain, weight, hidden),
         None,
         2 * TOK * D * B,
-        8 * MB,
+        12 * MB,
         in_specs=[VM, VM, HBM, HBM],
-        out_specs=HBM,
+        out_specs=(HBM, HBM, HBM, VM),
         scratch_shapes=[
             pltpu.VMEM((D, B), BF),
             pltpu.VMEM((TOK, D), BF),
             pltpu.VMEM((NG, PIECE, B), BF),
+            pltpu.VMEM((TOK, 17 * B), BF),
+            pltpu.VMEM((TOK, 16 * B), BF),
+            pltpu.VMEM((64, 128), F32),
             pltpu.SemaphoreType.DMA((NZ,)),
-            pltpu.SemaphoreType.DMA((NZ,)),
+            pltpu.SemaphoreType.DMA((TOK // ROWS,)),
             pltpu.SemaphoreType.DMA((NZ * NX + NG,)),
+            pltpu.SemaphoreType.DMA((2,)),
         ],
-        name="partial",
+        name="front",
     )
 
 
@@ -264,9 +263,7 @@
     rinv = rinv_ref[...]
     stat = jnp.sum(jnp.where(eye(), stat, 0.0), axis=1, keepdims=True) * rinv / D
     xhat = h_ref[:, aligned(own * B, B)].astype(F32) * rinv
-    total = jnp.sum(grad * xhat, axis=0, keepdims=True)
-    for i in range(NY * NH * NC):
-        gain_ref[i] = total
+    gain_ref[...] = jnp.sum(grad * xhat, axis=0, keepdims=True)
     out_ref[...] = (rinv * (grad * two_rows(g32, own) - xhat * stat)).astype(BF)
 
 
@@ -275,7 +272,7 @@
         finish_kernel,
         (
             jax.ShapeDtypeStruct((TOK, B), BF),
-            jax.ShapeDtypeStruct((NY * NH * NC, 1, B), F32),
+            jax.ShapeDtypeStruct((1, B), F32),
         ),
         (keep, got, hidden, gain, rinv),
         10,
@@ -335,8 +332,10 @@
 
 
 def sum_y_kernel(keep_ref, left_ref, right_ref, out_ref):
-    out_ref[0, :128, :] = (keep_ref[:128, :].astype(F32) + left_ref[...].astype(F32)).astype(BF)
-    out_ref[0, 128:, :] = (keep_ref[128:, :].astype(F32) + right_ref[...].astype(F32)).astype(BF)
+    for k in range(4):
+        at = slice(k * 512, (k + 1) * 512)
+        out_ref[k, :128, :] = (keep_ref[:128, at].astype(F32) + left_ref[:, at].astype(F32)).astype(BF)
+        out_ref[k, 128:, :] = (keep_ref[128:, at].astype(F32) + right_ref[:, at].astype(F32)).astype(BF)
 
 
 def sum_y(keep, left, right):
@@ -347,13 +346,8 @@
         8,
         TOK * D,
         3 * MB,
-        grid=(4,),
-        in_specs=[
-            pl.BlockSpec((B, 512), lambda k: (0, k)),
-            pl.BlockSpec((128, 512), lambda k: (0, k)),
-            pl.BlockSpec((128, 512), lambda k: (0, k)),
-        ],
-        out_specs=pl.BlockSpec((1, B, 512), lambda k: (k, 0, 0)),
+        in_specs=[VM] * 3,
+        out_specs=VM,
         name="sum_y",
     )
 
@@ -419,12 +413,11 @@
 
 def body(hidden, gain, weight, q_grad, q_main, gain_main):
     gain2 = gain.reshape(64, 128)
-    part = partial(q_grad, weight, hidden, gain2)
+    part, send, own, rinv = front(q_grad, gain2, weight, hidden)
+    got = swap(send, "c", NC, lambda i: i ^ 1)
     groups = [list(range(i * NG, (i + 1) * NG)) for i in range(NZ * NX // NG)]
     part = exchange(part, ("zl", "x"), axis_index_groups=groups)
 
-    send, own, rinv = norm(hidden, gain2, q_grad)
-    got = swap(send, "c", NC, lambda i: i ^ 1)
     left, right, keep = product(own, got, q_grad)
     left = swap(left, "y", NY, lambda i: i ^ 1)
     right = swap(right, "y", NY, lambda i: i + 1 if i % 2 else i - 1)
@@ -437,11 +430,13 @@
 
     send3, keep3 = sum_z(keep2, got2, 2, 4)
     got3 = swap(send3, "zl", NZ, lambda i: i ^ 4)
-    grad, all_gain = finish(keep3, got3, hidden, gain2, rinv)
-    all_gain = exchange(all_gain, ("y", "zh", "c"))
+    grad, own_gain = finish(keep3, got3, hidden, gain2, rinv)
+    got_gain = swap(own_gain, "zh", NH, lambda i: i ^ 1)
 
     send_h, keep_h = sum_y4(four)
     got_h = swap(send_h, "zh", NH, lambda i: i ^ 1)
+    all_gain = jnp.broadcast_to((own_gain + got_gain)[None], (NY * NC, 1, B))
+    all_gain = exchange(all_gain, ("y", "c"))
     q_new = last(q_main, keep_h, got_h)
     gain_new = gain_main + jnp.sum(all_gain, axis=(0, 1)) / (NY * NH * NC)
     return grad, q_new, gain_new

time: 129 us -> 145 us (1.12)
  waiting for transfers between devices: 47.8 us -> 68 us
  local copies, waits for them, and re-layouts: 7.31 us -> 2.24 us
  starting transfers between devices: 55 us -> 58.7 us
  Pallas kernels: 16.4 us -> 13.9 us
    ppermute x6 -> x7, waiting for transfers between devices: 21.9 us -> 38.6 us  [swap(): return lax.ppermute(v, axis, pairs(n, f))]
    ppermute x6 -> x7, starting transfers between devices: 35.9 us -> 42.1 us  [swap(): return lax.ppermute(v, axis, pairs(n, f))]
    unnamed x26 -> x14, local copies, waits for them, and re-layouts: 7.31 us -> 1.63 us
    all_to_all x3, waiting for transfers between devices: 25.9 us -> 29.4 us  [exchange(): return lax.all_to_all(v, axis, 0, 0, tiled=True, **kw)]
    all_to_all x3, starting transfers between devices: 19.1 us -> 16.6 us  [exchange(): return lax.all_to_all(v, axis, 0, 0, tiled=True, **kw)]
    pallas_call x9 -> x8, Pallas kernels: 16.4 us -> 13.9 us  [call(): pl.pallas_call(kernel, out_shape=out_shape, compiler_params=params(mib),...]
  transfers between devices with their start and end apart: 9 -> 10, of which waited for: 6 -> 7; matrix products, arithmetic and copies ran while one was open for 0% -> 0% of each run, Pallas kernels for 8% -> 4%
where the time goes in v3:
time: 145 us; the launch traced here: 144 us
  waiting for transfers between devices  68 us (47%)
  starting transfers between devices  58.7 us (40%)
  Pallas kernels  13.9 us (10%)
  local copies, waits for them, and re-layouts  2.24 us (2%)
    ppermute x7, starting transfers between devices, swap(): return lax.ppermute(v, axis, pairs(n, f))  42.1 us
    ppermute x7, waiting for transfers between devices, swap(): return lax.ppermute(v, axis, pairs(n, f))  38.6 us
    all_to_all x3, waiting for transfers between devices, exchange(): return lax.all_to_all(v, axis, 0, 0, tiled=True, **kw)  29.4 us
    all_to_all x3, starting transfers between devices, exchange(): return lax.all_to_all(v, axis, 0, 0, tiled=True, **kw)  16.6 us
    pallas_call x8, Pallas kernels, call(): pl.pallas_call(kernel, out_shape=out_shape, compiler_params=params(mib),...  13.9 us
  transfers between devices with their start and end apart: 10, of which 7 were waited for; matrix products, arithmetic and copies ran while one was open for 0% of the time, Pallas kernels for 4%

profile of v3, /device:TPU:1, one launch (start us, length us, event | category | flops | bytes accessed | tf_op | source)
XLA Modules:
  0.0 144.2 jit_solution(18328175157603202591)
XLA Ops:
  0.6 7.9 %front.1 = (bf16[8,520,256]{2,1,0:T(8,128)(2,1)}, bf16[128,4352]{1,0:T(8,128)(2,1)}, bf16[128,4096]{1,0:T(8,128)(2,1)}, f32[128,1]{1,0:T(8,128)}) custom-call(bf16[128,256]{1,0:T(8,128)(2,1)} %q_ref.3, bf16[64,128]{1,0:T(8,128)(2,1)} %bitcast.2, bf16[8192,256]{1,0:T(8,128)(2,1)} %w_hbm.1, bf16[128,8192]{1,0:T(8,128)(2,1)} %h_ref.1), custom_call_target="tpu_custom_call" | custom-call | flops 536870912 | bytes 12582912 | tf_op jit(solution)/shard_map/front/pallas_call | solution.py:30
  8.6 0.0 copy-start.1
  8.6 0.0 copy-start.2
  8.6 6.8 %all-to-all-start = ((bf16[8,520,256]{2,1,0:T(8,128)(2,1)}), bf16[8,520,256]{2,1,0:T(8,128)(2,1)S(1)}, u32[]{:S(2)}, u32[]{:S(2)}) async-start(bf16[8,520,256]{2,1,0:T(8,128)(2,1)} %get-tuple-element.18), calls=%async_computation | async-start | bytes 4259840 | tf_op jit(solution)/shard_map/all_to_all | solution.py:411
  15.4 13.0 %collective-permute-start.2 = (bf16[128,4352]{1,0:T(8,128)(2,1)}, bf16[128,4352]{1,0:T(8,128)(2,1)S(1)}, u32[]{:S(2)}, u32[]{:S(2)}) collective-permute-start(bf16[128,4352]{1,0:T(8,128)(2,1)} %get-tuple-element.26), channel_id=1, source_target_pairs={{0,32},{32,0},{1,33},{33,1},{2,34},{34,2},{3,35},{35,3},{4,36},{36... | collective-permute-start | bytes 3342344 | tf_op jit(solution)/shard_map/ppermute | solution.py:407
  28.4 2.6 %collective-permute-done.2.got_ref.gq_ref = bf16[128,4352]{1,0:T(8,128)(2,1)S(1)} collective-permute-done((bf16[128,4352]{1,0:T(8,128)(2,1)}, bf16[128,4352]{1,0:T(8,128)(2,1)S(1)}, u32[]{:S(2)}, u32[]{:S(2)}) %collective-permute-start.2) | collective-permute-done | bytes 1114144 | tf_op jit(solution)/shard_map/ppermute | solution.py:407
  31.0 0.0 copy-done.1
  31.0 0.0 copy-done.2
  31.0 2.1 %product.1 = (bf16[128,2048]{1,0:T(8,128)(2,1)S(1)}, bf16[128,2048]{1,0:T(8,128)(2,1)S(1)}, bf16[256,2048]{1,0:T(8,128)(2,1)S(1)}) custom-call(bf16[128,4096]{1,0:T(8,128)(2,1)S(1)} %copy-done.1, bf16[128,4352]{1,0:T(8,128)(2,1)S(1)} %collective-permute-done.2.got_ref.gq_ref, bf16[128,256]{1,0:T(8,128)(2,1)S(1)} %copy-done.2, ...), custom_call_target="tpu_custom_call" | custom-call | flops 536870912 | bytes 4194304 | tf_op jit(solution)/shard_map/product/pallas_call | solution.py:30
  33.0 1.9 %collective-permute-start.3 = (bf16[128,2048]{1,0:T(8,128)(2,1)S(1)}, bf16[128,2048]{1,0:T(8,128)(2,1)S(1)}, u32[]{:S(2)}, u32[]{:S(2)}) collective-permute-start(bf16[128,2048]{1,0:T(8,128)(2,1)S(1)} %get-tuple-element.28), channel_id=1, source_target_pairs={{0,128},{128,0},{256,384},{384,256},{512,640},{640,512},{768,896},... | collective-permute-start | bytes 1572872 | tf_op jit(solution)/shard_map/ppermute | solution.py:407
  35.0 1.9 %collective-permute-start.4 = (bf16[128,2048]{1,0:T(8,128)(2,1)S(1)}, bf16[128,2048]{1,0:T(8,128)(2,1)S(1)}, u32[]{:S(2)}, u32[]{:S(2)}) collective-permute-start(bf16[128,2048]{1,0:T(8,128)(2,1)S(1)} %get-tuple-element.29), channel_id=1, source_target_pairs={{0,896},{128,256},{256,128},{384,512},{512,384},{640,768},{768,640... | collective-permute-start | bytes 1572872 | tf_op jit(solution)/shard_map/ppermute | solution.py:407
  36.9 11.1 %collective-permute-done.3.left_ref = bf16[128,2048]{1,0:T(8,128)(2,1)S(1)} collective-permute-done((bf16[128,2048]{1,0:T(8,128)(2,1)S(1)}, bf16[128,2048]{1,0:T(8,128)(2,1)S(1)}, u32[]{:S(2)}, u32[]{:S(2)}) %collective-permute-start.3) | collective-permute-done | bytes 524320 | tf_op jit(solution)/shard_map/ppermute | solution.py:407
  48.0 3.1 %collective-permute-done.4.right_ref = bf16[128,2048]{1,0:T(8,128)(2,1)S(1)} collective-permute-done((bf16[128,2048]{1,0:T(8,128)(2,1)S(1)}, bf16[128,2048]{1,0:T(8,128)(2,1)S(1)}, u32[]{:S(2)}, u32[]{:S(2)}) %collective-permute-start.4) | collective-permute-done | bytes 524320 | tf_op jit(solution)/shard_map/ppermute | solution.py:407
  51.2 1.2 sum_y.1
  52.4 0.0 all-to-all-done.in_ref
  52.4 3.5 %all-to-all-start.1 = ((bf16[4,256,512]{2,1,0:T(8,128)(2,1)}), bf16[4,256,512]{2,1,0:T(8,128)(2,1)S(1)}, u32[]{:S(2)}, u32[]{:S(2)}) async-start(bf16[4,256,512]{2,1,0:T(8,128)(2,1)} %sum_y.1), calls=%async_computation.1 | async-start | bytes 2097152 | tf_op jit(solution)/shard_map/all_to_all | solution.py:411
  55.9 0.0 copy-start.4
  56.0 0.0 copy-start.5
  56.0 0.9 sum_xz.1
  56.8 0.0 copy-start.3
  56.8 2.0 %collective-permute-start = (bf16[264,256]{1,0:T(8,128)(2,1)}, bf16[264,256]{1,0:T(8,128)(2,1)S(1)}, u32[]{:S(2)}, u32[]{:S(2)}) collective-permute-start(bf16[264,256]{1,0:T(8,128)(2,1)} %get-tuple-element.20), channel_id=1, source_target_pairs={{0,8},{4,12},{8,0},{12,4},{16,24},{20,28},{24,16},{28,20},{1,9},{5... | collective-permute-start | bytes 405512 | tf_op jit(solution)/shard_map/ppermute | solution.py:407
  58.9 22.9 %all-to-all-done.1.in_ref = bf16[4,256,512]{2,1,0:T(8,128)(2,1)S(1)} async-done(((bf16[4,256,512]{2,1,0:T(8,128)(2,1)}), bf16[4,256,512]{2,1,0:T(8,128)(2,1)S(1)}, u32[]{:S(2)}, u32[]{:S(2)}) %all-to-all-start.1) | async-done | bytes 1048608 | tf_op jit(solution)/shard_map/all_to_all | solution.py:411
  81.8 0.1 sum_y4.1
  81.9 0.0 copy-start.6
  81.9 11.5 %collective-permute-start.5 = (bf16[256,256]{1,0:T(8,128)(2,1)S(1)}, bf16[256,256]{1,0:T(8,128)(2,1)S(1)}, u32[]{:S(2)}, u32[]{:S(2)}) collective-permute-start(bf16[256,256]{1,0:T(8,128)(2,1)S(1)} %get-tuple-element.31), channel_id=1, source_target_pairs={{0,64},{64,0},{1,65},{65,1},{2,66},{66,2},{3,67},{67,3},{4,68},{68... | collective-permute-start | bytes 393224 | tf_op jit(solution)/shard_map/ppermute | solution.py:407
  93.4 0.0 collective-permute-done.got_ref
  93.4 5.8 %collective-permute-start.1 = (bf16[136,256]{1,0:T(8,128)(2,1)S(1)}, bf16[136,256]{1,0:T(8,128)(2,1)S(1)}, u32[]{:S(2)}, u32[]{:S(2)}) collective-permute-start(bf16[136,256]{1,0:T(8,128)(2,1)S(1)} %get-tuple-element.22), channel_id=1, source_target_pairs={{0,16},{4,20},{8,24},{12,28},{16,0},{20,4},{24,8},{28,12},{1,17},{... | collective-permute-start | bytes 208904 | tf_op jit(solution)/shard_map/ppermute | solution.py:407
  99.3 14.7 %collective-permute-done.1.got_ref = bf16[136,256]{1,0:T(8,128)(2,1)S(1)} collective-permute-done((bf16[136,256]{1,0:T(8,128)(2,1)S(1)}, bf16[136,256]{1,0:T(8,128)(2,1)S(1)}, u32[]{:S(2)}, u32[]{:S(2)}) %collective-permute-start.1) | collective-permute-done | bytes 69664 | tf_op jit(solution)/shard_map/ppermute | solution.py:407
  114.0 0.0 copy-done.4
  114.0 0.0 copy-done.5
  114.0 0.0 copy-start
  114.0 1.6 %copy-done = bf16[128,8192]{1,0:T(8,128)(2,1)S(1)} copy-done((bf16[128,8192]{1,0:T(8,128)(2,1)S(1)}, bf16[128,8192]{1,0:T(8,128)(2,1)}, u32[]{:S(2)}) %copy-start) | copy-done | bytes 2097176
  115.6 0.8 finish.1
  116.4 5.9 %collective-permute-start.6 = (f32[1,256]{1,0:T(1,128)S(1)}, f32[1,256]{1,0:T(1,128)S(1)}, u32[]{:S(2)}, u32[]{:S(2)}) collective-permute-start(f32[1,256]{1,0:T(1,128)S(1)} %get-tuple-element.32), channel_id=1, source_target_pairs={{0,64},{64,0},{1,65},{65,1},{2,66},{66,2},{3,67},{67,3},{4,68},{68... | collective-permute-start | bytes 3080 | tf_op jit(solution)/shard_map/ppermute | solution.py:407
  122.3 7.1 %collective-permute-done.6 = f32[1,256]{1,0:T(1,128)S(1)} collective-permute-done((f32[1,256]{1,0:T(1,128)S(1)}, f32[1,256]{1,0:T(1,128)S(1)}, u32[]{:S(2)}, u32[]{:S(2)}) %collective-permute-start.6) | collective-permute-done | bytes 1056 | tf_op jit(solution)/shard_map/ppermute | solution.py:407
  129.4 0.6 broadcast_in_dim.9
  130.0 6.3 %all-to-all-start.2 = ((f32[16,1,256]{2,1,0:T(1,128)}), f32[16,1,256]{2,1,0:T(1,128)S(1)}, u32[]{:S(2)}, u32[]{:S(2)}) async-start(f32[16,1,256]{2,1,0:T(1,128)} %broadcast_in_dim.9), calls=%async_computation.2 | async-start | bytes 32768 | tf_op jit(solution)/shard_map/all_to_all | solution.py:411
  136.3 0.0 collective-permute-done.5.got_ref
  136.3 0.0 copy-done.3
  136.3 0.8 last.1
  137.1 6.5 %all-to-all-done.2 = f32[16,1,256]{2,1,0:T(1,128)S(1)} async-done(((f32[16,1,256]{2,1,0:T(1,128)}), f32[16,1,256]{2,1,0:T(1,128)S(1)}, u32[]{:S(2)}, u32[]{:S(2)}) %all-to-all-start.2) | async-done | bytes 16416 | tf_op jit(solution)/shard_map/all_to_all | solution.py:411
  143.7 0.0 copy-done.6
  143.7 0.6 multiply_add_fusion
  (3 shorter events, 0.1 us)
Async XLA Ops:
  8.6 22.4 %copy-start.1 = (bf16[128,4096]{1,0:T(8,128)(2,1)S(1)}, bf16[128,4096]{1,0:T(8,128)(2,1)}, u32[]{:S(2)}) copy-start(bf16[128,4096]{1,0:T(8,128)(2,1)} %get-tuple-element.25.own_ref) | copy-start | bytes 3145732
  8.6 22.4 %copy-start.2 = (bf16[128,256]{1,0:T(8,128)(2,1)S(1)}, bf16[128,256]{1,0:T(8,128)(2,1)}, u32[]{:S(2)}) copy-start(bf16[128,256]{1,0:T(8,128)(2,1)} %q_ref.3) | copy-start | bytes 196612
  8.6 43.8 %all-to-all-start = ((bf16[8,520,256]{2,1,0:T(8,128)(2,1)}), bf16[8,520,256]{2,1,0:T(8,128)(2,1)S(1)}, u32[]{:S(2)}, u32[]{:S(2)}) async-start(bf16[8,520,256]{2,1,0:T(8,128)(2,1)} %get-tuple-element.18), calls=%async_computation | async-start | bytes 4259840 | tf_op jit(solution)/shard_map/all_to_all | solution.py:411
  15.4 15.6 %collective-permute-start.2 = (bf16[128,4352]{1,0:T(8,128)(2,1)}, bf16[128,4352]{1,0:T(8,128)(2,1)S(1)}, u32[]{:S(2)}, u32[]{:S(2)}) collective-permute-start(bf16[128,4352]{1,0:T(8,128)(2,1)} %get-tuple-element.26), channel_id=1, source_target_pairs={{0,32},{32,0},{1,33},{33,1},{2,34},{34,2},{3,35},{35,3},{4,36},{36... | collective-permute-start | bytes 3342344 | tf_op jit(solution)/shard_map/ppermute | solution.py:407
  33.0 15.0 %collective-permute-start.3 = (bf16[128,2048]{1,0:T(8,128)(2,1)S(1)}, bf16[128,2048]{1,0:T(8,128)(2,1)S(1)}, u32[]{:S(2)}, u32[]{:S(2)}) collective-permute-start(bf16[128,2048]{1,0:T(8,128)(2,1)S(1)} %get-tuple-element.28), channel_id=1, source_target_pairs={{0,128},{128,0},{256,384},{384,256},{512,640},{640,512},{768,896},... | collective-permute-start | bytes 1572872 | tf_op jit(solution)/shard_map/ppermute | solution.py:407
  35.0 16.2 %collective-permute-start.4 = (bf16[128,2048]{1,0:T(8,128)(2,1)S(1)}, bf16[128,2048]{1,0:T(8,128)(2,1)S(1)}, u32[]{:S(2)}, u32[]{:S(2)}) collective-permute-start(bf16[128,2048]{1,0:T(8,128)(2,1)S(1)} %get-tuple-element.29), channel_id=1, source_target_pairs={{0,896},{128,256},{256,128},{384,512},{512,384},{640,768},{768,640... | collective-permute-start | bytes 1572872 | tf_op jit(solution)/shard_map/ppermute | solution.py:407
  52.4 29.4 %all-to-all-start.1 = ((bf16[4,256,512]{2,1,0:T(8,128)(2,1)}), bf16[4,256,512]{2,1,0:T(8,128)(2,1)S(1)}, u32[]{:S(2)}, u32[]{:S(2)}) async-start(bf16[4,256,512]{2,1,0:T(8,128)(2,1)} %sum_y.1), calls=%async_computation.1 | async-start | bytes 2097152 | tf_op jit(solution)/shard_map/all_to_all | solution.py:411
  55.9 58.0 %copy-start.4 = (bf16[8192]{0:T(1024)(128)(2,1)S(1)}, bf16[8192]{0:T(1024)(128)(2,1)}, u32[]{:S(2)}) copy-start(bf16[8192]{0:T(1024)(128)(2,1)} %param.7) | copy-start | bytes 49156
  56.0 58.0 %copy-start.5 = (f32[128,1]{1,0:T(8,128)S(1)}, f32[128,1]{1,0:T(8,128)}, u32[]{:S(2)}) copy-start(f32[128,1]{1,0:T(8,128)} %get-tuple-element.23.rinv_ref) | copy-start | bytes 1540
  56.8 79.5 %copy-start.3 = (f32[256,256]{1,0:T(8,128)S(1)}, f32[256,256]{1,0:T(8,128)}, u32[]{:S(2)}) copy-start(f32[256,256]{1,0:T(8,128)} %main_ref.1) | copy-start | bytes 786436
  56.8 36.6 %collective-permute-start = (bf16[264,256]{1,0:T(8,128)(2,1)}, bf16[264,256]{1,0:T(8,128)(2,1)S(1)}, u32[]{:S(2)}, u32[]{:S(2)}) collective-permute-start(bf16[264,256]{1,0:T(8,128)(2,1)} %get-tuple-element.20), channel_id=1, source_target_pairs={{0,8},{4,12},{8,0},{12,4},{16,24},{20,28},{24,16},{28,20},{1,9},{5... | collective-permute-start | bytes 405512 | tf_op jit(solution)/shard_map/ppermute | solution.py:407
  81.9 61.8 %copy-start.6 = (f32[256]{0:T(256)S(1)}, f32[256]{0:T(256)}, u32[]{:S(2)}) copy-start(f32[256]{0:T(256)} %param.11) | copy-start | bytes 3076
  81.9 54.4 %collective-permute-start.5 = (bf16[256,256]{1,0:T(8,128)(2,1)S(1)}, bf16[256,256]{1,0:T(8,128)(2,1)S(1)}, u32[]{:S(2)}, u32[]{:S(2)}) collective-permute-start(bf16[256,256]{1,0:T(8,128)(2,1)S(1)} %get-tuple-element.31), channel_id=1, source_target_pairs={{0,64},{64,0},{1,65},{65,1},{2,66},{66,2},{3,67},{67,3},{4,68},{68... | collective-permute-start | bytes 393224 | tf_op jit(solution)/shard_map/ppermute | solution.py:407
  93.4 20.5 %collective-permute-start.1 = (bf16[136,256]{1,0:T(8,128)(2,1)S(1)}, bf16[136,256]{1,0:T(8,128)(2,1)S(1)}, u32[]{:S(2)}, u32[]{:S(2)}) collective-permute-start(bf16[136,256]{1,0:T(8,128)(2,1)S(1)} %get-tuple-element.22), channel_id=1, source_target_pairs={{0,16},{4,20},{8,24},{12,28},{16,0},{20,4},{24,8},{28,12},{1,17},{... | collective-permute-start | bytes 208904 | tf_op jit(solution)/shard_map/ppermute | solution.py:407
  114.0 1.6 %copy-start = (bf16[128,8192]{1,0:T(8,128)(2,1)S(1)}, bf16[128,8192]{1,0:T(8,128)(2,1)}, u32[]{:S(2)}) copy-start(bf16[128,8192]{1,0:T(8,128)(2,1)} %h_ref.1) | copy-start | bytes 6291460
  116.4 13.0 %collective-permute-start.6 = (f32[1,256]{1,0:T(1,128)S(1)}, f32[1,256]{1,0:T(1,128)S(1)}, u32[]{:S(2)}, u32[]{:S(2)}) collective-permute-start(f32[1,256]{1,0:T(1,128)S(1)} %get-tuple-element.32), channel_id=1, source_target_pairs={{0,64},{64,0},{1,65},{65,1},{2,66},{66,2},{3,67},{67,3},{4,68},{68... | collective-permute-start | bytes 3080 | tf_op jit(solution)/shard_map/ppermute | solution.py:407
  130.0 13.6 %all-to-all-start.2 = ((f32[16,1,256]{2,1,0:T(1,128)}), f32[16,1,256]{2,1,0:T(1,128)S(1)}, u32[]{:S(2)}, u32[]{:S(2)}) async-start(f32[16,1,256]{2,1,0:T(1,128)} %broadcast_in_dim.9), calls=%async_computation.2 | async-start | bytes 32768 | tf_op jit(solution)/shard_map/all_to_all | solution.py:411

commit v4 on v2

--- a/solution.py
+++ b/solution.py
@@ -109,6 +109,7 @@
 ZQ = NZ // 2
 NG = 2 * NX
 PIECE = ZQ * TOK + 8
+AHEAD = 2
 
 
 def partial_kernel(q_ref, g_ref, w_hbm, h_hbm, out_hbm, w_ref, h_ref, out_ref, w_sem, h_sem, out_sem):
@@ -130,13 +131,16 @@
         at = (d, slice(ZQ * TOK, PIECE))
         return pltpu.make_async_copy(out_ref.at[at], out_hbm.at[at], out_sem.at[NZ * NX + d])
 
-    for z in range(NZ):
+    for z in range(AHEAD):
         w_copy(z).start()
         h_copy(z).start()
     q = q_ref[...]
     g = g_ref[...].astype(F32)
     acc = jnp.zeros((TOK, 128), F32)
     for z in range(NZ):
+        if z + AHEAD < NZ:
+            w_copy(z + AHEAD).start()
+            h_copy(z + AHEAD).start()
         w_copy(z).wait()
         h_copy(z).wait()
         for x in range(NX):
@@ -264,9 +268,7 @@
     rinv = rinv_ref[...]
     stat = jnp.sum(jnp.where(eye(), stat, 0.0), axis=1, keepdims=True) * rinv / D
     xhat = h_ref[:, aligned(own * B, B)].astype(F32) * rinv
-    total = jnp.sum(grad * xhat, axis=0, keepdims=True)
-    for i in range(NY * NH * NC):
-        gain_ref[i] = total
+    gain_ref[...] = jnp.sum(grad * xhat, axis=0, keepdims=True)
     out_ref[...] = (rinv * (grad * two_rows(g32, own) - xhat * stat)).astype(BF)
 
 
@@ -275,7 +277,7 @@
         finish_kernel,
         (
             jax.ShapeDtypeStruct((TOK, B), BF),
-            jax.ShapeDtypeStruct((NY * NH * NC, 1, B), F32),
+            jax.ShapeDtypeStruct((1, B), F32),
         ),
         (keep, got, hidden, gain, rinv),
         10,
@@ -335,8 +337,10 @@
 
 
 def sum_y_kernel(keep_ref, left_ref, right_ref, out_ref):
-    out_ref[0, :128, :] = (keep_ref[:128, :].astype(F32) + left_ref[...].astype(F32)).astype(BF)
-    out_ref[0, 128:, :] = (keep_ref[128:, :].astype(F32) + right_ref[...].astype(F32)).astype(BF)
+    for k in range(4):
+        at = slice(k * 512, (k + 1) * 512)
+        out_ref[k, :128, :] = (keep_ref[:128, at].astype(F32) + left_ref[:, at].astype(F32)).astype(BF)
+        out_ref[k, 128:, :] = (keep_ref[128:, at].astype(F32) + right_ref[:, at].astype(F32)).astype(BF)
 
 
 def sum_y(keep, left, right):
@@ -347,18 +351,13 @@
         8,
         TOK * D,
         3 * MB,
-        grid=(4,),
-        in_specs=[
-            pl.BlockSpec((B, 512), lambda k: (0, k)),
-            pl.BlockSpec((128, 512), lambda k: (0, k)),
-            pl.BlockSpec((128, 512), lambda k: (0, k)),
-        ],
-        out_specs=pl.BlockSpec((1, B, 512), lambda k: (k, 0, 0)),
+        in_specs=[VM] * 3,
+        out_specs=VM,
         name="sum_y",
     )
 
 
-def sum_y4_kernel(in_ref, send_ref, keep_ref):
+def sum_y4_kernel(in_ref, gain_ref, send_ref, keep_ref):
     zh = lax.axis_index("zh")
 
     def total(z):
@@ -368,39 +367,48 @@
             s = s + in_ref[k, :, at].astype(F32)
         return s
 
-    send_ref[...] = total(1 - zh).astype(BF)
+    send_ref[:B, :] = total(1 - zh).astype(BF)
     keep_ref[...] = total(zh)
-
-
-def sum_y4(got):
+    hi = gain_ref[...].astype(BF).astype(F32)
+    mid = (gain_ref[...] - hi).astype(BF).astype(F32)
+    low = gain_ref[...] - hi - mid
+    row = lax.broadcasted_iota(jnp.int32, (8, B), 0)
+    rows = jnp.where(row == 0, hi, jnp.where(row == 1, mid, jnp.where(row == 2, low, 0.0)))
+    send_ref[B:, :] = rows.astype(BF)
+
+
+def sum_y4(got, gain):
     return call(
         sum_y4_kernel,
-        (jax.ShapeDtypeStruct((B, B), BF), jax.ShapeDtypeStruct((B, B), F32)),
-        (got,),
+        (jax.ShapeDtypeStruct((B + 8, B), BF), jax.ShapeDtypeStruct((B, B), F32)),
+        (got, gain),
         6,
         TOK * D,
         2 * MB,
-        in_specs=[VM],
+        in_specs=[VM, VM],
         out_specs=(VM, VM),
         name="sum_y4",
     )
 
 
-def last_kernel(main_ref, keep_ref, got_ref, out_ref):
-    s = keep_ref[...] + got_ref[...].astype(F32)
-    out_ref[...] = main_ref[...] + s.T / (NY * NH * NC)
-
-
-def last(main, keep, got):
+def last_kernel(main_ref, keep_ref, got_ref, gain_ref, gain_main_ref, out_ref, gain_out_ref):
+    n = NY * NH * NC
+    s = keep_ref[...] + got_ref[:B, :].astype(F32)
+    out_ref[...] = main_ref[...] + s.T / n
+    got = jnp.sum(got_ref[B:, :].astype(F32), axis=0, keepdims=True)
+    gain_out_ref[...] = gain_main_ref[...] + (gain_ref[...] + got) / n
+
+
+def last(main, keep, got, gain, gain_main):
     return call(
         last_kernel,
-        jax.ShapeDtypeStruct((B, B), F32),
-        (main, keep, got),
+        (jax.ShapeDtypeStruct((B, B), F32), jax.ShapeDtypeStruct((1, B), F32)),
+        (main, keep, got, gain, gain_main),
         4,
         B * B * 4,
         MB,
-        in_specs=[VM] * 3,
-        out_specs=VM,
+        in_specs=[VM] * 5,
+        out_specs=(VM, VM),
         name="last",
     )
 
@@ -437,13 +445,16 @@
 
     send3, keep3 = sum_z(keep2, got2, 2, 4)
     got3 = swap(send3, "zl", NZ, lambda i: i ^ 4)
-    grad, all_gain = finish(keep3, got3, hidden, gain2, rinv)
-    all_gain = exchange(all_gain, ("y", "zh", "c"))
-
-    send_h, keep_h = sum_y4(four)
+    grad, own_gain = finish(keep3, got3, hidden, gain2, rinv)
+    own_gain += swap(own_gain, "c", NC, lambda i: i ^ 1)
+    own_gain += swap(own_gain, "y", NY, lambda i: i ^ 1)
+    own_gain += swap(own_gain, "y", NY, lambda i: i ^ 2)
+    own_gain += swap(own_gain, "y", NY, lambda i: i ^ 4)
+
+    send_h, keep_h = sum_y4(four, own_gain)
     got_h = swap(send_h, "zh", NH, lambda i: i ^ 1)
-    q_new = last(q_main, keep_h, got_h)
-    gain_new = gain_main + jnp.sum(all_gain, axis=(0, 1)) / (NY * NH * NC)
+    q_new, gain_new = last(q_main, keep_h, got_h, own_gain, gain_main.reshape(1, B))
+    gain_new = gain_new.reshape(B)
     return grad, q_new, gain_new
 
 

time: 129 us -> 133 us (1.031)
  the two profiles are of different devices: /device:TPU:1 before, /device:TPU:18 now
where the time goes in v4:
time: 133 us; the launch traced here: 132 us
  starting transfers between devices  61.5 us (46%)
  waiting for transfers between devices  51.5 us (39%)
  Pallas kernels  16.9 us (13%)
    ppermute x10, waiting for transfers between devices, swap(): return lax.ppermute(v, axis, pairs(n, f))  51.5 us
    ppermute x10, starting transfers between devices, swap(): return lax.ppermute(v, axis, pairs(n, f))  48.5 us
    pallas_call x9, Pallas kernels, call(): pl.pallas_call(kernel, out_shape=out_shape, compiler_params=params(mib),...  16.9 us
    all_to_all x2, starting transfers between devices, exchange(): return lax.all_to_all(v, axis, 0, 0, tiled=True, **kw)  13 us
  transfers between devices with their start and end apart: 12, of which 10 were waited for; matrix products, arithmetic and copies ran while one was open for 0% of the time, Pallas kernels for 7%

profile of v4, /device:TPU:18, one launch (start us, length us, event | category | flops | bytes accessed | tf_op | source)
XLA Modules:
  0.0 131.9 jit_solution(3414671412392701156)
XLA Ops:
  0.6 6.5 %partial.1 = bf16[8,520,256]{2,1,0:T(8,128)(2,1)} custom-call(bf16[128,256]{1,0:T(8,128)(2,1)} %q_ref.5, bf16[64,128]{1,0:T(8,128)(2,1)} %bitcast.3, bf16[8192,256]{1,0:T(8,128)(2,1)} %w_hbm.1, bf16[128,8192]{1,0:T(8,128)(2,1)} %h_ref.3), custom_call_target="tpu_custom_call" | custom-call | flops 536870912 | bytes 8388608 | tf_op jit(solution)/shard_map/partial/pallas_call | solution.py:30
  7.2 6.7 %all-to-all-start = ((bf16[8,520,256]{2,1,0:T(8,128)(2,1)}), bf16[8,520,256]{2,1,0:T(8,128)(2,1)}, u32[]{:S(2)}, u32[]{:S(2)}) async-start(bf16[8,520,256]{2,1,0:T(8,128)(2,1)} %partial.1), calls=%async_computation | async-start | bytes 4259840 | tf_op jit(solution)/shard_map/all_to_all | solution.py:425
  13.8 0.0 copy-start.2
  13.8 3.3 %norm.1 = (bf16[128,4352]{1,0:T(8,128)(2,1)}, bf16[128,4096]{1,0:T(8,128)(2,1)}, f32[128,1]{1,0:T(8,128)}) custom-call(bf16[128,8192]{1,0:T(8,128)(2,1)} %h_ref.3, bf16[64,128]{1,0:T(8,128)(2,1)} %bitcast.4, bf16[128,256]{1,0:T(8,128)(2,1)} %q_ref.5), custom_call_target="tpu_custom_call" | custom-call | flops 6291456 | bytes 4194304 | tf_op jit(solution)/shard_map/norm/pallas_call | solution.py:30
  17.1 1.9 %collective-permute-start.2 = (bf16[128,4352]{1,0:T(8,128)(2,1)}, bf16[128,4352]{1,0:T(8,128)(2,1)S(1)}, u32[]{:S(2)}, u32[]{:S(2)}) collective-permute-start(bf16[128,4352]{1,0:T(8,128)(2,1)} %get-tuple-element.26), channel_id=1, source_target_pairs={{0,32},{32,0},{1,33},{33,1},{2,34},{34,2},{3,35},{35,3},{4,36},{36... | collective-permute-start | bytes 3342344 | tf_op jit(solution)/shard_map/ppermute | solution.py:421
  19.0 2.9 %collective-permute-done.2.got_ref.gq_ref = bf16[128,4352]{1,0:T(8,128)(2,1)S(1)} collective-permute-done((bf16[128,4352]{1,0:T(8,128)(2,1)}, bf16[128,4352]{1,0:T(8,128)(2,1)S(1)}, u32[]{:S(2)}, u32[]{:S(2)}) %collective-permute-start.2) | collective-permute-done | bytes 1114144 | tf_op jit(solution)/shard_map/ppermute | solution.py:421
  22.0 0.0 copy-done.2
  22.0 0.0 copy-start.1
  22.0 1.2 copy-done.1
  23.2 2.1 %product.1 = (bf16[128,2048]{1,0:T(8,128)(2,1)S(1)}, bf16[128,2048]{1,0:T(8,128)(2,1)S(1)}, bf16[256,2048]{1,0:T(8,128)(2,1)S(1)}) custom-call(bf16[128,4096]{1,0:T(8,128)(2,1)S(1)} %copy-done.1, bf16[128,4352]{1,0:T(8,128)(2,1)S(1)} %collective-permute-done.2.got_ref.gq_ref, bf16[128,256]{1,0:T(8,128)(2,1)S(1)} %copy-done.2, ...), custom_call_target="tpu_custom_call" | custom-call | flops 536870912 | bytes 4194304 | tf_op jit(solution)/shard_map/product/pallas_call | solution.py:30
  25.3 3.5 %collective-permute-start.3 = (bf16[128,2048]{1,0:T(8,128)(2,1)S(1)}, bf16[128,2048]{1,0:T(8,128)(2,1)S(1)}, u32[]{:S(2)}, u32[]{:S(2)}) collective-permute-start(bf16[128,2048]{1,0:T(8,128)(2,1)S(1)} %get-tuple-element.28), channel_id=1, source_target_pairs={{0,128},{128,0},{256,384},{384,256},{512,640},{640,512},{768,896},... | collective-permute-start | bytes 1572872 | tf_op jit(solution)/shard_map/ppermute | solution.py:421
  28.8 12.0 %collective-permute-start.4 = (bf16[128,2048]{1,0:T(8,128)(2,1)S(1)}, bf16[128,2048]{1,0:T(8,128)(2,1)S(1)}, u32[]{:S(2)}, u32[]{:S(2)}) collective-permute-start(bf16[128,2048]{1,0:T(8,128)(2,1)S(1)} %get-tuple-element.29), channel_id=1, source_target_pairs={{0,896},{128,256},{256,128},{384,512},{512,384},{640,768},{768,640... | collective-permute-start | bytes 1572872 | tf_op jit(solution)/shard_map/ppermute | solution.py:421
  40.7 0.4 collective-permute-done.3.left_ref
  41.1 11.5 %collective-permute-done.4.right_ref = bf16[128,2048]{1,0:T(8,128)(2,1)S(1)} collective-permute-done((bf16[128,2048]{1,0:T(8,128)(2,1)S(1)}, bf16[128,2048]{1,0:T(8,128)(2,1)S(1)}, u32[]{:S(2)}, u32[]{:S(2)}) %collective-permute-start.4) | collective-permute-done | bytes 524320 | tf_op jit(solution)/shard_map/ppermute | solution.py:421
  52.7 1.3 sum_y.1
  53.9 0.0 copy-start
  53.9 0.0 copy-start.4
  53.9 0.0 copy-start.5
  53.9 0.0 all-to-all-done.in_ref
  53.9 6.3 %all-to-all-start.1 = ((bf16[4,256,512]{2,1,0:T(8,128)(2,1)}), bf16[4,256,512]{2,1,0:T(8,128)(2,1)S(1)}, u32[]{:S(2)}, u32[]{:S(2)}) async-start(bf16[4,256,512]{2,1,0:T(8,128)(2,1)} %sum_y.1), calls=%async_computation.1 | async-start | bytes 2097152 | tf_op jit(solution)/shard_map/all_to_all | solution.py:425
  60.2 1.9 %sum_xz.1 = (bf16[264,256]{1,0:T(8,128)(2,1)S(1)}, f32[264,256]{1,0:T(8,128)S(1)}) custom-call(bf16[8,520,256]{2,1,0:T(8,128)(2,1)} %all-to-all-done.in_ref), custom_call_target="tpu_custom_call" | custom-call | flops 1048576 | bytes 4194304 | tf_op jit(solution)/shard_map/sum_xz/pallas_call | solution.py:30
  62.1 0.0 copy-start.3
  62.1 0.0 copy-start.6
  62.1 2.1 %collective-permute-start = (bf16[264,256]{1,0:T(8,128)(2,1)S(1)}, bf16[264,256]{1,0:T(8,128)(2,1)S(1)}, u32[]{:S(2)}, u32[]{:S(2)}) collective-permute-start(bf16[264,256]{1,0:T(8,128)(2,1)S(1)} %get-tuple-element.20), channel_id=1, source_target_pairs={{0,8},{4,12},{8,0},{12,4},{16,24},{20,28},{24,16},{28,20},{1,9},{5... | collective-permute-start | bytes 405512 | tf_op jit(solution)/shard_map/ppermute | solution.py:421
  64.2 8.3 %collective-permute-done.got_ref = bf16[264,256]{1,0:T(8,128)(2,1)S(1)} collective-permute-done((bf16[264,256]{1,0:T(8,128)(2,1)S(1)}, bf16[264,256]{1,0:T(8,128)(2,1)S(1)}, u32[]{:S(2)}, u32[]{:S(2)}) %collective-permute-start) | collective-permute-done | bytes 135200 | tf_op jit(solution)/shard_map/ppermute | solution.py:421
  72.5 5.2 %collective-permute-start.1 = (bf16[136,256]{1,0:T(8,128)(2,1)S(1)}, bf16[136,256]{1,0:T(8,128)(2,1)S(1)}, u32[]{:S(2)}, u32[]{:S(2)}) collective-permute-start(bf16[136,256]{1,0:T(8,128)(2,1)S(1)} %get-tuple-element.22), channel_id=1, source_target_pairs={{0,16},{4,20},{8,24},{12,28},{16,0},{20,4},{24,8},{28,12},{1,17},{... | collective-permute-start | bytes 208904 | tf_op jit(solution)/shard_map/ppermute | solution.py:421
  77.7 6.9 %collective-permute-done.1.got_ref = bf16[136,256]{1,0:T(8,128)(2,1)S(1)} collective-permute-done((bf16[136,256]{1,0:T(8,128)(2,1)S(1)}, bf16[136,256]{1,0:T(8,128)(2,1)S(1)}, u32[]{:S(2)}, u32[]{:S(2)}) %collective-permute-start.1) | collective-permute-done | bytes 69664 | tf_op jit(solution)/shard_map/ppermute | solution.py:421
  84.5 0.0 copy-done
  84.5 0.0 copy-done.4
  84.5 0.0 copy-done.5
  84.5 0.8 finish.1
  85.4 1.9 %collective-permute-start.5 = (f32[1,256]{1,0:T(1,128)S(1)}, f32[1,256]{1,0:T(1,128)S(1)}, u32[]{:S(2)}, u32[]{:S(2)}) collective-permute-start(f32[1,256]{1,0:T(1,128)S(1)} %get-tuple-element.30), channel_id=1, source_target_pairs={{0,32},{32,0},{1,33},{33,1},{2,34},{34,2},{3,35},{35,3},{4,36},{36... | collective-permute-start | bytes 3080 | tf_op jit(solution)/shard_map/ppermute | solution.py:421
  87.3 1.1 collective-permute-done.5
  88.4 2.1 %collective-permute-start.6 = (f32[1,256]{1,0:T(1,128)S(1)}, f32[1,256]{1,0:T(1,128)S(1)}, u32[]{:S(2)}, u32[]{:S(2)}) collective-permute-start(f32[1,256]{1,0:T(1,128)S(1)} %add.12), channel_id=1, source_target_pairs={{0,128},{128,0},{256,384},{384,256},{512,640},{640,512},{768,896},... | collective-permute-start | bytes 3080 | tf_op jit(solution)/shard_map/ppermute | solution.py:421
  90.5 3.3 %collective-permute-done.6 = f32[1,256]{1,0:T(1,128)S(1)} collective-permute-done((f32[1,256]{1,0:T(1,128)S(1)}, f32[1,256]{1,0:T(1,128)S(1)}, u32[]{:S(2)}, u32[]{:S(2)}) %collective-permute-start.6) | collective-permute-done | bytes 1056 | tf_op jit(solution)/shard_map/ppermute | solution.py:421
  93.9 2.4 %collective-permute-start.7 = (f32[1,256]{1,0:T(1,128)S(1)}, f32[1,256]{1,0:T(1,128)S(1)}, u32[]{:S(2)}, u32[]{:S(2)}) collective-permute-start(f32[1,256]{1,0:T(1,128)S(1)} %add.13), channel_id=1, source_target_pairs={{0,256},{128,384},{256,0},{384,128},{512,768},{640,896},{768,512},... | collective-permute-start | bytes 3080 | tf_op jit(solution)/shard_map/ppermute | solution.py:421
  96.2 4.0 %collective-permute-done.7 = f32[1,256]{1,0:T(1,128)S(1)} collective-permute-done((f32[1,256]{1,0:T(1,128)S(1)}, f32[1,256]{1,0:T(1,128)S(1)}, u32[]{:S(2)}, u32[]{:S(2)}) %collective-permute-start.7) | collective-permute-done | bytes 1056 | tf_op jit(solution)/shard_map/ppermute | solution.py:421
  100.2 5.5 %collective-permute-start.8 = (f32[1,256]{1,0:T(1,128)S(1)}, f32[1,256]{1,0:T(1,128)S(1)}, u32[]{:S(2)}, u32[]{:S(2)}) collective-permute-start(f32[1,256]{1,0:T(1,128)S(1)} %add.14), channel_id=1, source_target_pairs={{0,512},{128,640},{256,768},{384,896},{512,0},{640,128},{768,256},... | collective-permute-start | bytes 3080 | tf_op jit(solution)/shard_map/ppermute | solution.py:421
  105.7 3.9 %collective-permute-done.8 = f32[1,256]{1,0:T(1,128)S(1)} collective-permute-done((f32[1,256]{1,0:T(1,128)S(1)}, f32[1,256]{1,0:T(1,128)S(1)}, u32[]{:S(2)}, u32[]{:S(2)}) %collective-permute-start.8) | collective-permute-done | bytes 1056 | tf_op jit(solution)/shard_map/ppermute | solution.py:421
  109.6 0.0 all-to-all-done.1.in_ref
  109.6 0.1 sum_y4.1
  109.7 12.1 %collective-permute-start.9 = (bf16[264,256]{1,0:T(8,128)(2,1)S(1)}, bf16[264,256]{1,0:T(8,128)(2,1)S(1)}, u32[]{:S(2)}, u32[]{:S(2)}) collective-permute-start(bf16[264,256]{1,0:T(8,128)(2,1)S(1)} %get-tuple-element.32), channel_id=1, source_target_pairs={{0,64},{64,0},{1,65},{65,1},{2,66},{66,2},{3,67},{67,3},{4,68},{68... | collective-permute-start | bytes 405512 | tf_op jit(solution)/shard_map/ppermute | solution.py:421
  121.9 9.2 %collective-permute-done.9.got_ref = bf16[264,256]{1,0:T(8,128)(2,1)S(1)} collective-permute-done((bf16[264,256]{1,0:T(8,128)(2,1)S(1)}, bf16[264,256]{1,0:T(8,128)(2,1)S(1)}, u32[]{:S(2)}, u32[]{:S(2)}) %collective-permute-start.9) | collective-permute-done | bytes 135200 | tf_op jit(solution)/shard_map/ppermute | solution.py:421
  131.0 0.0 copy-done.3
  131.0 0.0 copy-done.6
  131.0 0.8 last.1
  (5 shorter events, 0.1 us)
Async XLA Ops:
  7.2 46.8 %all-to-all-start = ((bf16[8,520,256]{2,1,0:T(8,128)(2,1)}), bf16[8,520,256]{2,1,0:T(8,128)(2,1)}, u32[]{:S(2)}, u32[]{:S(2)}) async-start(bf16[8,520,256]{2,1,0:T(8,128)(2,1)} %partial.1), calls=%async_computation | async-start | bytes 4259840 | tf_op jit(solution)/shard_map/all_to_all | solution.py:425
  13.8 8.1 %copy-start.2 = (bf16[128,256]{1,0:T(8,128)(2,1)S(1)}, bf16[128,256]{1,0:T(8,128)(2,1)}, u32[]{:S(2)}) copy-start(bf16[128,256]{1,0:T(8,128)(2,1)} %q_ref.5) | copy-start | bytes 196612
  17.1 4.8 %collective-permute-start.2 = (bf16[128,4352]{1,0:T(8,128)(2,1)}, bf16[128,4352]{1,0:T(8,128)(2,1)S(1)}, u32[]{:S(2)}, u32[]{:S(2)}) collective-permute-start(bf16[128,4352]{1,0:T(8,128)(2,1)} %get-tuple-element.26), channel_id=1, source_target_pairs={{0,32},{32,0},{1,33},{33,1},{2,34},{34,2},{3,35},{35,3},{4,36},{36... | collective-permute-start | bytes 3342344 | tf_op jit(solution)/shard_map/ppermute | solution.py:421
  22.0 1.2 copy-start.1
  25.3 15.9 %collective-permute-start.3 = (bf16[128,2048]{1,0:T(8,128)(2,1)S(1)}, bf16[128,2048]{1,0:T(8,128)(2,1)S(1)}, u32[]{:S(2)}, u32[]{:S(2)}) collective-permute-start(bf16[128,2048]{1,0:T(8,128)(2,1)S(1)} %get-tuple-element.28), channel_id=1, source_target_pairs={{0,128},{128,0},{256,384},{384,256},{512,640},{640,512},{768,896},... | collective-permute-start | bytes 1572872 | tf_op jit(solution)/shard_map/ppermute | solution.py:421
  28.8 23.9 %collective-permute-start.4 = (bf16[128,2048]{1,0:T(8,128)(2,1)S(1)}, bf16[128,2048]{1,0:T(8,128)(2,1)S(1)}, u32[]{:S(2)}, u32[]{:S(2)}) collective-permute-start(bf16[128,2048]{1,0:T(8,128)(2,1)S(1)} %get-tuple-element.29), channel_id=1, source_target_pairs={{0,896},{128,256},{256,128},{384,512},{512,384},{640,768},{768,640... | collective-permute-start | bytes 1572872 | tf_op jit(solution)/shard_map/ppermute | solution.py:421
  53.9 30.6 %copy-start = (bf16[128,8192]{1,0:T(8,128)(2,1)S(1)}, bf16[128,8192]{1,0:T(8,128)(2,1)}, u32[]{:S(2)}) copy-start(bf16[128,8192]{1,0:T(8,128)(2,1)} %h_ref.3) | copy-start | bytes 6291460
  53.9 30.6 %copy-start.4 = (bf16[8192]{0:T(1024)(128)(2,1)S(1)}, bf16[8192]{0:T(1024)(128)(2,1)}, u32[]{:S(2)}) copy-start(bf16[8192]{0:T(1024)(128)(2,1)} %param.7) | copy-start | bytes 49156
  53.9 30.6 %copy-start.5 = (f32[128,1]{1,0:T(8,128)S(1)}, f32[128,1]{1,0:T(8,128)}, u32[]{:S(2)}) copy-start(f32[128,1]{1,0:T(8,128)} %get-tuple-element.23.rinv_ref) | copy-start | bytes 1540
  53.9 55.7 %all-to-all-start.1 = ((bf16[4,256,512]{2,1,0:T(8,128)(2,1)}), bf16[4,256,512]{2,1,0:T(8,128)(2,1)S(1)}, u32[]{:S(2)}, u32[]{:S(2)}) async-start(bf16[4,256,512]{2,1,0:T(8,128)(2,1)} %sum_y.1), calls=%async_computation.1 | async-start | bytes 2097152 | tf_op jit(solution)/shard_map/all_to_all | solution.py:425
  62.1 68.9 %copy-start.3 = (f32[256,256]{1,0:T(8,128)S(1)}, f32[256,256]{1,0:T(8,128)}, u32[]{:S(2)}) copy-start(f32[256,256]{1,0:T(8,128)} %main_ref.1) | copy-start | bytes 786436
  62.1 68.9 %copy-start.6 = (f32[256]{0:T(256)S(1)}, f32[256]{0:T(256)}, u32[]{:S(2)}) copy-start(f32[256]{0:T(256)} %param.11) | copy-start | bytes 3076
  62.1 10.3 %collective-permute-start = (bf16[264,256]{1,0:T(8,128)(2,1)S(1)}, bf16[264,256]{1,0:T(8,128)(2,1)S(1)}, u32[]{:S(2)}, u32[]{:S(2)}) collective-permute-start(bf16[264,256]{1,0:T(8,128)(2,1)S(1)} %get-tuple-element.20), channel_id=1, source_target_pairs={{0,8},{4,12},{8,0},{12,4},{16,24},{20,28},{24,16},{28,20},{1,9},{5... | collective-permute-start | bytes 405512 | tf_op jit(solution)/shard_map/ppermute | solution.py:421
  72.5 12.0 %collective-permute-start.1 = (bf16[136,256]{1,0:T(8,128)(2,1)S(1)}, bf16[136,256]{1,0:T(8,128)(2,1)S(1)}, u32[]{:S(2)}, u32[]{:S(2)}) collective-permute-start(bf16[136,256]{1,0:T(8,128)(2,1)S(1)} %get-tuple-element.22), channel_id=1, source_target_pairs={{0,16},{4,20},{8,24},{12,28},{16,0},{20,4},{24,8},{28,12},{1,17},{... | collective-permute-start | bytes 208904 | tf_op jit(solution)/shard_map/ppermute | solution.py:421
  85.4 3.0 %collective-permute-start.5 = (f32[1,256]{1,0:T(1,128)S(1)}, f32[1,256]{1,0:T(1,128)S(1)}, u32[]{:S(2)}, u32[]{:S(2)}) collective-permute-start(f32[1,256]{1,0:T(1,128)S(1)} %get-tuple-element.30), channel_id=1, source_target_pairs={{0,32},{32,0},{1,33},{33,1},{2,34},{34,2},{3,35},{35,3},{4,36},{36... | collective-permute-start | bytes 3080 | tf_op jit(solution)/shard_map/ppermute | solution.py:421
  88.4 5.5 %collective-permute-start.6 = (f32[1,256]{1,0:T(1,128)S(1)}, f32[1,256]{1,0:T(1,128)S(1)}, u32[]{:S(2)}, u32[]{:S(2)}) collective-permute-start(f32[1,256]{1,0:T(1,128)S(1)} %add.12), channel_id=1, source_target_pairs={{0,128},{128,0},{256,384},{384,256},{512,640},{640,512},{768,896},... | collective-permute-start | bytes 3080 | tf_op jit(solution)/shard_map/ppermute | solution.py:421
  93.9 6.4 %collective-permute-start.7 = (f32[1,256]{1,0:T(1,128)S(1)}, f32[1,256]{1,0:T(1,128)S(1)}, u32[]{:S(2)}, u32[]{:S(2)}) collective-permute-start(f32[1,256]{1,0:T(1,128)S(1)} %add.13), channel_id=1, source_target_pairs={{0,256},{128,384},{256,0},{384,128},{512,768},{640,896},{768,512},... | collective-permute-start | bytes 3080 | tf_op jit(solution)/shard_map/ppermute | solution.py:421
  100.2 9.4 %collective-permute-start.8 = (f32[1,256]{1,0:T(1,128)S(1)}, f32[1,256]{1,0:T(1,128)S(1)}, u32[]{:S(2)}, u32[]{:S(2)}) collective-permute-start(f32[1,256]{1,0:T(1,128)S(1)} %add.14), channel_id=1, source_target_pairs={{0,512},{128,640},{256,768},{384,896},{512,0},{640,128},{768,256},... | collective-permute-start | bytes 3080 | tf_op jit(solution)/shard_map/ppermute | solution.py:421
  109.7 21.3 %collective-permute-start.9 = (bf16[264,256]{1,0:T(8,128)(2,1)S(1)}, bf16[264,256]{1,0:T(8,128)(2,1)S(1)}, u32[]{:S(2)}, u32[]{:S(2)}) collective-permute-start(bf16[264,256]{1,0:T(8,128)(2,1)S(1)} %get-tuple-element.32), channel_id=1, source_target_pairs={{0,64},{64,0},{1,65},{65,1},{2,66},{66,2},{3,67},{67,3},{4,68},{68... | collective-permute-start | bytes 405512 | tf_op jit(solution)/shard_map/ppermute | solution.py:421

commit v5 on v2

--- a/solution.py
+++ b/solution.py
@@ -1,5 +1,3 @@
-import functools
-
 import jax
 import jax.numpy as jnp
 from jax import lax
@@ -77,7 +75,7 @@
             jax.ShapeDtypeStruct((TOK, 1), F32),
         ),
         (hidden, gain, q_grad),
-        None,
+        16,
         6 * TOK * D,
         4 * TOK * D,
         grid=(TOK // ROWS,),
@@ -190,9 +188,7 @@
     )
 
 
-def sum_xz_kernel(in_ref, send_ref, keep_ref):
-    bit = lax.rem(lax.div(lax.axis_index("zl"), 2), 2)
-
+def sum_xz_kernel(in_ref, out_ref):
     def total(at):
         s = in_ref[0, at, :].astype(F32)
         for d in range(1, NG):
@@ -200,88 +196,49 @@
         return s
 
     rows = stat_rows(stat_of(total(slice(ZQ * TOK, PIECE))))
-    for k in range(ZQ // 2):
-        at = slice(k * TOK, (k + 1) * TOK)
-        send_ref[at, :] = total(aligned((2 * k + 1 - bit) * TOK, TOK)).astype(BF)
-        keep_ref[at, :] = total(aligned((2 * k + bit) * TOK, TOK))
-    send_ref[ZQ // 2 * TOK :, :] = rows
-    keep_ref[ZQ // 2 * TOK :, :] = rows.astype(F32)
+    for k in range(ZQ):
+        out_ref[k, :TOK, :] = total(slice(k * TOK, (k + 1) * TOK)).astype(BF)
+        out_ref[k, TOK:, :] = rows
 
 
 def sum_xz(got):
-    rows = ZQ // 2 * TOK + 8
     return call(
         sum_xz_kernel,
-        (jax.ShapeDtypeStruct((rows, B), BF), jax.ShapeDtypeStruct((rows, B), F32)),
+        jax.ShapeDtypeStruct((ZQ, TOK + 8, B), BF),
         (got,),
         12,
         TOK * D,
         4 * MB,
         in_specs=[VM],
-        out_specs=(VM, VM),
+        out_specs=VM,
         name="sum_xz",
     )
 
 
-def sum_z_kernel(count, shift, keep_ref, got_ref, send_ref, out_ref):
-    bit = lax.rem(lax.div(lax.axis_index("zl"), shift), 2)
-    half = count // 2
-
-    def total(at):
-        return keep_ref[at, :] + got_ref[at, :].astype(F32)
-
-    for k in range(half):
-        at = slice(k * TOK, (k + 1) * TOK)
-        send_ref[at, :] = total(aligned((2 * k + 1 - bit) * TOK, TOK)).astype(BF)
-    rows = stat_rows(stat_of(total(slice(count * TOK, count * TOK + 8))))
-    send_ref[half * TOK :, :] = rows
-    for k in range(half):
-        at = slice(k * TOK, (k + 1) * TOK)
-        out_ref[at, :] = total(aligned((2 * k + bit) * TOK, TOK))
-    out_ref[half * TOK :, :] = rows.astype(F32)
-
-
-def sum_z(keep, got, count, shift):
-    rows = count // 2 * TOK + 8
-    return call(
-        functools.partial(sum_z_kernel, count, shift),
-        (jax.ShapeDtypeStruct((rows, B), BF), jax.ShapeDtypeStruct((rows, B), F32)),
-        (keep, got),
-        6,
-        count * TOK * B,
-        count * MB // 2,
-        in_specs=[VM, VM],
-        out_specs=(VM, VM),
-        name=f"sum_z{shift}",
-    )
-
-
-def finish_kernel(keep_ref, got_ref, h_ref, g_ref, rinv_ref, out_ref, gain_ref, g32):
+def finish_kernel(got_ref, h_ref, g_ref, rinv_ref, out_ref, gain_ref, g32):
     own = lax.axis_index("zl") * NX + lax.axis_index("x")
     g32[...] = g_ref[...].astype(F32)
-    grad = keep_ref[:TOK, :] + got_ref[:TOK, :].astype(F32)
-    stat = stat_of(keep_ref[TOK:, :] + got_ref[TOK:, :].astype(F32))
+    grad = got_ref[0, :TOK, :].astype(F32)
+    stat = stat_of(got_ref[0, TOK:, :])
+    for k in range(1, ZQ):
+        grad = grad + got_ref[k, :TOK, :].astype(F32)
+        stat = stat + stat_of(got_ref[k, TOK:, :])
     rinv = rinv_ref[...]
     stat = jnp.sum(jnp.where(eye(), stat, 0.0), axis=1, keepdims=True) * rinv / D
     xhat = h_ref[:, aligned(own * B, B)].astype(F32) * rinv
-    total = jnp.sum(grad * xhat, axis=0, keepdims=True)
-    for i in range(NY * NH * NC):
-        gain_ref[i] = total
+    gain_ref[...] = jnp.sum(grad * xhat, axis=0, keepdims=True)
     out_ref[...] = (rinv * (grad * two_rows(g32, own) - xhat * stat)).astype(BF)
 
 
-def finish(keep, got, hidden, gain, rinv):
+def finish(got, hidden, gain, rinv):
     return call(
         finish_kernel,
-        (
-            jax.ShapeDtypeStruct((TOK, B), BF),
-            jax.ShapeDtypeStruct((NY * NH * NC, 1, B), F32),
-        ),
-        (keep, got, hidden, gain, rinv),
+        (jax.ShapeDtypeStruct((TOK, B), BF), jax.ShapeDtypeStruct((1, B), F32)),
+        (got, hidden, gain, rinv),
         10,
         TOK * B * 16,
         MB,
-        in_specs=[VM] * 5,
+        in_specs=[VM] * 4,
         out_specs=(VM, VM),
         scratch_shapes=[pltpu.VMEM((64, 128), F32)],
         name="finish",
@@ -335,8 +292,10 @@
 
 
 def sum_y_kernel(keep_ref, left_ref, right_ref, out_ref):
-    out_ref[0, :128, :] = (keep_ref[:128, :].astype(F32) + left_ref[...].astype(F32)).astype(BF)
-    out_ref[0, 128:, :] = (keep_ref[128:, :].astype(F32) + right_ref[...].astype(F32)).astype(BF)
+    for k in range(4):
+        at = slice(k * 512, (k + 1) * 512)
+        out_ref[k, :128, :] = (keep_ref[:128, at].astype(F32) + left_ref[:, at].astype(F32)).astype(BF)
+        out_ref[k, 128:, :] = (keep_ref[128:, at].astype(F32) + right_ref[:, at].astype(F32)).astype(BF)
 
 
 def sum_y(keep, left, right):
@@ -347,13 +306,8 @@
         8,
         TOK * D,
         3 * MB,
-        grid=(4,),
-        in_specs=[
-            pl.BlockSpec((B, 512), lambda k: (0, k)),
-            pl.BlockSpec((128, 512), lambda k: (0, k)),
-            pl.BlockSpec((128, 512), lambda k: (0, k)),
-        ],
-        out_specs=pl.BlockSpec((1, B, 512), lambda k: (k, 0, 0)),
+        in_specs=[VM] * 3,
+        out_specs=VM,
         name="sum_y",
     )
 
@@ -429,19 +383,17 @@
     left = swap(left, "y", NY, lambda i: i ^ 1)
     right = swap(right, "y", NY, lambda i: i + 1 if i % 2 else i - 1)
 
-    send2, keep2 = sum_xz(part)
-    got2 = swap(send2, "zl", NZ, lambda i: i ^ 2)
-
-    four = sum_y(keep, left, right)
-    four = exchange(four, "y", axis_index_groups=[[0, 2, 4, 6], [1, 3, 5, 7]])
-
-    send3, keep3 = sum_z(keep2, got2, 2, 4)
-    got3 = swap(send3, "zl", NZ, lambda i: i ^ 4)
-    grad, all_gain = finish(keep3, got3, hidden, gain2, rinv)
-    all_gain = exchange(all_gain, ("y", "zh", "c"))
+    evens_odds = [[0, 2, 4, 6], [1, 3, 5, 7]]
+    part = exchange(sum_xz(part), "zl", axis_index_groups=evens_odds)
+    grad, own_gain = finish(part, hidden, gain2, rinv)
+
+    four = exchange(sum_y(keep, left, right), "y", axis_index_groups=evens_odds)
+    got_gain = swap(own_gain, "zh", NH, lambda i: i ^ 1)
 
     send_h, keep_h = sum_y4(four)
     got_h = swap(send_h, "zh", NH, lambda i: i ^ 1)
+    all_gain = jnp.broadcast_to((own_gain + got_gain)[None], (NY * NC, 1, B))
+    all_gain = exchange(all_gain, ("y", "c"))
     q_new = last(q_main, keep_h, got_h)
     gain_new = gain_main + jnp.sum(all_gain, axis=(0, 1)) / (NY * NH * NC)
     return grad, q_new, gain_new

time: 129 us -> 146 us (1.13)
  starting transfers between devices: 55 us -> 75.9 us
  local copies, waits for them, and re-layouts: 7.31 us -> 2.04 us
  waiting for transfers between devices: 47.8 us -> 51.7 us
  Pallas kernels: 16.4 us -> 14.5 us
    all_to_all x3 -> x4, starting transfers between devices: 19.1 us -> 38.9 us  [exchange(): return lax.all_to_all(v, axis, 0, 0, tiled=True, **kw)]
    unnamed x26 -> x16, local copies, waits for them, and re-layouts: 7.31 us -> 1.43 us
    all_to_all x3 -> x4, waiting for transfers between devices: 25.9 us -> 29.7 us  [exchange(): return lax.all_to_all(v, axis, 0, 0, tiled=True, **kw)]
    pallas_call x9 -> x8, Pallas kernels: 16.4 us -> 14.5 us  [call(): pl.pallas_call(kernel, out_shape=out_shape, compiler_params=params(mib),...]
    ppermute x6 -> x5, starting transfers between devices: 35.9 us -> 37 us  [swap(): return lax.ppermute(v, axis, pairs(n, f))]
    ppermute x6 -> x5, waiting for transfers between devices: 21.9 us -> 22 us  [swap(): return lax.ppermute(v, axis, pairs(n, f))]
  transfers between devices with their start and end apart: 9 -> 9, of which waited for: 6 -> 6; matrix products, arithmetic and copies ran while one was open for 0% -> 0% of each run, Pallas kernels for 8% -> 6%
where the time goes in v5:
time: 146 us
  starting transfers between devices  75.9 us (52%)
  waiting for transfers between devices  51.7 us (35%)
  Pallas kernels  14.5 us (10%)
  local copies, waits for them, and re-layouts  2.04 us (1%)
    all_to_all x4, starting transfers between devices, exchange(): return lax.all_to_all(v, axis, 0, 0, tiled=True, **kw)  38.9 us
    ppermute x5, starting transfers between devices, swap(): return lax.ppermute(v, axis, pairs(n, f))  37 us
    all_to_all x4, waiting for transfers between devices, exchange(): return lax.all_to_all(v, axis, 0, 0, tiled=True, **kw)  29.7 us
    ppermute x5, waiting for transfers between devices, swap(): return lax.ppermute(v, axis, pairs(n, f))  22 us
    pallas_call x8, Pallas kernels, call(): pl.pallas_call(kernel, out_shape=out_shape, compiler_params=params(mib),...  14.5 us
  transfers between devices with their start and end apart: 9, of which 6 were waited for; matrix products, arithmetic and copies ran while one was open for 0% of the time, Pallas kernels for 6%

profile of v5, /device:TPU:1, one launch (start us, length us, event | category | flops | bytes accessed | tf_op | source)
XLA Modules:
  0.0 145.6 jit_solution(6750201405872348224)
XLA Ops:
  0.6 5.9 %partial.1 = bf16[8,520,256]{2,1,0:T(8,128)(2,1)} custom-call(bf16[128,256]{1,0:T(8,128)(2,1)} %q_ref.5, bf16[64,128]{1,0:T(8,128)(2,1)} %bitcast.2, bf16[8192,256]{1,0:T(8,128)(2,1)} %w_hbm.1, bf16[128,8192]{1,0:T(8,128)(2,1)} %h_ref.3), custom_call_target="tpu_custom_call" | custom-call | flops 536870912 | bytes 8388608 | tf_op jit(solution)/shard_map/partial/pallas_call | solution.py:28
  6.5 0.0 copy-start
  6.6 0.0 copy-start.2
  6.6 0.0 copy-start.6
  6.6 6.8 %all-to-all-start = ((bf16[8,520,256]{2,1,0:T(8,128)(2,1)}), bf16[8,520,256]{2,1,0:T(8,128)(2,1)}, u32[]{:S(2)}, u32[]{:S(2)}) async-start(bf16[8,520,256]{2,1,0:T(8,128)(2,1)} %partial.1), calls=%async_computation | async-start | bytes 4259840 | tf_op jit(solution)/shard_map/all_to_all | solution.py:371
  13.4 0.0 copy-done
  13.4 0.0 copy-done.2
  13.4 0.0 copy-done.6
  13.4 1.0 norm.1
  14.4 13.7 %collective-permute-start = (bf16[128,4352]{1,0:T(8,128)(2,1)S(1)}, bf16[128,4352]{1,0:T(8,128)(2,1)S(1)}, u32[]{:S(2)}, u32[]{:S(2)}) collective-permute-start(bf16[128,4352]{1,0:T(8,128)(2,1)S(1)} %get-tuple-element.16), channel_id=1, source_target_pairs={{0,32},{32,0},{1,33},{33,1},{2,34},{34,2},{3,35},{35,3},{4,36},{36... | collective-permute-start | bytes 3342344 | tf_op jit(solution)/shard_map/ppermute | solution.py:367
  28.2 2.4 %collective-permute-done.got_ref.gq_ref = bf16[128,4352]{1,0:T(8,128)(2,1)S(1)} collective-permute-done((bf16[128,4352]{1,0:T(8,128)(2,1)S(1)}, bf16[128,4352]{1,0:T(8,128)(2,1)S(1)}, u32[]{:S(2)}, u32[]{:S(2)}) %collective-permute-start) | collective-permute-done | bytes 1114144 | tf_op jit(solution)/shard_map/ppermute | solution.py:367
  30.5 2.1 %product.1 = (bf16[128,2048]{1,0:T(8,128)(2,1)S(1)}, bf16[128,2048]{1,0:T(8,128)(2,1)S(1)}, bf16[256,2048]{1,0:T(8,128)(2,1)S(1)}) custom-call(bf16[128,4096]{1,0:T(8,128)(2,1)S(1)} %get-tuple-element.15.own_ref, bf16[128,4352]{1,0:T(8,128)(2,1)S(1)} %collective-permute-done.got_ref.gq_ref, bf16[128,256]{1,0:T(8,128)(2,1)S(1)} %copy-done.2, ...), custom_call_target="tpu_custom_call" | custom-call | flops 536870912 | bytes 4194304 | tf_op jit(solution)/shard_map/product/pallas_call | solution.py:28
  32.6 1.9 %collective-permute-start.1 = (bf16[128,2048]{1,0:T(8,128)(2,1)S(1)}, bf16[128,2048]{1,0:T(8,128)(2,1)S(1)}, u32[]{:S(2)}, u32[]{:S(2)}) collective-permute-start(bf16[128,2048]{1,0:T(8,128)(2,1)S(1)} %get-tuple-element.18), channel_id=1, source_target_pairs={{0,128},{128,0},{256,384},{384,256},{512,640},{640,512},{768,896},... | collective-permute-start | bytes 1572872 | tf_op jit(solution)/shard_map/ppermute | solution.py:367
  34.5 1.9 %collective-permute-start.2 = (bf16[128,2048]{1,0:T(8,128)(2,1)S(1)}, bf16[128,2048]{1,0:T(8,128)(2,1)S(1)}, u32[]{:S(2)}, u32[]{:S(2)}) collective-permute-start(bf16[128,2048]{1,0:T(8,128)(2,1)S(1)} %get-tuple-element.19), channel_id=1, source_target_pairs={{0,896},{128,256},{256,128},{384,512},{512,384},{640,768},{768,640... | collective-permute-start | bytes 1572872 | tf_op jit(solution)/shard_map/ppermute | solution.py:367
  36.5 11.1 %collective-permute-done.1.left_ref = bf16[128,2048]{1,0:T(8,128)(2,1)S(1)} collective-permute-done((bf16[128,2048]{1,0:T(8,128)(2,1)S(1)}, bf16[128,2048]{1,0:T(8,128)(2,1)S(1)}, u32[]{:S(2)}, u32[]{:S(2)}) %collective-permute-start.1) | collective-permute-done | bytes 524320 | tf_op jit(solution)/shard_map/ppermute | solution.py:367
  47.6 3.1 %collective-permute-done.2.right_ref = bf16[128,2048]{1,0:T(8,128)(2,1)S(1)} collective-permute-done((bf16[128,2048]{1,0:T(8,128)(2,1)S(1)}, bf16[128,2048]{1,0:T(8,128)(2,1)S(1)}, u32[]{:S(2)}, u32[]{:S(2)}) %collective-permute-start.2) | collective-permute-done | bytes 524320 | tf_op jit(solution)/shard_map/ppermute | solution.py:367
  50.8 1.2 sum_y.1
  52.0 0.0 all-to-all-done.in_ref
  52.0 3.5 %all-to-all-start.2 = ((bf16[4,256,512]{2,1,0:T(8,128)(2,1)}), bf16[4,256,512]{2,1,0:T(8,128)(2,1)S(1)}, u32[]{:S(2)}, u32[]{:S(2)}) async-start(bf16[4,256,512]{2,1,0:T(8,128)(2,1)} %sum_y.1), calls=%async_computation.2 | async-start | bytes 2097152 | tf_op jit(solution)/shard_map/all_to_all | solution.py:371
  55.5 1.9 %sum_xz.1 = bf16[4,136,256]{2,1,0:T(8,128)(2,1)S(1)} custom-call(bf16[8,520,256]{2,1,0:T(8,128)(2,1)} %all-to-all-done.in_ref), custom_call_target="tpu_custom_call" | custom-call | flops 1048576 | bytes 4194304 | tf_op jit(solution)/shard_map/sum_xz/pallas_call | solution.py:28
  57.4 0.0 copy-start.1
  57.4 0.7 copy-done.1
  58.1 23.2 %all-to-all-done.2.in_ref = bf16[4,256,512]{2,1,0:T(8,128)(2,1)S(1)} async-done(((bf16[4,256,512]{2,1,0:T(8,128)(2,1)}), bf16[4,256,512]{2,1,0:T(8,128)(2,1)S(1)}, u32[]{:S(2)}, u32[]{:S(2)}) %all-to-all-start.2) | async-done | bytes 1048608 | tf_op jit(solution)/shard_map/all_to_all | solution.py:371
  81.4 6.2 %all-to-all-start.1 = ((bf16[4,136,256]{2,1,0:T(8,128)(2,1)}), bf16[4,136,256]{2,1,0:T(8,128)(2,1)S(1)}, u32[]{:S(2)}, u32[]{:S(2)}) async-start(bf16[4,136,256]{2,1,0:T(8,128)(2,1)} %copy-done.1), calls=%async_computation.1 | async-start | bytes 557056 | tf_op jit(solution)/shard_map/all_to_all | solution.py:371
  87.5 0.0 copy-start.7
  87.5 0.7 sum_y4.1
  88.2 0.0 copy-start.4
  88.2 0.7 copy-done.4
  88.9 0.0 copy-start.3
  88.9 0.0 copy-start.5
  89.0 11.7 %collective-permute-start.3 = (bf16[256,256]{1,0:T(8,128)(2,1)}, bf16[256,256]{1,0:T(8,128)(2,1)S(1)}, u32[]{:S(2)}, u32[]{:S(2)}) collective-permute-start(bf16[256,256]{1,0:T(8,128)(2,1)} %get-tuple-element.21), channel_id=1, source_target_pairs={{0,64},{64,0},{1,65},{65,1},{2,66},{66,2},{3,67},{67,3},{4,68},{68... | collective-permute-start | bytes 393224 | tf_op jit(solution)/shard_map/ppermute | solution.py:367
  100.7 0.0 all-to-all-done.1.got_ref
  100.7 0.8 finish.1
  101.5 7.8 %collective-permute-start.4 = (f32[1,256]{1,0:T(1,128)S(1)}, f32[1,256]{1,0:T(1,128)S(1)}, u32[]{:S(2)}, u32[]{:S(2)}) collective-permute-start(f32[1,256]{1,0:T(1,128)S(1)} %get-tuple-element.22), channel_id=1, source_target_pairs={{0,64},{64,0},{1,65},{65,1},{2,66},{66,2},{3,67},{67,3},{4,68},{68... | collective-permute-start | bytes 3080 | tf_op jit(solution)/shard_map/ppermute | solution.py:367
  109.3 5.4 %collective-permute-done.4 = f32[1,256]{1,0:T(1,128)S(1)} collective-permute-done((f32[1,256]{1,0:T(1,128)S(1)}, f32[1,256]{1,0:T(1,128)S(1)}, u32[]{:S(2)}, u32[]{:S(2)}) %collective-permute-start.4) | collective-permute-done | bytes 1056 | tf_op jit(solution)/shard_map/ppermute | solution.py:367
  114.6 0.6 broadcast_in_dim.9
  115.2 22.4 %all-to-all-start.3 = ((f32[16,1,256]{2,1,0:T(1,128)}), f32[16,1,256]{2,1,0:T(1,128)S(1)}, u32[]{:S(2)}, u32[]{:S(2)}) async-start(f32[16,1,256]{2,1,0:T(1,128)} %broadcast_in_dim.9), calls=%async_computation.3 | async-start | bytes 32768 | tf_op jit(solution)/shard_map/all_to_all | solution.py:371
  137.7 0.0 collective-permute-done.3.got_ref
  137.7 0.0 copy-done.3
  137.7 0.0 copy-done.5
  137.7 0.8 last.1
  138.5 6.5 %all-to-all-done.3 = f32[16,1,256]{2,1,0:T(1,128)S(1)} async-done(((f32[16,1,256]{2,1,0:T(1,128)}), f32[16,1,256]{2,1,0:T(1,128)S(1)}, u32[]{:S(2)}, u32[]{:S(2)}) %all-to-all-start.3) | async-done | bytes 16416 | tf_op jit(solution)/shard_map/all_to_all | solution.py:371
  145.0 0.0 copy-done.7
  145.0 0.6 multiply_add_fusion
  (2 shorter events, 0.0 us)
Async XLA Ops:
  6.5 6.8 %copy-start = (bf16[128,8192]{1,0:T(8,128)(2,1)S(1)}, bf16[128,8192]{1,0:T(8,128)(2,1)}, u32[]{:S(2)}) copy-start(bf16[128,8192]{1,0:T(8,128)(2,1)} %h_ref.3) | copy-start | bytes 6291460
  6.6 6.8 %copy-start.2 = (bf16[128,256]{1,0:T(8,128)(2,1)S(1)}, bf16[128,256]{1,0:T(8,128)(2,1)}, u32[]{:S(2)}) copy-start(bf16[128,256]{1,0:T(8,128)(2,1)} %q_ref.5) | copy-start | bytes 196612
  6.6 6.8 %copy-start.6 = (bf16[8192]{0:T(1024)(128)(2,1)S(1)}, bf16[8192]{0:T(1024)(128)(2,1)}, u32[]{:S(2)}) copy-start(bf16[8192]{0:T(1024)(128)(2,1)} %param.7) | copy-start | bytes 49156
  6.6 45.4 %all-to-all-start = ((bf16[8,520,256]{2,1,0:T(8,128)(2,1)}), bf16[8,520,256]{2,1,0:T(8,128)(2,1)}, u32[]{:S(2)}, u32[]{:S(2)}) async-start(bf16[8,520,256]{2,1,0:T(8,128)(2,1)} %partial.1), calls=%async_computation | async-start | bytes 4259840 | tf_op jit(solution)/shard_map/all_to_all | solution.py:371
  14.4 16.1 %collective-permute-start = (bf16[128,4352]{1,0:T(8,128)(2,1)S(1)}, bf16[128,4352]{1,0:T(8,128)(2,1)S(1)}, u32[]{:S(2)}, u32[]{:S(2)}) collective-permute-start(bf16[128,4352]{1,0:T(8,128)(2,1)S(1)} %get-tuple-element.16), channel_id=1, source_target_pairs={{0,32},{32,0},{1,33},{33,1},{2,34},{34,2},{3,35},{35,3},{4,36},{36... | collective-permute-start | bytes 3342344 | tf_op jit(solution)/shard_map/ppermute | solution.py:367
  32.6 15.0 %collective-permute-start.1 = (bf16[128,2048]{1,0:T(8,128)(2,1)S(1)}, bf16[128,2048]{1,0:T(8,128)(2,1)S(1)}, u32[]{:S(2)}, u32[]{:S(2)}) collective-permute-start(bf16[128,2048]{1,0:T(8,128)(2,1)S(1)} %get-tuple-element.18), channel_id=1, source_target_pairs={{0,128},{128,0},{256,384},{384,256},{512,640},{640,512},{768,896},... | collective-permute-start | bytes 1572872 | tf_op jit(solution)/shard_map/ppermute | solution.py:367
  34.5 16.2 %collective-permute-start.2 = (bf16[128,2048]{1,0:T(8,128)(2,1)S(1)}, bf16[128,2048]{1,0:T(8,128)(2,1)S(1)}, u32[]{:S(2)}, u32[]{:S(2)}) collective-permute-start(bf16[128,2048]{1,0:T(8,128)(2,1)S(1)} %get-tuple-element.19), channel_id=1, source_target_pairs={{0,896},{128,256},{256,128},{384,512},{512,384},{640,768},{768,640... | collective-permute-start | bytes 1572872 | tf_op jit(solution)/shard_map/ppermute | solution.py:367
  52.0 29.4 %all-to-all-start.2 = ((bf16[4,256,512]{2,1,0:T(8,128)(2,1)}), bf16[4,256,512]{2,1,0:T(8,128)(2,1)S(1)}, u32[]{:S(2)}, u32[]{:S(2)}) async-start(bf16[4,256,512]{2,1,0:T(8,128)(2,1)} %sum_y.1), calls=%async_computation.2 | async-start | bytes 2097152 | tf_op jit(solution)/shard_map/all_to_all | solution.py:371
  57.4 0.7 copy-start.1
  81.4 19.3 %all-to-all-start.1 = ((bf16[4,136,256]{2,1,0:T(8,128)(2,1)}), bf16[4,136,256]{2,1,0:T(8,128)(2,1)S(1)}, u32[]{:S(2)}, u32[]{:S(2)}) async-start(bf16[4,136,256]{2,1,0:T(8,128)(2,1)} %copy-done.1), calls=%async_computation.1 | async-start | bytes 557056 | tf_op jit(solution)/shard_map/all_to_all | solution.py:371
  87.5 57.5 %copy-start.7 = (f32[256]{0:T(256)S(1)}, f32[256]{0:T(256)}, u32[]{:S(2)}) copy-start(f32[256]{0:T(256)} %param.11) | copy-start | bytes 3076
  88.2 0.7 copy-start.4
  88.9 48.7 %copy-start.3 = (f32[256,256]{1,0:T(8,128)S(1)}, f32[256,256]{1,0:T(8,128)}, u32[]{:S(2)}) copy-start(f32[256,256]{1,0:T(8,128)} %main_ref.1) | copy-start | bytes 786436
  88.9 48.7 %copy-start.5 = (f32[256,256]{1,0:T(8,128)S(1)}, f32[256,256]{1,0:T(8,128)}, u32[]{:S(2)}) copy-start(f32[256,256]{1,0:T(8,128)} %copy-done.4) | copy-start | bytes 786436
  89.0 48.7 %collective-permute-start.3 = (bf16[256,256]{1,0:T(8,128)(2,1)}, bf16[256,256]{1,0:T(8,128)(2,1)S(1)}, u32[]{:S(2)}, u32[]{:S(2)}) collective-permute-start(bf16[256,256]{1,0:T(8,128)(2,1)} %get-tuple-element.21), channel_id=1, source_target_pairs={{0,64},{64,0},{1,65},{65,1},{2,66},{66,2},{3,67},{67,3},{4,68},{68... | collective-permute-start | bytes 393224 | tf_op jit(solution)/shard_map/ppermute | solution.py:367
  101.5 13.1 %collective-permute-start.4 = (f32[1,256]{1,0:T(1,128)S(1)}, f32[1,256]{1,0:T(1,128)S(1)}, u32[]{:S(2)}, u32[]{:S(2)}) collective-permute-start(f32[1,256]{1,0:T(1,128)S(1)} %get-tuple-element.22), channel_id=1, source_target_pairs={{0,64},{64,0},{1,65},{65,1},{2,66},{66,2},{3,67},{67,3},{4,68},{68... | collective-permute-start | bytes 3080 | tf_op jit(solution)/shard_map/ppermute | solution.py:367
  115.2 29.8 %all-to-all-start.3 = ((f32[16,1,256]{2,1,0:T(1,128)}), f32[16,1,256]{2,1,0:T(1,128)S(1)}, u32[]{:S(2)}, u32[]{:S(2)}) async-start(f32[16,1,256]{2,1,0:T(1,128)} %broadcast_in_dim.9), calls=%async_computation.3 | async-start | bytes 32768 | tf_op jit(solution)/shard_map/all_to_all | solution.py:371

commit v6 on v2

--- a/solution.py
+++ b/solution.py
@@ -77,7 +77,7 @@
             jax.ShapeDtypeStruct((TOK, 1), F32),
         ),
         (hidden, gain, q_grad),
-        None,
+        16,
         6 * TOK * D,
         4 * TOK * D,
         grid=(TOK // ROWS,),
@@ -264,9 +264,7 @@
     rinv = rinv_ref[...]
     stat = jnp.sum(jnp.where(eye(), stat, 0.0), axis=1, keepdims=True) * rinv / D
     xhat = h_ref[:, aligned(own * B, B)].astype(F32) * rinv
-    total = jnp.sum(grad * xhat, axis=0, keepdims=True)
-    for i in range(NY * NH * NC):
-        gain_ref[i] = total
+    gain_ref[...] = jnp.sum(grad * xhat, axis=0, keepdims=True)
     out_ref[...] = (rinv * (grad * two_rows(g32, own) - xhat * stat)).astype(BF)
 
 
@@ -275,7 +273,7 @@
         finish_kernel,
         (
             jax.ShapeDtypeStruct((TOK, B), BF),
-            jax.ShapeDtypeStruct((NY * NH * NC, 1, B), F32),
+            jax.ShapeDtypeStruct((1, B), F32),
         ),
         (keep, got, hidden, gain, rinv),
         10,
@@ -335,8 +333,10 @@
 
 
 def sum_y_kernel(keep_ref, left_ref, right_ref, out_ref):
-    out_ref[0, :128, :] = (keep_ref[:128, :].astype(F32) + left_ref[...].astype(F32)).astype(BF)
-    out_ref[0, 128:, :] = (keep_ref[128:, :].astype(F32) + right_ref[...].astype(F32)).astype(BF)
+    for k in range(4):
+        at = slice(k * 512, (k + 1) * 512)
+        out_ref[k, :128, :] = (keep_ref[:128, at].astype(F32) + left_ref[:, at].astype(F32)).astype(BF)
+        out_ref[k, 128:, :] = (keep_ref[128:, at].astype(F32) + right_ref[:, at].astype(F32)).astype(BF)
 
 
 def sum_y(keep, left, right):
@@ -347,13 +347,8 @@
         8,
         TOK * D,
         3 * MB,
-        grid=(4,),
-        in_specs=[
-            pl.BlockSpec((B, 512), lambda k: (0, k)),
-            pl.BlockSpec((128, 512), lambda k: (0, k)),
-            pl.BlockSpec((128, 512), lambda k: (0, k)),
-        ],
-        out_specs=pl.BlockSpec((1, B, 512), lambda k: (k, 0, 0)),
+        in_specs=[VM] * 3,
+        out_specs=VM,
         name="sum_y",
     )
 
@@ -405,6 +400,26 @@
     )
 
 
+def gain_mix_kernel(own_ref, got_ref, out_ref):
+    total = own_ref[...] + got_ref[...]
+    for i in range(NY * NC):
+        out_ref[i] = total
+
+
+def gain_mix(own, got):
+    return call(
+        gain_mix_kernel,
+        jax.ShapeDtypeStruct((NY * NC, 1, B), F32),
+        (own, got),
+        4,
+        B,
+        MB // 16,
+        in_specs=[VM] * 2,
+        out_specs=VM,
+        name="gain_mix",
+    )
+
+
 def pairs(n, f):
     return [(i, f(i) % n) for i in range(n)]
 
@@ -437,11 +452,12 @@
 
     send3, keep3 = sum_z(keep2, got2, 2, 4)
     got3 = swap(send3, "zl", NZ, lambda i: i ^ 4)
-    grad, all_gain = finish(keep3, got3, hidden, gain2, rinv)
-    all_gain = exchange(all_gain, ("y", "zh", "c"))
+    grad, own_gain = finish(keep3, got3, hidden, gain2, rinv)
+    got_gain = swap(own_gain, "zh", NH, lambda i: i ^ 1)
 
     send_h, keep_h = sum_y4(four)
     got_h = swap(send_h, "zh", NH, lambda i: i ^ 1)
+    all_gain = exchange(gain_mix(own_gain, got_gain), ("y", "c"))
     q_new = last(q_main, keep_h, got_h)
     gain_new = gain_main + jnp.sum(all_gain, axis=(0, 1)) / (NY * NH * NC)
     return grad, q_new, gain_new

time: 129 us -> 144 us (1.12)
  waiting for transfers between devices: 47.8 us -> 69.2 us
  local copies, waits for them, and re-layouts: 7.31 us -> 0.04 us
    ppermute x6 -> x7, waiting for transfers between devices: 21.9 us -> 41.3 us  [swap(): return lax.ppermute(v, axis, pairs(n, f))]
    unnamed x26 -> x14, local copies, waits for them, and re-layouts: 7.31 us -> 0.04 us
    ppermute x6 -> x7, starting transfers between devices: 35.9 us -> 39.1 us  [swap(): return lax.ppermute(v, axis, pairs(n, f))]
    all_to_all x3, starting transfers between devices: 19.1 us -> 16.7 us  [exchange(): return lax.all_to_all(v, axis, 0, 0, tiled=True, **kw)]
    all_to_all x3, waiting for transfers between devices: 25.9 us -> 27.9 us  [exchange(): return lax.all_to_all(v, axis, 0, 0, tiled=True, **kw)]
    pallas_call x9 -> x10, Pallas kernels: 16.4 us -> 16.6 us  [call(): pl.pallas_call(kernel, out_shape=out_shape, compiler_params=params(mib),...]
  transfers between devices with their start and end apart: 9 -> 10, of which waited for: 6 -> 7; matrix products, arithmetic and copies ran while one was open for 0% -> 0% of each run, Pallas kernels for 8% -> 8%
where the time goes in v6:
time: 144 us; the launch traced here: 143 us
  waiting for transfers between devices  69.2 us (48%)
  starting transfers between devices  55.8 us (39%)
  Pallas kernels  16.6 us (12%)
    ppermute x7, waiting for transfers between devices, swap(): return lax.ppermute(v, axis, pairs(n, f))  41.3 us
    ppermute x7, starting transfers between devices, swap(): return lax.ppermute(v, axis, pairs(n, f))  39.1 us
    all_to_all x3, waiting for transfers between devices, exchange(): return lax.all_to_all(v, axis, 0, 0, tiled=True, **kw)  27.9 us
    all_to_all x3, starting transfers between devices, exchange(): return lax.all_to_all(v, axis, 0, 0, tiled=True, **kw)  16.7 us
    pallas_call x10, Pallas kernels, call(): pl.pallas_call(kernel, out_shape=out_shape, compiler_params=params(mib),...  16.6 us
  transfers between devices with their start and end apart: 10, of which 7 were waited for; matrix products, arithmetic and copies ran while one was open for 0% of the time, Pallas kernels for 8%

profile of v6, /device:TPU:1, one launch (start us, length us, event | category | flops | bytes accessed | tf_op | source)
XLA Modules:
  0.0 143.0 jit_solution(2293406784229474355)
XLA Ops:
  0.6 5.9 %partial.1 = bf16[8,520,256]{2,1,0:T(8,128)(2,1)} custom-call(bf16[128,256]{1,0:T(8,128)(2,1)} %q_ref.5, bf16[64,128]{1,0:T(8,128)(2,1)} %bitcast.1, bf16[8192,256]{1,0:T(8,128)(2,1)} %w_hbm.1, bf16[128,8192]{1,0:T(8,128)(2,1)} %h_ref.3), custom_call_target="tpu_custom_call" | custom-call | flops 536870912 | bytes 8388608 | tf_op jit(solution)/shard_map/partial/pallas_call | solution.py:30
  6.5 0.0 copy-start
  6.6 0.0 copy-start.1
  6.6 0.0 copy-start.5
  6.6 6.8 %all-to-all-start = ((bf16[8,520,256]{2,1,0:T(8,128)(2,1)}), bf16[8,520,256]{2,1,0:T(8,128)(2,1)}, u32[]{:S(2)}, u32[]{:S(2)}) async-start(bf16[8,520,256]{2,1,0:T(8,128)(2,1)} %partial.1), calls=%async_computation | async-start | bytes 4259840 | tf_op jit(solution)/shard_map/all_to_all | solution.py:432
  13.4 0.0 copy-done
  13.4 0.0 copy-done.1
  13.4 0.0 copy-done.5
  13.4 1.0 norm.1
  14.4 13.7 %collective-permute-start.2 = (bf16[128,4352]{1,0:T(8,128)(2,1)S(1)}, bf16[128,4352]{1,0:T(8,128)(2,1)S(1)}, u32[]{:S(2)}, u32[]{:S(2)}) collective-permute-start(bf16[128,4352]{1,0:T(8,128)(2,1)S(1)} %get-tuple-element.24), channel_id=1, source_target_pairs={{0,32},{32,0},{1,33},{33,1},{2,34},{34,2},{3,35},{35,3},{4,36},{36... | collective-permute-start | bytes 3342344 | tf_op jit(solution)/shard_map/ppermute | solution.py:428
  28.2 2.4 %collective-permute-done.2.got_ref.gq_ref = bf16[128,4352]{1,0:T(8,128)(2,1)S(1)} collective-permute-done((bf16[128,4352]{1,0:T(8,128)(2,1)S(1)}, bf16[128,4352]{1,0:T(8,128)(2,1)S(1)}, u32[]{:S(2)}, u32[]{:S(2)}) %collective-permute-start.2) | collective-permute-done | bytes 1114144 | tf_op jit(solution)/shard_map/ppermute | solution.py:428
  30.5 2.1 %product.1 = (bf16[128,2048]{1,0:T(8,128)(2,1)S(1)}, bf16[128,2048]{1,0:T(8,128)(2,1)S(1)}, bf16[256,2048]{1,0:T(8,128)(2,1)S(1)}) custom-call(bf16[128,4096]{1,0:T(8,128)(2,1)S(1)} %get-tuple-element.23.own_ref, bf16[128,4352]{1,0:T(8,128)(2,1)S(1)} %collective-permute-done.2.got_ref.gq_ref, bf16[128,256]{1,0:T(8,128)(2,1)S(1)} %copy-done.1, ...), custom_call_target="tpu_custom_call" | custom-call | flops 536870912 | bytes 4194304 | tf_op jit(solution)/shard_map/product/pallas_call | solution.py:30
  32.6 1.9 %collective-permute-start.3 = (bf16[128,2048]{1,0:T(8,128)(2,1)S(1)}, bf16[128,2048]{1,0:T(8,128)(2,1)S(1)}, u32[]{:S(2)}, u32[]{:S(2)}) collective-permute-start(bf16[128,2048]{1,0:T(8,128)(2,1)S(1)} %get-tuple-element.26), channel_id=1, source_target_pairs={{0,128},{128,0},{256,384},{384,256},{512,640},{640,512},{768,896},... | collective-permute-start | bytes 1572872 | tf_op jit(solution)/shard_map/ppermute | solution.py:428
  34.5 1.9 %collective-permute-start.4 = (bf16[128,2048]{1,0:T(8,128)(2,1)S(1)}, bf16[128,2048]{1,0:T(8,128)(2,1)S(1)}, u32[]{:S(2)}, u32[]{:S(2)}) collective-permute-start(bf16[128,2048]{1,0:T(8,128)(2,1)S(1)} %get-tuple-element.27), channel_id=1, source_target_pairs={{0,896},{128,256},{256,128},{384,512},{512,384},{640,768},{768,640... | collective-permute-start | bytes 1572872 | tf_op jit(solution)/shard_map/ppermute | solution.py:428
  36.5 11.1 %collective-permute-done.3.left_ref = bf16[128,2048]{1,0:T(8,128)(2,1)S(1)} collective-permute-done((bf16[128,2048]{1,0:T(8,128)(2,1)S(1)}, bf16[128,2048]{1,0:T(8,128)(2,1)S(1)}, u32[]{:S(2)}, u32[]{:S(2)}) %collective-permute-start.3) | collective-permute-done | bytes 524320 | tf_op jit(solution)/shard_map/ppermute | solution.py:428
  47.6 3.1 %collective-permute-done.4.right_ref = bf16[128,2048]{1,0:T(8,128)(2,1)S(1)} collective-permute-done((bf16[128,2048]{1,0:T(8,128)(2,1)S(1)}, bf16[128,2048]{1,0:T(8,128)(2,1)S(1)}, u32[]{:S(2)}, u32[]{:S(2)}) %collective-permute-start.4) | collective-permute-done | bytes 524320 | tf_op jit(solution)/shard_map/ppermute | solution.py:428
  50.8 1.2 sum_y.1
  52.0 0.0 all-to-all-done.in_ref
  52.0 3.5 %all-to-all-start.1 = ((bf16[4,256,512]{2,1,0:T(8,128)(2,1)}), bf16[4,256,512]{2,1,0:T(8,128)(2,1)S(1)}, u32[]{:S(2)}, u32[]{:S(2)}) async-start(bf16[4,256,512]{2,1,0:T(8,128)(2,1)} %sum_y.1), calls=%async_computation.1 | async-start | bytes 2097152 | tf_op jit(solution)/shard_map/all_to_all | solution.py:432
  55.5 2.5 %sum_xz.1 = (bf16[264,256]{1,0:T(8,128)(2,1)}, f32[264,256]{1,0:T(8,128)S(1)}) custom-call(bf16[8,520,256]{2,1,0:T(8,128)(2,1)} %all-to-all-done.in_ref), custom_call_target="tpu_custom_call" | custom-call | flops 1048576 | bytes 4194304 | tf_op jit(solution)/shard_map/sum_xz/pallas_call | solution.py:30
  58.0 1.9 %collective-permute-start = (bf16[264,256]{1,0:T(8,128)(2,1)}, bf16[264,256]{1,0:T(8,128)(2,1)}, u32[]{:S(2)}, u32[]{:S(2)}) collective-permute-start(bf16[264,256]{1,0:T(8,128)(2,1)} %get-tuple-element.18), channel_id=1, source_target_pairs={{0,8},{4,12},{8,0},{12,4},{16,24},{20,28},{24,16},{28,20},{1,9},{5... | collective-permute-start | bytes 405512 | tf_op jit(solution)/shard_map/ppermute | solution.py:428
  59.9 21.4 %all-to-all-done.1.in_ref = bf16[4,256,512]{2,1,0:T(8,128)(2,1)S(1)} async-done(((bf16[4,256,512]{2,1,0:T(8,128)(2,1)}), bf16[4,256,512]{2,1,0:T(8,128)(2,1)S(1)}, u32[]{:S(2)}, u32[]{:S(2)}) %all-to-all-start.1) | async-done | bytes 1048608 | tf_op jit(solution)/shard_map/all_to_all | solution.py:432
  81.3 0.7 sum_y4.1
  82.1 0.0 copy-start.3
  82.1 0.0 copy-start.2
  82.1 0.0 copy-start.6
  82.1 10.9 %collective-permute-start.5 = (bf16[256,256]{1,0:T(8,128)(2,1)}, bf16[256,256]{1,0:T(8,128)(2,1)S(1)}, u32[]{:S(2)}, u32[]{:S(2)}) collective-permute-start(bf16[256,256]{1,0:T(8,128)(2,1)} %get-tuple-element.29), channel_id=1, source_target_pairs={{0,64},{64,0},{1,65},{65,1},{2,66},{66,2},{3,67},{67,3},{4,68},{68... | collective-permute-start | bytes 393224 | tf_op jit(solution)/shard_map/ppermute | solution.py:428
  93.0 0.0 collective-permute-done.got_ref
  93.0 0.9 sum_z4.1
  93.9 0.0 copy-done.3
  93.9 0.0 copy-start.4
  93.9 6.0 %collective-permute-start.1 = (bf16[136,256]{1,0:T(8,128)(2,1)S(1)}, bf16[136,256]{1,0:T(8,128)(2,1)S(1)}, u32[]{:S(2)}, u32[]{:S(2)}) collective-permute-start(bf16[136,256]{1,0:T(8,128)(2,1)S(1)} %get-tuple-element.20), channel_id=1, source_target_pairs={{0,16},{4,20},{8,24},{12,28},{16,0},{20,4},{24,8},{28,12},{1,17},{... | collective-permute-start | bytes 208904 | tf_op jit(solution)/shard_map/ppermute | solution.py:428
  99.9 14.4 %collective-permute-done.1.got_ref = bf16[136,256]{1,0:T(8,128)(2,1)S(1)} collective-permute-done((bf16[136,256]{1,0:T(8,128)(2,1)S(1)}, bf16[136,256]{1,0:T(8,128)(2,1)S(1)}, u32[]{:S(2)}, u32[]{:S(2)}) %collective-permute-start.1) | collective-permute-done | bytes 69664 | tf_op jit(solution)/shard_map/ppermute | solution.py:428
  114.3 0.8 finish.1
  115.1 2.8 %collective-permute-start.6 = (f32[1,256]{1,0:T(1,128)S(1)}, f32[1,256]{1,0:T(1,128)S(1)}, u32[]{:S(2)}, u32[]{:S(2)}) collective-permute-start(f32[1,256]{1,0:T(1,128)S(1)} %get-tuple-element.30.own_ref), channel_id=1, source_target_pairs={{0,64},{64,0},{1,65},{65,1},{2,66},{66,2},{3,67},{67,3},{4,68},{68... | collective-permute-start | bytes 3080 | tf_op jit(solution)/shard_map/ppermute | solution.py:428
  117.9 10.3 %collective-permute-done.6.got_ref = f32[1,256]{1,0:T(1,128)S(1)} collective-permute-done((f32[1,256]{1,0:T(1,128)S(1)}, f32[1,256]{1,0:T(1,128)S(1)}, u32[]{:S(2)}, u32[]{:S(2)}) %collective-permute-start.6) | collective-permute-done | bytes 1056 | tf_op jit(solution)/shard_map/ppermute | solution.py:428
  128.1 0.6 gain_mix.1
  128.7 6.4 %all-to-all-start.2 = ((f32[16,1,256]{2,1,0:T(1,128)}), f32[16,1,256]{2,1,0:T(1,128)S(1)}, u32[]{:S(2)}, u32[]{:S(2)}) async-start(f32[16,1,256]{2,1,0:T(1,128)} %gain_mix.1), calls=%async_computation.2 | async-start | bytes 32768 | tf_op jit(solution)/shard_map/all_to_all | solution.py:432
  135.1 0.0 collective-permute-done.5.got_ref
  135.1 0.0 copy-done.2
  135.1 0.0 copy-done.4
  135.1 0.9 last.1
  136.0 6.5 %all-to-all-done.2 = f32[16,1,256]{2,1,0:T(1,128)S(1)} async-done(((f32[16,1,256]{2,1,0:T(1,128)}), f32[16,1,256]{2,1,0:T(1,128)S(1)}, u32[]{:S(2)}, u32[]{:S(2)}) %all-to-all-start.2) | async-done | bytes 16416 | tf_op jit(solution)/shard_map/all_to_all | solution.py:432
  142.5 0.0 copy-done.6
  142.5 0.6 multiply_add_fusion
  (1 shorter events, 0.0 us)
Async XLA Ops:
  6.5 6.8 %copy-start = (bf16[128,8192]{1,0:T(8,128)(2,1)S(1)}, bf16[128,8192]{1,0:T(8,128)(2,1)}, u32[]{:S(2)}) copy-start(bf16[128,8192]{1,0:T(8,128)(2,1)} %h_ref.3) | copy-start | bytes 6291460
  6.6 6.8 %copy-start.1 = (bf16[128,256]{1,0:T(8,128)(2,1)S(1)}, bf16[128,256]{1,0:T(8,128)(2,1)}, u32[]{:S(2)}) copy-start(bf16[128,256]{1,0:T(8,128)(2,1)} %q_ref.5) | copy-start | bytes 196612
  6.6 6.8 %copy-start.5 = (bf16[8192]{0:T(1024)(128)(2,1)S(1)}, bf16[8192]{0:T(1024)(128)(2,1)}, u32[]{:S(2)}) copy-start(bf16[8192]{0:T(1024)(128)(2,1)} %param.7) | copy-start | bytes 49156
  6.6 45.4 %all-to-all-start = ((bf16[8,520,256]{2,1,0:T(8,128)(2,1)}), bf16[8,520,256]{2,1,0:T(8,128)(2,1)}, u32[]{:S(2)}, u32[]{:S(2)}) async-start(bf16[8,520,256]{2,1,0:T(8,128)(2,1)} %partial.1), calls=%async_computation | async-start | bytes 4259840 | tf_op jit(solution)/shard_map/all_to_all | solution.py:432
  14.4 16.1 %collective-permute-start.2 = (bf16[128,4352]{1,0:T(8,128)(2,1)S(1)}, bf16[128,4352]{1,0:T(8,128)(2,1)S(1)}, u32[]{:S(2)}, u32[]{:S(2)}) collective-permute-start(bf16[128,4352]{1,0:T(8,128)(2,1)S(1)} %get-tuple-element.24), channel_id=1, source_target_pairs={{0,32},{32,0},{1,33},{33,1},{2,34},{34,2},{3,35},{35,3},{4,36},{36... | collective-permute-start | bytes 3342344 | tf_op jit(solution)/shard_map/ppermute | solution.py:428
  32.6 15.0 %collective-permute-start.3 = (bf16[128,2048]{1,0:T(8,128)(2,1)S(1)}, bf16[128,2048]{1,0:T(8,128)(2,1)S(1)}, u32[]{:S(2)}, u32[]{:S(2)}) collective-permute-start(bf16[128,2048]{1,0:T(8,128)(2,1)S(1)} %get-tuple-element.26), channel_id=1, source_target_pairs={{0,128},{128,0},{256,384},{384,256},{512,640},{640,512},{768,896},... | collective-permute-start | bytes 1572872 | tf_op jit(solution)/shard_map/ppermute | solution.py:428
  34.5 16.2 %collective-permute-start.4 = (bf16[128,2048]{1,0:T(8,128)(2,1)S(1)}, bf16[128,2048]{1,0:T(8,128)(2,1)S(1)}, u32[]{:S(2)}, u32[]{:S(2)}) collective-permute-start(bf16[128,2048]{1,0:T(8,128)(2,1)S(1)} %get-tuple-element.27), channel_id=1, source_target_pairs={{0,896},{128,256},{256,128},{384,512},{512,384},{640,768},{768,640... | collective-permute-start | bytes 1572872 | tf_op jit(solution)/shard_map/ppermute | solution.py:428
  52.0 29.3 %all-to-all-start.1 = ((bf16[4,256,512]{2,1,0:T(8,128)(2,1)}), bf16[4,256,512]{2,1,0:T(8,128)(2,1)S(1)}, u32[]{:S(2)}, u32[]{:S(2)}) async-start(bf16[4,256,512]{2,1,0:T(8,128)(2,1)} %sum_y.1), calls=%async_computation.1 | async-start | bytes 2097152 | tf_op jit(solution)/shard_map/all_to_all | solution.py:432
  58.0 35.0 %collective-permute-start = (bf16[264,256]{1,0:T(8,128)(2,1)}, bf16[264,256]{1,0:T(8,128)(2,1)}, u32[]{:S(2)}, u32[]{:S(2)}) collective-permute-start(bf16[264,256]{1,0:T(8,128)(2,1)} %get-tuple-element.18), channel_id=1, source_target_pairs={{0,8},{4,12},{8,0},{12,4},{16,24},{20,28},{24,16},{28,20},{1,9},{5... | collective-permute-start | bytes 405512 | tf_op jit(solution)/shard_map/ppermute | solution.py:428
  82.1 11.9 %copy-start.3 = (f32[256,256]{1,0:T(8,128)}, f32[256,256]{1,0:T(8,128)S(1)}, u32[]{:S(2)}) copy-start(f32[256,256]{1,0:T(8,128)S(1)} %get-tuple-element.28.keep_ref) | copy-start | bytes 786436
  82.1 53.0 %copy-start.2 = (f32[256,256]{1,0:T(8,128)S(1)}, f32[256,256]{1,0:T(8,128)}, u32[]{:S(2)}) copy-start(f32[256,256]{1,0:T(8,128)} %main_ref.1) | copy-start | bytes 786436
  82.1 60.4 %copy-start.6 = (f32[256]{0:T(256)S(1)}, f32[256]{0:T(256)}, u32[]{:S(2)}) copy-start(f32[256]{0:T(256)} %param.11) | copy-start | bytes 3076
  82.1 53.0 %collective-permute-start.5 = (bf16[256,256]{1,0:T(8,128)(2,1)}, bf16[256,256]{1,0:T(8,128)(2,1)S(1)}, u32[]{:S(2)}, u32[]{:S(2)}) collective-permute-start(bf16[256,256]{1,0:T(8,128)(2,1)} %get-tuple-element.29), channel_id=1, source_target_pairs={{0,64},{64,0},{1,65},{65,1},{2,66},{66,2},{3,67},{67,3},{4,68},{68... | collective-permute-start | bytes 393224 | tf_op jit(solution)/shard_map/ppermute | solution.py:428
  93.9 41.2 %copy-start.4 = (f32[256,256]{1,0:T(8,128)S(1)}, f32[256,256]{1,0:T(8,128)}, u32[]{:S(2)}) copy-start(f32[256,256]{1,0:T(8,128)} %copy-done.3) | copy-start | bytes 786436
  93.9 20.3 %collective-permute-start.1 = (bf16[136,256]{1,0:T(8,128)(2,1)S(1)}, bf16[136,256]{1,0:T(8,128)(2,1)S(1)}, u32[]{:S(2)}, u32[]{:S(2)}) collective-permute-start(bf16[136,256]{1,0:T(8,128)(2,1)S(1)} %get-tuple-element.20), channel_id=1, source_target_pairs={{0,16},{4,20},{8,24},{12,28},{16,0},{20,4},{24,8},{28,12},{1,17},{... | collective-permute-start | bytes 208904 | tf_op jit(solution)/shard_map/ppermute | solution.py:428
  115.1 13.0 %collective-permute-start.6 = (f32[1,256]{1,0:T(1,128)S(1)}, f32[1,256]{1,0:T(1,128)S(1)}, u32[]{:S(2)}, u32[]{:S(2)}) collective-permute-start(f32[1,256]{1,0:T(1,128)S(1)} %get-tuple-element.30.own_ref), channel_id=1, source_target_pairs={{0,64},{64,0},{1,65},{65,1},{2,66},{66,2},{3,67},{67,3},{4,68},{68... | collective-permute-start | bytes 3080 | tf_op jit(solution)/shard_map/ppermute | solution.py:428
  128.7 13.7 %all-to-all-start.2 = ((f32[16,1,256]{2,1,0:T(1,128)}), f32[16,1,256]{2,1,0:T(1,128)S(1)}, u32[]{:S(2)}, u32[]{:S(2)}) async-start(f32[16,1,256]{2,1,0:T(1,128)} %gain_mix.1), calls=%async_computation.2 | async-start | bytes 32768 | tf_op jit(solution)/shard_map/all_to_all | solution.py:432

commit v7 on v6

--- a/solution.py
+++ b/solution.py
@@ -77,7 +77,7 @@
             jax.ShapeDtypeStruct((TOK, 1), F32),
         ),
         (hidden, gain, q_grad),
-        16,
+        56,
         6 * TOK * D,
         4 * TOK * D,
         grid=(TOK // ROWS,),
@@ -286,49 +286,44 @@
     )
 
 
-STEPS = 4
-
-
-def product_kernel(own_ref, got_ref, q_ref, gq_ref, left_ref, right_ref, keep_ref):
-    i = pl.program_id(0)
+STEPS = 2
+
+
+def product_of(own_ref, got_ref, q_ref, gq_ref):
     a = jnp.concatenate([own_ref[...], got_ref[...]], axis=0)
     q = jnp.concatenate([q_ref[...], gq_ref[...]], axis=0)
-    p = lax.dot_general(q, a, (((0,), (0,)), ((), ())), preferred_element_type=F32).astype(BF)
-
-    @pl.when(i < STEPS // 2)
-    def _():
-        left_ref[...] = p[:128, :]
-        right_ref[...] = p[128:, :]
-
-    @pl.when(i >= STEPS // 2)
-    def _():
-        keep_ref[...] = p
-
-
-def product(own, got, q_grad):
-    w = 16 * B // STEPS
-    half = jax.ShapeDtypeStruct((128, 8 * B), BF)
-    first = lambda i: (0, jnp.minimum(i, STEPS // 2 - 1))
-    return call(
-        product_kernel,
-        (half, half, jax.ShapeDtypeStruct((B, 8 * B), BF)),
+    return lax.dot_general(q, a, (((0,), (0,)), ((), ())), preferred_element_type=F32).astype(BF)
+
+
+def sent_kernel(own_ref, got_ref, q_ref, gq_ref, left_ref, right_ref):
+    p = product_of(own_ref, got_ref, q_ref, gq_ref)
+    left_ref[...] = p[:128, :]
+    right_ref[...] = p[128:, :]
+
+
+def kept_kernel(own_ref, got_ref, q_ref, gq_ref, keep_ref):
+    keep_ref[...] = product_of(own_ref, got_ref, q_ref, gq_ref)
+
+
+def product(kernel, own, got, q_grad, first, rows, name):
+    w = 8 * B // STEPS
+    shape = tuple(jax.ShapeDtypeStruct((r, 8 * B), BF) for r in rows)
+    return call(
+        kernel,
+        shape,
         (own, got, q_grad, got),
         16,
-        2 * TOK * D * B,
-        4 * MB,
+        TOK * D * B,
+        2 * MB,
         grid=(STEPS,),
         in_specs=[
-            pl.BlockSpec((TOK, w), lambda i: (0, i)),
-            pl.BlockSpec((TOK, w), lambda i: (0, i)),
+            pl.BlockSpec((TOK, w), lambda i: (0, i + first)),
+            pl.BlockSpec((TOK, w), lambda i: (0, i + first)),
             pl.BlockSpec((TOK, B), lambda i: (0, 0)),
             pl.BlockSpec((TOK, B), lambda i: (0, 16)),
         ],
-        out_specs=(
-            pl.BlockSpec((128, w), first),
-            pl.BlockSpec((128, w), first),
-            pl.BlockSpec((B, w), lambda i: (0, jnp.maximum(i - STEPS // 2, 0))),
-        ),
-        name="product",
+        out_specs=tuple(pl.BlockSpec((r, w), lambda i: (0, i)) for r in rows),
+        name=name,
     )
 
 
@@ -381,21 +376,26 @@
     )
 
 
-def last_kernel(main_ref, keep_ref, got_ref, out_ref):
+def last_kernel(main_ref, keep_ref, got_ref, gain_ref, gain_main_ref, out_ref, gain_out_ref):
+    n = NY * NH * NC
+    total = gain_ref[0]
+    for i in range(1, NY * NC):
+        total = total + gain_ref[i]
+    gain_out_ref[...] = gain_main_ref[...] + total / n
     s = keep_ref[...] + got_ref[...].astype(F32)
-    out_ref[...] = main_ref[...] + s.T / (NY * NH * NC)
-
-
-def last(main, keep, got):
+    out_ref[...] = main_ref[...] + s.T / n
+
+
+def last(main, keep, got, gain, gain_main):
     return call(
         last_kernel,
-        jax.ShapeDtypeStruct((B, B), F32),
-        (main, keep, got),
+        (jax.ShapeDtypeStruct((B, B), F32), jax.ShapeDtypeStruct((1, B), F32)),
+        (main, keep, got, gain, gain_main),
         4,
         B * B * 4,
         MB,
-        in_specs=[VM] * 3,
-        out_specs=VM,
+        in_specs=[VM] * 5,
+        out_specs=(VM, VM),
         name="last",
     )
 
@@ -440,7 +440,8 @@
 
     send, own, rinv = norm(hidden, gain2, q_grad)
     got = swap(send, "c", NC, lambda i: i ^ 1)
-    left, right, keep = product(own, got, q_grad)
+    left, right = product(sent_kernel, own, got, q_grad, 0, (128, 128), "sent")
+    (keep,) = product(kept_kernel, own, got, q_grad, STEPS, (B,), "kept")
     left = swap(left, "y", NY, lambda i: i ^ 1)
     right = swap(right, "y", NY, lambda i: i + 1 if i % 2 else i - 1)
 
@@ -458,8 +459,8 @@
     send_h, keep_h = sum_y4(four)
     got_h = swap(send_h, "zh", NH, lambda i: i ^ 1)
     all_gain = exchange(gain_mix(own_gain, got_gain), ("y", "c"))
-    q_new = last(q_main, keep_h, got_h)
-    gain_new = gain_main + jnp.sum(all_gain, axis=(0, 1)) / (NY * NH * NC)
+    q_new, gain_new = last(q_main, keep_h, got_h, all_gain, gain_main.reshape(1, B))
+    gain_new = gain_new.reshape(B)
     return grad, q_new, gain_new
 
 

time: 144 us -> 147 us (1.021)
  local copies, waits for them, and re-layouts: 0.04 us -> 4.22 us
  waiting for transfers between devices: 69.2 us -> 65.7 us
  starting transfers between devices: 55.8 us -> 58.6 us
    ppermute x7, waiting for transfers between devices: 41.3 us -> 37.1 us  [swap(): return lax.ppermute(v, axis, pairs(n, f))]
    unnamed x14 -> x22, local copies, waits for them, and re-layouts: 0.04 us -> 4.22 us
    ppermute x7, starting transfers between devices: 39.1 us -> 42.2 us  [swap(): return lax.ppermute(v, axis, pairs(n, f))]
    pallas_call x10 -> x11, Pallas kernels: 16.6 us -> 17 us  [call(): pl.pallas_call(kernel, out_shape=out_shape, compiler_params=params(mib),...]
  transfers between devices with their start and end apart: 10 -> 10, of which waited for: 7 -> 7; matrix products, arithmetic and copies ran while one was open for 0% -> 0% of each run, Pallas kernels for 8% -> 7%
where the time goes in v7:
time: 147 us; the launch traced here: 146 us
  waiting for transfers between devices  65.7 us (45%)
  starting transfers between devices  58.6 us (40%)
  Pallas kernels  17 us (12%)
  local copies, waits for them, and re-layouts  4.22 us (3%)
    ppermute x7, starting transfers between devices, swap(): return lax.ppermute(v, axis, pairs(n, f))  42.2 us
    ppermute x7, waiting for transfers between devices, swap(): return lax.ppermute(v, axis, pairs(n, f))  37.1 us
    all_to_all x3, waiting for transfers between devices, exchange(): return lax.all_to_all(v, axis, 0, 0, tiled=True, **kw)  28.7 us
    pallas_call x11, Pallas kernels, call(): pl.pallas_call(kernel, out_shape=out_shape, compiler_params=params(mib),...  17 us
    all_to_all x3, starting transfers between devices, exchange(): return lax.all_to_all(v, axis, 0, 0, tiled=True, **kw)  16.4 us
    unnamed x22, local copies, waits for them, and re-layouts  4.22 us
  transfers between devices with their start and end apart: 10, of which 7 were waited for; matrix products, arithmetic and copies ran while one was open for 0% of the time, Pallas kernels for 7%

profile of v7, /device:TPU:1, one launch (start us, length us, event | category | flops | bytes accessed | tf_op | source)
XLA Modules:
  0.0 146.3 jit_solution(12058088978160088076)
XLA Ops:
  0.6 6.0 %partial.1 = bf16[8,520,256]{2,1,0:T(8,128)(2,1)} custom-call(bf16[128,256]{1,0:T(8,128)(2,1)} %q_ref.7, bf16[64,128]{1,0:T(8,128)(2,1)} %bitcast.3, bf16[8192,256]{1,0:T(8,128)(2,1)} %w_hbm.1, bf16[128,8192]{1,0:T(8,128)(2,1)} %h_ref.3), custom_call_target="tpu_custom_call" | custom-call | flops 536870912 | bytes 8388608 | tf_op jit(solution)/shard_map/partial/pallas_call | solution.py:30
  6.6 6.7 %all-to-all-start = ((bf16[8,520,256]{2,1,0:T(8,128)(2,1)}), bf16[8,520,256]{2,1,0:T(8,128)(2,1)S(1)}, u32[]{:S(2)}, u32[]{:S(2)}) async-start(bf16[8,520,256]{2,1,0:T(8,128)(2,1)} %partial.1), calls=%async_computation | async-start | bytes 4259840 | tf_op jit(solution)/shard_map/all_to_all | solution.py:432
  13.3 0.0 copy-start.4
  13.3 3.3 %norm.1 = (bf16[128,4352]{1,0:T(8,128)(2,1)}, bf16[128,4096]{1,0:T(8,128)(2,1)}, f32[128,1]{1,0:T(8,128)}) custom-call(bf16[128,8192]{1,0:T(8,128)(2,1)} %h_ref.3, bf16[64,128]{1,0:T(8,128)(2,1)} %bitcast.4, bf16[128,256]{1,0:T(8,128)(2,1)} %q_ref.7), custom_call_target="tpu_custom_call" | custom-call | flops 6291456 | bytes 4194304 | tf_op jit(solution)/shard_map/norm/pallas_call | solution.py:30
  16.5 13.0 %collective-permute-start.2 = (bf16[128,4352]{1,0:T(8,128)(2,1)}, bf16[128,4352]{1,0:T(8,128)(2,1)S(1)}, u32[]{:S(2)}, u32[]{:S(2)}) collective-permute-start(bf16[128,4352]{1,0:T(8,128)(2,1)} %get-tuple-element.25), channel_id=1, source_target_pairs={{0,32},{32,0},{1,33},{33,1},{2,34},{34,2},{3,35},{35,3},{4,36},{36... | collective-permute-start | bytes 3342344 | tf_op jit(solution)/shard_map/ppermute | solution.py:428
  29.5 2.6 %collective-permute-done.2.got_ref.gq_ref = bf16[128,4352]{1,0:T(8,128)(2,1)S(1)} collective-permute-done((bf16[128,4352]{1,0:T(8,128)(2,1)}, bf16[128,4352]{1,0:T(8,128)(2,1)S(1)}, u32[]{:S(2)}, u32[]{:S(2)}) %collective-permute-start.2) | collective-permute-done | bytes 1114144 | tf_op jit(solution)/shard_map/ppermute | solution.py:428
  32.1 0.0 copy-done.4
  32.1 0.0 copy-start.3
  32.1 1.2 copy-done.3
  33.3 0.9 sent.1
  34.2 1.9 %collective-permute-start.3 = (bf16[128,2048]{1,0:T(8,128)(2,1)S(1)}, bf16[128,2048]{1,0:T(8,128)(2,1)S(1)}, u32[]{:S(2)}, u32[]{:S(2)}) collective-permute-start(bf16[128,2048]{1,0:T(8,128)(2,1)S(1)} %get-tuple-element.26), channel_id=1, source_target_pairs={{0,128},{128,0},{256,384},{384,256},{512,640},{640,512},{768,896},... | collective-permute-start | bytes 1572872 | tf_op jit(solution)/shard_map/ppermute | solution.py:428
  36.1 1.9 %collective-permute-start.4 = (bf16[128,2048]{1,0:T(8,128)(2,1)S(1)}, bf16[128,2048]{1,0:T(8,128)(2,1)S(1)}, u32[]{:S(2)}, u32[]{:S(2)}) collective-permute-start(bf16[128,2048]{1,0:T(8,128)(2,1)S(1)} %get-tuple-element.27), channel_id=1, source_target_pairs={{0,896},{128,256},{256,128},{384,512},{512,384},{640,768},{768,640... | collective-permute-start | bytes 1572872 | tf_op jit(solution)/shard_map/ppermute | solution.py:428
  38.0 0.9 kept.1.keep_ref
  38.9 10.2 %collective-permute-done.3.left_ref = bf16[128,2048]{1,0:T(8,128)(2,1)S(1)} collective-permute-done((bf16[128,2048]{1,0:T(8,128)(2,1)S(1)}, bf16[128,2048]{1,0:T(8,128)(2,1)S(1)}, u32[]{:S(2)}, u32[]{:S(2)}) %collective-permute-start.3) | collective-permute-done | bytes 524320 | tf_op jit(solution)/shard_map/ppermute | solution.py:428
  49.2 3.1 %collective-permute-done.4.right_ref = bf16[128,2048]{1,0:T(8,128)(2,1)S(1)} collective-permute-done((bf16[128,2048]{1,0:T(8,128)(2,1)S(1)}, bf16[128,2048]{1,0:T(8,128)(2,1)S(1)}, u32[]{:S(2)}, u32[]{:S(2)}) %collective-permute-start.4) | collective-permute-done | bytes 524320 | tf_op jit(solution)/shard_map/ppermute | solution.py:428
  52.3 1.2 sum_y.1
  53.5 0.0 all-to-all-done.in_ref
  53.6 0.0 copy-start.1
  53.6 1.4 copy-done.1
  54.9 3.5 %all-to-all-start.1 = ((bf16[4,256,512]{2,1,0:T(8,128)(2,1)}), bf16[4,256,512]{2,1,0:T(8,128)(2,1)S(1)}, u32[]{:S(2)}, u32[]{:S(2)}) async-start(bf16[4,256,512]{2,1,0:T(8,128)(2,1)} %sum_y.1), calls=%async_computation.1 | async-start | bytes 2097152 | tf_op jit(solution)/shard_map/all_to_all | solution.py:432
  58.4 0.0 copy-start.2
  58.5 1.6 %copy-done.2 = bf16[8,520,256]{2,1,0:T(8,128)(2,1)S(1)} copy-done((bf16[8,520,256]{2,1,0:T(8,128)(2,1)S(1)}, bf16[8,520,256]{2,1,0:T(8,128)(2,1)}, u32[]{:S(2)}) %copy-start.2) | copy-done | bytes 2129944
  60.0 0.0 copy-start
  60.0 0.0 copy-start.8
  60.1 0.0 copy-start.9
  60.1 0.8 sum_xz.1
  60.9 0.0 copy-start.10
  60.9 2.0 %collective-permute-start = (bf16[264,256]{1,0:T(8,128)(2,1)}, bf16[264,256]{1,0:T(8,128)(2,1)}, u32[]{:S(2)}, u32[]{:S(2)}) collective-permute-start(bf16[264,256]{1,0:T(8,128)(2,1)} %get-tuple-element.19), channel_id=1, source_target_pairs={{0,8},{4,12},{8,0},{12,4},{16,24},{20,28},{24,16},{28,20},{1,9},{5... | collective-permute-start | bytes 405512 | tf_op jit(solution)/shard_map/ppermute | solution.py:428
  63.0 21.3 %all-to-all-done.1.in_ref = bf16[4,256,512]{2,1,0:T(8,128)(2,1)S(1)} async-done(((bf16[4,256,512]{2,1,0:T(8,128)(2,1)}), bf16[4,256,512]{2,1,0:T(8,128)(2,1)S(1)}, u32[]{:S(2)}, u32[]{:S(2)}) %all-to-all-start.1) | async-done | bytes 1048608 | tf_op jit(solution)/shard_map/all_to_all | solution.py:432
  84.3 0.7 sum_y4.1
  85.0 0.0 copy-start.6
  85.0 0.0 copy-start.5
  85.0 11.5 %collective-permute-start.5 = (bf16[256,256]{1,0:T(8,128)(2,1)}, bf16[256,256]{1,0:T(8,128)(2,1)S(1)}, u32[]{:S(2)}, u32[]{:S(2)}) collective-permute-start(bf16[256,256]{1,0:T(8,128)(2,1)} %get-tuple-element.29), channel_id=1, source_target_pairs={{0,64},{64,0},{1,65},{65,1},{2,66},{66,2},{3,67},{67,3},{4,68},{68... | collective-permute-start | bytes 393224 | tf_op jit(solution)/shard_map/ppermute | solution.py:428
  96.5 0.0 collective-permute-done.got_ref
  96.5 0.9 sum_z4.1
  97.5 0.0 copy-done.6
  97.5 0.0 copy-start.7
  97.5 6.0 %collective-permute-start.1 = (bf16[136,256]{1,0:T(8,128)(2,1)S(1)}, bf16[136,256]{1,0:T(8,128)(2,1)S(1)}, u32[]{:S(2)}, u32[]{:S(2)}) collective-permute-start(bf16[136,256]{1,0:T(8,128)(2,1)S(1)} %get-tuple-element.21), channel_id=1, source_target_pairs={{0,16},{4,20},{8,24},{12,28},{16,0},{20,4},{24,8},{28,12},{1,17},{... | collective-permute-start | bytes 208904 | tf_op jit(solution)/shard_map/ppermute | solution.py:428
  103.5 14.0 %collective-permute-done.1.got_ref = bf16[136,256]{1,0:T(8,128)(2,1)S(1)} collective-permute-done((bf16[136,256]{1,0:T(8,128)(2,1)S(1)}, bf16[136,256]{1,0:T(8,128)(2,1)S(1)}, u32[]{:S(2)}, u32[]{:S(2)}) %collective-permute-start.1) | collective-permute-done | bytes 69664 | tf_op jit(solution)/shard_map/ppermute | solution.py:428
  117.4 0.0 copy-done
  117.4 0.0 copy-done.8
  117.4 0.0 copy-done.9
  117.4 0.8 finish.1
  118.3 5.9 %collective-permute-start.6 = (f32[1,256]{1,0:T(1,128)S(1)}, f32[1,256]{1,0:T(1,128)S(1)}, u32[]{:S(2)}, u32[]{:S(2)}) collective-permute-start(f32[1,256]{1,0:T(1,128)S(1)} %get-tuple-element.30.own_ref), channel_id=1, source_target_pairs={{0,64},{64,0},{1,65},{65,1},{2,66},{66,2},{3,67},{67,3},{4,68},{68... | collective-permute-start | bytes 3080 | tf_op jit(solution)/shard_map/ppermute | solution.py:428
  124.1 7.2 %collective-permute-done.6.got_ref = f32[1,256]{1,0:T(1,128)S(1)} collective-permute-done((f32[1,256]{1,0:T(1,128)S(1)}, f32[1,256]{1,0:T(1,128)S(1)}, u32[]{:S(2)}, u32[]{:S(2)}) %collective-permute-start.6) | collective-permute-done | bytes 1056 | tf_op jit(solution)/shard_map/ppermute | solution.py:428
  131.3 0.6 gain_mix.1
  131.9 6.2 %all-to-all-start.2 = ((f32[16,1,256]{2,1,0:T(1,128)}), f32[16,1,256]{2,1,0:T(1,128)S(1)}, u32[]{:S(2)}, u32[]{:S(2)}) async-start(f32[16,1,256]{2,1,0:T(1,128)} %gain_mix.1), calls=%async_computation.2 | async-start | bytes 32768 | tf_op jit(solution)/shard_map/all_to_all | solution.py:432
  138.1 0.0 collective-permute-done.5.got_ref
  138.1 7.3 %all-to-all-done.2.gain_ref = f32[16,1,256]{2,1,0:T(1,128)S(1)} async-done(((f32[16,1,256]{2,1,0:T(1,128)}), f32[16,1,256]{2,1,0:T(1,128)S(1)}, u32[]{:S(2)}, u32[]{:S(2)}) %all-to-all-start.2) | async-done | bytes 16416 | tf_op jit(solution)/shard_map/all_to_all | solution.py:432
  145.5 0.0 copy-done.10
  145.5 0.0 copy-done.5
  145.5 0.0 copy-done.7
  145.5 0.9 last.1
Async XLA Ops:
  6.6 47.0 %all-to-all-start = ((bf16[8,520,256]{2,1,0:T(8,128)(2,1)}), bf16[8,520,256]{2,1,0:T(8,128)(2,1)S(1)}, u32[]{:S(2)}, u32[]{:S(2)}) async-start(bf16[8,520,256]{2,1,0:T(8,128)(2,1)} %partial.1), calls=%async_computation | async-start | bytes 4259840 | tf_op jit(solution)/shard_map/all_to_all | solution.py:432
  13.3 18.8 %copy-start.4 = (bf16[128,256]{1,0:T(8,128)(2,1)S(1)}, bf16[128,256]{1,0:T(8,128)(2,1)}, u32[]{:S(2)}) copy-start(bf16[128,256]{1,0:T(8,128)(2,1)} %q_ref.7) | copy-start | bytes 196612
  16.5 15.6 %collective-permute-start.2 = (bf16[128,4352]{1,0:T(8,128)(2,1)}, bf16[128,4352]{1,0:T(8,128)(2,1)S(1)}, u32[]{:S(2)}, u32[]{:S(2)}) collective-permute-start(bf16[128,4352]{1,0:T(8,128)(2,1)} %get-tuple-element.25), channel_id=1, source_target_pairs={{0,32},{32,0},{1,33},{33,1},{2,34},{34,2},{3,35},{35,3},{4,36},{36... | collective-permute-start | bytes 3342344 | tf_op jit(solution)/shard_map/ppermute | solution.py:428
  32.1 1.2 copy-start.3
  34.2 15.0 %collective-permute-start.3 = (bf16[128,2048]{1,0:T(8,128)(2,1)S(1)}, bf16[128,2048]{1,0:T(8,128)(2,1)S(1)}, u32[]{:S(2)}, u32[]{:S(2)}) collective-permute-start(bf16[128,2048]{1,0:T(8,128)(2,1)S(1)} %get-tuple-element.26), channel_id=1, source_target_pairs={{0,128},{128,0},{256,384},{384,256},{512,640},{640,512},{768,896},... | collective-permute-start | bytes 1572872 | tf_op jit(solution)/shard_map/ppermute | solution.py:428
  36.1 16.2 %collective-permute-start.4 = (bf16[128,2048]{1,0:T(8,128)(2,1)S(1)}, bf16[128,2048]{1,0:T(8,128)(2,1)S(1)}, u32[]{:S(2)}, u32[]{:S(2)}) collective-permute-start(bf16[128,2048]{1,0:T(8,128)(2,1)S(1)} %get-tuple-element.27), channel_id=1, source_target_pairs={{0,896},{128,256},{256,128},{384,512},{512,384},{640,768},{768,640... | collective-permute-start | bytes 1572872 | tf_op jit(solution)/shard_map/ppermute | solution.py:428
  53.6 1.4 copy-start.1
  54.9 29.3 %all-to-all-start.1 = ((bf16[4,256,512]{2,1,0:T(8,128)(2,1)}), bf16[4,256,512]{2,1,0:T(8,128)(2,1)S(1)}, u32[]{:S(2)}, u32[]{:S(2)}) async-start(bf16[4,256,512]{2,1,0:T(8,128)(2,1)} %sum_y.1), calls=%async_computation.1 | async-start | bytes 2097152 | tf_op jit(solution)/shard_map/all_to_all | solution.py:432
  58.4 1.6 %copy-start.2 = (bf16[8,520,256]{2,1,0:T(8,128)(2,1)S(1)}, bf16[8,520,256]{2,1,0:T(8,128)(2,1)}, u32[]{:S(2)}) copy-start(bf16[8,520,256]{2,1,0:T(8,128)(2,1)} %copy-done.1) | copy-start | bytes 6389764
  60.0 57.4 %copy-start = (bf16[128,8192]{1,0:T(8,128)(2,1)S(1)}, bf16[128,8192]{1,0:T(8,128)(2,1)}, u32[]{:S(2)}) copy-start(bf16[128,8192]{1,0:T(8,128)(2,1)} %h_ref.3) | copy-start | bytes 6291460
  60.0 57.4 %copy-start.8 = (bf16[8192]{0:T(1024)(128)(2,1)S(1)}, bf16[8192]{0:T(1024)(128)(2,1)}, u32[]{:S(2)}) copy-start(bf16[8192]{0:T(1024)(128)(2,1)} %param.7) | copy-start | bytes 49156
  60.1 57.4 %copy-start.9 = (f32[128,1]{1,0:T(8,128)S(1)}, f32[128,1]{1,0:T(8,128)}, u32[]{:S(2)}) copy-start(f32[128,1]{1,0:T(8,128)} %get-tuple-element.22.rinv_ref) | copy-start | bytes 1540
  60.9 84.6 %copy-start.10 = (f32[256]{0:T(256)S(1)}, f32[256]{0:T(256)}, u32[]{:S(2)}) copy-start(f32[256]{0:T(256)} %param.11) | copy-start | bytes 3076
  60.9 35.6 %collective-permute-start = (bf16[264,256]{1,0:T(8,128)(2,1)}, bf16[264,256]{1,0:T(8,128)(2,1)}, u32[]{:S(2)}, u32[]{:S(2)}) collective-permute-start(bf16[264,256]{1,0:T(8,128)(2,1)} %get-tuple-element.19), channel_id=1, source_target_pairs={{0,8},{4,12},{8,0},{12,4},{16,24},{20,28},{24,16},{28,20},{1,9},{5... | collective-permute-start | bytes 405512 | tf_op jit(solution)/shard_map/ppermute | solution.py:428
  85.0 12.5 %copy-start.6 = (f32[256,256]{1,0:T(8,128)}, f32[256,256]{1,0:T(8,128)S(1)}, u32[]{:S(2)}) copy-start(f32[256,256]{1,0:T(8,128)S(1)} %get-tuple-element.28.keep_ref) | copy-start | bytes 786436
  85.0 60.5 %copy-start.5 = (f32[256,256]{1,0:T(8,128)S(1)}, f32[256,256]{1,0:T(8,128)}, u32[]{:S(2)}) copy-start(f32[256,256]{1,0:T(8,128)} %main_ref.1) | copy-start | bytes 786436
  85.0 53.1 %collective-permute-start.5 = (bf16[256,256]{1,0:T(8,128)(2,1)}, bf16[256,256]{1,0:T(8,128)(2,1)S(1)}, u32[]{:S(2)}, u32[]{:S(2)}) collective-permute-start(bf16[256,256]{1,0:T(8,128)(2,1)} %get-tuple-element.29), channel_id=1, source_target_pairs={{0,64},{64,0},{1,65},{65,1},{2,66},{66,2},{3,67},{67,3},{4,68},{68... | collective-permute-start | bytes 393224 | tf_op jit(solution)/shard_map/ppermute | solution.py:428
  97.5 48.0 %copy-start.7 = (f32[256,256]{1,0:T(8,128)S(1)}, f32[256,256]{1,0:T(8,128)}, u32[]{:S(2)}) copy-start(f32[256,256]{1,0:T(8,128)} %copy-done.6) | copy-start | bytes 786436
  97.5 19.9 %collective-permute-start.1 = (bf16[136,256]{1,0:T(8,128)(2,1)S(1)}, bf16[136,256]{1,0:T(8,128)(2,1)S(1)}, u32[]{:S(2)}, u32[]{:S(2)}) collective-permute-start(bf16[136,256]{1,0:T(8,128)(2,1)S(1)} %get-tuple-element.21), channel_id=1, source_target_pairs={{0,16},{4,20},{8,24},{12,28},{16,0},{20,4},{24,8},{28,12},{1,17},{... | collective-permute-start | bytes 208904 | tf_op jit(solution)/shard_map/ppermute | solution.py:428
  118.3 13.0 %collective-permute-start.6 = (f32[1,256]{1,0:T(1,128)S(1)}, f32[1,256]{1,0:T(1,128)S(1)}, u32[]{:S(2)}, u32[]{:S(2)}) collective-permute-start(f32[1,256]{1,0:T(1,128)S(1)} %get-tuple-element.30.own_ref), channel_id=1, source_target_pairs={{0,64},{64,0},{1,65},{65,1},{2,66},{66,2},{3,67},{67,3},{4,68},{68... | collective-permute-start | bytes 3080 | tf_op jit(solution)/shard_map/ppermute | solution.py:428
  131.9 13.6 %all-to-all-start.2 = ((f32[16,1,256]{2,1,0:T(1,128)}), f32[16,1,256]{2,1,0:T(1,128)S(1)}, u32[]{:S(2)}, u32[]{:S(2)}) async-start(f32[16,1,256]{2,1,0:T(1,128)} %gain_mix.1), calls=%async_computation.2 | async-start | bytes 32768 | tf_op jit(solution)/shard_map/all_to_all | solution.py:432

commit v8 on v6

--- a/solution.py
+++ b/solution.py
@@ -45,7 +45,7 @@
     return jnp.concatenate([at(0), at(1)], axis=1)
 
 
-ROWS = 64
+ROWS = 32
 
 
 def norm_kernel(h_ref, g_ref, q_ref, send_ref, own_ref, rinv_ref, g32):
@@ -77,7 +77,7 @@
             jax.ShapeDtypeStruct((TOK, 1), F32),
         ),
         (hidden, gain, q_grad),
-        16,
+        56,
         6 * TOK * D,
         4 * TOK * D,
         grid=(TOK // ROWS,),
@@ -381,21 +381,26 @@
     )
 
 
-def last_kernel(main_ref, keep_ref, got_ref, out_ref):
+def last_kernel(main_ref, keep_ref, got_ref, gain_ref, gain_main_ref, out_ref, gain_out_ref):
+    n = NY * NH * NC
+    total = gain_ref[0]
+    for i in range(1, NY * NC):
+        total = total + gain_ref[i]
+    gain_out_ref[...] = gain_main_ref[...] + total / n
     s = keep_ref[...] + got_ref[...].astype(F32)
-    out_ref[...] = main_ref[...] + s.T / (NY * NH * NC)
-
-
-def last(main, keep, got):
+    out_ref[...] = main_ref[...] + s.T / n
+
+
+def last(main, keep, got, gain, gain_main):
     return call(
         last_kernel,
-        jax.ShapeDtypeStruct((B, B), F32),
-        (main, keep, got),
+        (jax.ShapeDtypeStruct((B, B), F32), jax.ShapeDtypeStruct((1, B), F32)),
+        (main, keep, got, gain, gain_main),
         4,
         B * B * 4,
         MB,
-        in_specs=[VM] * 3,
-        out_specs=VM,
+        in_specs=[VM] * 5,
+        out_specs=(VM, VM),
         name="last",
     )
 
@@ -458,8 +463,8 @@
     send_h, keep_h = sum_y4(four)
     got_h = swap(send_h, "zh", NH, lambda i: i ^ 1)
     all_gain = exchange(gain_mix(own_gain, got_gain), ("y", "c"))
-    q_new = last(q_main, keep_h, got_h)
-    gain_new = gain_main + jnp.sum(all_gain, axis=(0, 1)) / (NY * NH * NC)
+    q_new, gain_new = last(q_main, keep_h, got_h, all_gain, gain_main.reshape(1, B))
+    gain_new = gain_new.reshape(B)
     return grad, q_new, gain_new
 
 

time: 144 us -> 149 us (1.035)
  local copies, waits for them, and re-layouts: 0.04 us -> 4.22 us
  starting transfers between devices: 55.8 us -> 58.6 us
  waiting for transfers between devices: 69.2 us -> 66.7 us
  Pallas kernels: 16.6 us -> 18.3 us
    unnamed x14 -> x22, local copies, waits for them, and re-layouts: 0.04 us -> 4.22 us
    ppermute x7, waiting for transfers between devices: 41.3 us -> 38 us  [swap(): return lax.ppermute(v, axis, pairs(n, f))]
    ppermute x7, starting transfers between devices: 39.1 us -> 42.2 us  [swap(): return lax.ppermute(v, axis, pairs(n, f))]
    pallas_call x10, Pallas kernels: 16.6 us -> 18.3 us  [call(): pl.pallas_call(kernel, out_shape=out_shape, compiler_params=params(mib),...]
where the time goes in v8:
time: 149 us
  waiting for transfers between devices  66.7 us (45%)
  starting transfers between devices  58.6 us (39%)
  Pallas kernels  18.3 us (12%)
  local copies, waits for them, and re-layouts  4.22 us (3%)
    ppermute x7, starting transfers between devices, swap(): return lax.ppermute(v, axis, pairs(n, f))  42.2 us
    ppermute x7, waiting for transfers between devices, swap(): return lax.ppermute(v, axis, pairs(n, f))  38 us
    all_to_all x3, waiting for transfers between devices, exchange(): return lax.all_to_all(v, axis, 0, 0, tiled=True, **kw)  28.7 us
    pallas_call x10, Pallas kernels, call(): pl.pallas_call(kernel, out_shape=out_shape, compiler_params=params(mib),...  18.3 us
    all_to_all x3, starting transfers between devices, exchange(): return lax.all_to_all(v, axis, 0, 0, tiled=True, **kw)  16.4 us
    unnamed x22, local copies, waits for them, and re-layouts  4.22 us
  transfers between devices with their start and end apart: 10, of which 7 were waited for; matrix products, arithmetic and copies ran while one was open for 0% of the time, Pallas kernels for 8%

profile of v8, /device:TPU:1, one launch (start us, length us, event | category | flops | bytes accessed | tf_op | source)
XLA Modules:
  0.0 148.6 jit_solution(10762502754416145348)
XLA Ops:
  0.6 6.0 %partial.1 = bf16[8,520,256]{2,1,0:T(8,128)(2,1)} custom-call(bf16[128,256]{1,0:T(8,128)(2,1)} %q_ref.5, bf16[64,128]{1,0:T(8,128)(2,1)} %bitcast.3, bf16[8192,256]{1,0:T(8,128)(2,1)} %w_hbm.1, bf16[128,8192]{1,0:T(8,128)(2,1)} %h_ref.3), custom_call_target="tpu_custom_call" | custom-call | flops 536870912 | bytes 8388608 | tf_op jit(solution)/shard_map/partial/pallas_call | solution.py:30
  6.6 6.7 %all-to-all-start = ((bf16[8,520,256]{2,1,0:T(8,128)(2,1)}), bf16[8,520,256]{2,1,0:T(8,128)(2,1)S(1)}, u32[]{:S(2)}, u32[]{:S(2)}) async-start(bf16[8,520,256]{2,1,0:T(8,128)(2,1)} %partial.1), calls=%async_computation | async-start | bytes 4259840 | tf_op jit(solution)/shard_map/all_to_all | solution.py:437
  13.3 0.0 copy-start.4
  13.3 4.2 %norm.1 = (bf16[128,4352]{1,0:T(8,128)(2,1)}, bf16[128,4096]{1,0:T(8,128)(2,1)}, f32[128,1]{1,0:T(8,128)}) custom-call(bf16[128,8192]{1,0:T(8,128)(2,1)} %h_ref.3, bf16[64,128]{1,0:T(8,128)(2,1)} %bitcast.4, bf16[128,256]{1,0:T(8,128)(2,1)} %q_ref.5), custom_call_target="tpu_custom_call" | custom-call | flops 6291456 | bytes 4194304 | tf_op jit(solution)/shard_map/norm/pallas_call | solution.py:30
  17.5 13.0 %collective-permute-start.2 = (bf16[128,4352]{1,0:T(8,128)(2,1)}, bf16[128,4352]{1,0:T(8,128)(2,1)S(1)}, u32[]{:S(2)}, u32[]{:S(2)}) collective-permute-start(bf16[128,4352]{1,0:T(8,128)(2,1)} %get-tuple-element.26), channel_id=1, source_target_pairs={{0,32},{32,0},{1,33},{33,1},{2,34},{34,2},{3,35},{35,3},{4,36},{36... | collective-permute-start | bytes 3342344 | tf_op jit(solution)/shard_map/ppermute | solution.py:433
  30.5 2.6 %collective-permute-done.2.got_ref.gq_ref = bf16[128,4352]{1,0:T(8,128)(2,1)S(1)} collective-permute-done((bf16[128,4352]{1,0:T(8,128)(2,1)}, bf16[128,4352]{1,0:T(8,128)(2,1)S(1)}, u32[]{:S(2)}, u32[]{:S(2)}) %collective-permute-start.2) | collective-permute-done | bytes 1114144 | tf_op jit(solution)/shard_map/ppermute | solution.py:433
  33.1 0.0 copy-done.4
  33.1 0.0 copy-start.3
  33.1 1.2 copy-done.3
  34.3 2.1 %product.1 = (bf16[128,2048]{1,0:T(8,128)(2,1)S(1)}, bf16[128,2048]{1,0:T(8,128)(2,1)S(1)}, bf16[256,2048]{1,0:T(8,128)(2,1)S(1)}) custom-call(bf16[128,4096]{1,0:T(8,128)(2,1)S(1)} %copy-done.3, bf16[128,4352]{1,0:T(8,128)(2,1)S(1)} %collective-permute-done.2.got_ref.gq_ref, bf16[128,256]{1,0:T(8,128)(2,1)S(1)} %copy-done.4, ...), custom_call_target="tpu_custom_call" | custom-call | flops 536870912 | bytes 4194304 | tf_op jit(solution)/shard_map/product/pallas_call | solution.py:30
  36.4 1.9 %collective-permute-start.3 = (bf16[128,2048]{1,0:T(8,128)(2,1)S(1)}, bf16[128,2048]{1,0:T(8,128)(2,1)S(1)}, u32[]{:S(2)}, u32[]{:S(2)}) collective-permute-start(bf16[128,2048]{1,0:T(8,128)(2,1)S(1)} %get-tuple-element.28), channel_id=1, source_target_pairs={{0,128},{128,0},{256,384},{384,256},{512,640},{640,512},{768,896},... | collective-permute-start | bytes 1572872 | tf_op jit(solution)/shard_map/ppermute | solution.py:433
  38.3 1.9 %collective-permute-start.4 = (bf16[128,2048]{1,0:T(8,128)(2,1)S(1)}, bf16[128,2048]{1,0:T(8,128)(2,1)S(1)}, u32[]{:S(2)}, u32[]{:S(2)}) collective-permute-start(bf16[128,2048]{1,0:T(8,128)(2,1)S(1)} %get-tuple-element.29), channel_id=1, source_target_pairs={{0,896},{128,256},{256,128},{384,512},{512,384},{640,768},{768,640... | collective-permute-start | bytes 1572872 | tf_op jit(solution)/shard_map/ppermute | solution.py:433
  40.2 11.1 %collective-permute-done.3.left_ref = bf16[128,2048]{1,0:T(8,128)(2,1)S(1)} collective-permute-done((bf16[128,2048]{1,0:T(8,128)(2,1)S(1)}, bf16[128,2048]{1,0:T(8,128)(2,1)S(1)}, u32[]{:S(2)}, u32[]{:S(2)}) %collective-permute-start.3) | collective-permute-done | bytes 524320 | tf_op jit(solution)/shard_map/ppermute | solution.py:433
  51.4 3.1 %collective-permute-done.4.right_ref = bf16[128,2048]{1,0:T(8,128)(2,1)S(1)} collective-permute-done((bf16[128,2048]{1,0:T(8,128)(2,1)S(1)}, bf16[128,2048]{1,0:T(8,128)(2,1)S(1)}, u32[]{:S(2)}, u32[]{:S(2)}) %collective-permute-start.4) | collective-permute-done | bytes 524320 | tf_op jit(solution)/shard_map/ppermute | solution.py:433
  54.5 1.2 sum_y.1
  55.7 0.0 all-to-all-done.in_ref
  55.7 0.0 copy-start.1
  55.7 1.4 copy-done.1
  57.1 3.5 %all-to-all-start.1 = ((bf16[4,256,512]{2,1,0:T(8,128)(2,1)}), bf16[4,256,512]{2,1,0:T(8,128)(2,1)S(1)}, u32[]{:S(2)}, u32[]{:S(2)}) async-start(bf16[4,256,512]{2,1,0:T(8,128)(2,1)} %sum_y.1), calls=%async_computation.1 | async-start | bytes 2097152 | tf_op jit(solution)/shard_map/all_to_all | solution.py:437
  60.6 0.0 copy-start.2
  60.6 1.6 %copy-done.2 = bf16[8,520,256]{2,1,0:T(8,128)(2,1)S(1)} copy-done((bf16[8,520,256]{2,1,0:T(8,128)(2,1)S(1)}, bf16[8,520,256]{2,1,0:T(8,128)(2,1)}, u32[]{:S(2)}) %copy-start.2) | copy-done | bytes 2129944
  62.2 0.0 copy-start
  62.2 0.0 copy-start.8
  62.2 0.0 copy-start.9
  62.2 0.8 sum_xz.1
  63.1 0.0 copy-start.10
  63.1 2.0 %collective-permute-start = (bf16[264,256]{1,0:T(8,128)(2,1)}, bf16[264,256]{1,0:T(8,128)(2,1)}, u32[]{:S(2)}, u32[]{:S(2)}) collective-permute-start(bf16[264,256]{1,0:T(8,128)(2,1)} %get-tuple-element.20), channel_id=1, source_target_pairs={{0,8},{4,12},{8,0},{12,4},{16,24},{20,28},{24,16},{28,20},{1,9},{5... | collective-permute-start | bytes 405512 | tf_op jit(solution)/shard_map/ppermute | solution.py:433
  65.1 21.3 %all-to-all-done.1.in_ref = bf16[4,256,512]{2,1,0:T(8,128)(2,1)S(1)} async-done(((bf16[4,256,512]{2,1,0:T(8,128)(2,1)}), bf16[4,256,512]{2,1,0:T(8,128)(2,1)S(1)}, u32[]{:S(2)}, u32[]{:S(2)}) %all-to-all-start.1) | async-done | bytes 1048608 | tf_op jit(solution)/shard_map/all_to_all | solution.py:437
  86.5 0.7 sum_y4.1
  87.2 0.0 copy-start.6
  87.2 0.0 copy-start.5
  87.2 11.5 %collective-permute-start.5 = (bf16[256,256]{1,0:T(8,128)(2,1)}, bf16[256,256]{1,0:T(8,128)(2,1)S(1)}, u32[]{:S(2)}, u32[]{:S(2)}) collective-permute-start(bf16[256,256]{1,0:T(8,128)(2,1)} %get-tuple-element.31), channel_id=1, source_target_pairs={{0,64},{64,0},{1,65},{65,1},{2,66},{66,2},{3,67},{67,3},{4,68},{68... | collective-permute-start | bytes 393224 | tf_op jit(solution)/shard_map/ppermute | solution.py:433
  98.7 0.0 collective-permute-done.got_ref
  98.7 0.9 sum_z4.1
  99.7 0.0 copy-done.6
  99.7 0.0 copy-start.7
  99.7 6.0 %collective-permute-start.1 = (bf16[136,256]{1,0:T(8,128)(2,1)S(1)}, bf16[136,256]{1,0:T(8,128)(2,1)S(1)}, u32[]{:S(2)}, u32[]{:S(2)}) collective-permute-start(bf16[136,256]{1,0:T(8,128)(2,1)S(1)} %get-tuple-element.22), channel_id=1, source_target_pairs={{0,16},{4,20},{8,24},{12,28},{16,0},{20,4},{24,8},{28,12},{1,17},{... | collective-permute-start | bytes 208904 | tf_op jit(solution)/shard_map/ppermute | solution.py:433
  105.7 14.0 %collective-permute-done.1.got_ref = bf16[136,256]{1,0:T(8,128)(2,1)S(1)} collective-permute-done((bf16[136,256]{1,0:T(8,128)(2,1)S(1)}, bf16[136,256]{1,0:T(8,128)(2,1)S(1)}, u32[]{:S(2)}, u32[]{:S(2)}) %collective-permute-start.1) | collective-permute-done | bytes 69664 | tf_op jit(solution)/shard_map/ppermute | solution.py:433
  119.7 0.0 copy-done
  119.7 0.0 copy-done.8
  119.7 0.0 copy-done.9
  119.7 0.8 finish.1
  120.5 5.9 %collective-permute-start.6 = (f32[1,256]{1,0:T(1,128)S(1)}, f32[1,256]{1,0:T(1,128)S(1)}, u32[]{:S(2)}, u32[]{:S(2)}) collective-permute-start(f32[1,256]{1,0:T(1,128)S(1)} %get-tuple-element.32.own_ref), channel_id=1, source_target_pairs={{0,64},{64,0},{1,65},{65,1},{2,66},{66,2},{3,67},{67,3},{4,68},{68... | collective-permute-start | bytes 3080 | tf_op jit(solution)/shard_map/ppermute | solution.py:433
  126.3 7.2 %collective-permute-done.6.got_ref = f32[1,256]{1,0:T(1,128)S(1)} collective-permute-done((f32[1,256]{1,0:T(1,128)S(1)}, f32[1,256]{1,0:T(1,128)S(1)}, u32[]{:S(2)}, u32[]{:S(2)}) %collective-permute-start.6) | collective-permute-done | bytes 1056 | tf_op jit(solution)/shard_map/ppermute | solution.py:433
  133.5 0.6 gain_mix.1
  134.1 6.2 %all-to-all-start.2 = ((f32[16,1,256]{2,1,0:T(1,128)}), f32[16,1,256]{2,1,0:T(1,128)S(1)}, u32[]{:S(2)}, u32[]{:S(2)}) async-start(f32[16,1,256]{2,1,0:T(1,128)} %gain_mix.1), calls=%async_computation.2 | async-start | bytes 32768 | tf_op jit(solution)/shard_map/all_to_all | solution.py:437
  140.3 0.0 collective-permute-done.5.got_ref
  140.4 7.3 %all-to-all-done.2.gain_ref = f32[16,1,256]{2,1,0:T(1,128)S(1)} async-done(((f32[16,1,256]{2,1,0:T(1,128)}), f32[16,1,256]{2,1,0:T(1,128)S(1)}, u32[]{:S(2)}, u32[]{:S(2)}) %all-to-all-start.2) | async-done | bytes 16416 | tf_op jit(solution)/shard_map/all_to_all | solution.py:437
  147.7 0.0 copy-done.10
  147.7 0.0 copy-done.5
  147.7 0.0 copy-done.7
  147.7 0.9 last.1
Async XLA Ops:
  6.6 49.1 %all-to-all-start = ((bf16[8,520,256]{2,1,0:T(8,128)(2,1)}), bf16[8,520,256]{2,1,0:T(8,128)(2,1)S(1)}, u32[]{:S(2)}, u32[]{:S(2)}) async-start(bf16[8,520,256]{2,1,0:T(8,128)(2,1)} %partial.1), calls=%async_computation | async-start | bytes 4259840 | tf_op jit(solution)/shard_map/all_to_all | solution.py:437
  13.3 19.8 %copy-start.4 = (bf16[128,256]{1,0:T(8,128)(2,1)S(1)}, bf16[128,256]{1,0:T(8,128)(2,1)}, u32[]{:S(2)}) copy-start(bf16[128,256]{1,0:T(8,128)(2,1)} %q_ref.5) | copy-start | bytes 196612
  17.5 15.6 %collective-permute-start.2 = (bf16[128,4352]{1,0:T(8,128)(2,1)}, bf16[128,4352]{1,0:T(8,128)(2,1)S(1)}, u32[]{:S(2)}, u32[]{:S(2)}) collective-permute-start(bf16[128,4352]{1,0:T(8,128)(2,1)} %get-tuple-element.26), channel_id=1, source_target_pairs={{0,32},{32,0},{1,33},{33,1},{2,34},{34,2},{3,35},{35,3},{4,36},{36... | collective-permute-start | bytes 3342344 | tf_op jit(solution)/shard_map/ppermute | solution.py:433
  33.1 1.2 copy-start.3
  36.4 15.0 %collective-permute-start.3 = (bf16[128,2048]{1,0:T(8,128)(2,1)S(1)}, bf16[128,2048]{1,0:T(8,128)(2,1)S(1)}, u32[]{:S(2)}, u32[]{:S(2)}) collective-permute-start(bf16[128,2048]{1,0:T(8,128)(2,1)S(1)} %get-tuple-element.28), channel_id=1, source_target_pairs={{0,128},{128,0},{256,384},{384,256},{512,640},{640,512},{768,896},... | collective-permute-start | bytes 1572872 | tf_op jit(solution)/shard_map/ppermute | solution.py:433
  38.3 16.2 %collective-permute-start.4 = (bf16[128,2048]{1,0:T(8,128)(2,1)S(1)}, bf16[128,2048]{1,0:T(8,128)(2,1)S(1)}, u32[]{:S(2)}, u32[]{:S(2)}) collective-permute-start(bf16[128,2048]{1,0:T(8,128)(2,1)S(1)} %get-tuple-element.29), channel_id=1, source_target_pairs={{0,896},{128,256},{256,128},{384,512},{512,384},{640,768},{768,640... | collective-permute-start | bytes 1572872 | tf_op jit(solution)/shard_map/ppermute | solution.py:433
  55.7 1.4 copy-start.1
  57.1 29.3 %all-to-all-start.1 = ((bf16[4,256,512]{2,1,0:T(8,128)(2,1)}), bf16[4,256,512]{2,1,0:T(8,128)(2,1)S(1)}, u32[]{:S(2)}, u32[]{:S(2)}) async-start(bf16[4,256,512]{2,1,0:T(8,128)(2,1)} %sum_y.1), calls=%async_computation.1 | async-start | bytes 2097152 | tf_op jit(solution)/shard_map/all_to_all | solution.py:437
  60.6 1.6 %copy-start.2 = (bf16[8,520,256]{2,1,0:T(8,128)(2,1)S(1)}, bf16[8,520,256]{2,1,0:T(8,128)(2,1)}, u32[]{:S(2)}) copy-start(bf16[8,520,256]{2,1,0:T(8,128)(2,1)} %copy-done.1) | copy-start | bytes 6389764
  62.2 57.4 %copy-start = (bf16[128,8192]{1,0:T(8,128)(2,1)S(1)}, bf16[128,8192]{1,0:T(8,128)(2,1)}, u32[]{:S(2)}) copy-start(bf16[128,8192]{1,0:T(8,128)(2,1)} %h_ref.3) | copy-start | bytes 6291460
  62.2 57.4 %copy-start.8 = (bf16[8192]{0:T(1024)(128)(2,1)S(1)}, bf16[8192]{0:T(1024)(128)(2,1)}, u32[]{:S(2)}) copy-start(bf16[8192]{0:T(1024)(128)(2,1)} %param.7) | copy-start | bytes 49156
  62.2 57.4 %copy-start.9 = (f32[128,1]{1,0:T(8,128)S(1)}, f32[128,1]{1,0:T(8,128)}, u32[]{:S(2)}) copy-start(f32[128,1]{1,0:T(8,128)} %get-tuple-element.23.rinv_ref) | copy-start | bytes 1540
  63.1 84.6 %copy-start.10 = (f32[256]{0:T(256)S(1)}, f32[256]{0:T(256)}, u32[]{:S(2)}) copy-start(f32[256]{0:T(256)} %param.11) | copy-start | bytes 3076
  63.1 35.6 %collective-permute-start = (bf16[264,256]{1,0:T(8,128)(2,1)}, bf16[264,256]{1,0:T(8,128)(2,1)}, u32[]{:S(2)}, u32[]{:S(2)}) collective-permute-start(bf16[264,256]{1,0:T(8,128)(2,1)} %get-tuple-element.20), channel_id=1, source_target_pairs={{0,8},{4,12},{8,0},{12,4},{16,24},{20,28},{24,16},{28,20},{1,9},{5... | collective-permute-start | bytes 405512 | tf_op jit(solution)/shard_map/ppermute | solution.py:433
  87.2 12.5 %copy-start.6 = (f32[256,256]{1,0:T(8,128)}, f32[256,256]{1,0:T(8,128)S(1)}, u32[]{:S(2)}) copy-start(f32[256,256]{1,0:T(8,128)S(1)} %get-tuple-element.30.keep_ref) | copy-start | bytes 786436
  87.2 60.5 %copy-start.5 = (f32[256,256]{1,0:T(8,128)S(1)}, f32[256,256]{1,0:T(8,128)}, u32[]{:S(2)}) copy-start(f32[256,256]{1,0:T(8,128)} %main_ref.1) | copy-start | bytes 786436
  87.2 53.1 %collective-permute-start.5 = (bf16[256,256]{1,0:T(8,128)(2,1)}, bf16[256,256]{1,0:T(8,128)(2,1)S(1)}, u32[]{:S(2)}, u32[]{:S(2)}) collective-permute-start(bf16[256,256]{1,0:T(8,128)(2,1)} %get-tuple-element.31), channel_id=1, source_target_pairs={{0,64},{64,0},{1,65},{65,1},{2,66},{66,2},{3,67},{67,3},{4,68},{68... | collective-permute-start | bytes 393224 | tf_op jit(solution)/shard_map/ppermute | solution.py:433
  99.7 48.0 %copy-start.7 = (f32[256,256]{1,0:T(8,128)S(1)}, f32[256,256]{1,0:T(8,128)}, u32[]{:S(2)}) copy-start(f32[256,256]{1,0:T(8,128)} %copy-done.6) | copy-start | bytes 786436
  99.7 20.0 %collective-permute-start.1 = (bf16[136,256]{1,0:T(8,128)(2,1)S(1)}, bf16[136,256]{1,0:T(8,128)(2,1)S(1)}, u32[]{:S(2)}, u32[]{:S(2)}) collective-permute-start(bf16[136,256]{1,0:T(8,128)(2,1)S(1)} %get-tuple-element.22), channel_id=1, source_target_pairs={{0,16},{4,20},{8,24},{12,28},{16,0},{20,4},{24,8},{28,12},{1,17},{... | collective-permute-start | bytes 208904 | tf_op jit(solution)/shard_map/ppermute | solution.py:433
  120.5 13.0 %collective-permute-start.6 = (f32[1,256]{1,0:T(1,128)S(1)}, f32[1,256]{1,0:T(1,128)S(1)}, u32[]{:S(2)}, u32[]{:S(2)}) collective-permute-start(f32[1,256]{1,0:T(1,128)S(1)} %get-tuple-element.32.own_ref), channel_id=1, source_target_pairs={{0,64},{64,0},{1,65},{65,1},{2,66},{66,2},{3,67},{67,3},{4,68},{68... | collective-permute-start | bytes 3080 | tf_op jit(solution)/shard_map/ppermute | solution.py:433
  134.1 13.6 %all-to-all-start.2 = ((f32[16,1,256]{2,1,0:T(1,128)}), f32[16,1,256]{2,1,0:T(1,128)S(1)}, u32[]{:S(2)}, u32[]{:S(2)}) async-start(f32[16,1,256]{2,1,0:T(1,128)} %gain_mix.1), calls=%async_computation.2 | async-start | bytes 32768 | tf_op jit(solution)/shard_map/all_to_all | solution.py:437
